TPU v7x, 32 devices: a whole 2x2x4 slice. The times are simulated.
32 devices in a mesh: dp: 8 (over y, x, core), tensor: 4 (over z).
Axes of the slice: x: 2, y: 2, z: 4, core: 2. Of those that a mesh axis runs over, the one named last changes fastest.
Arguments:
- tokens: bfloat16 [4096, 2048], P(('dp', 'tensor')), may hold values from -6 to 6
- segments: int32 [8, 512], P('dp'), may hold values from 0 to 2, never falling along the last dimension, each value on 1 to 256 neighbouring positions
- routes: int32 [4096, 6], P('dp'), may hold values from 0 to 63, all different within a row; in each aligned block of 512 rows (0 to 511, 512 to 1023, ...) at most 72 rows name the same one
- cotangent: bfloat16 [4096, 2048], P(('dp', 'tensor')), may hold values from -6 to 6
- attention_gain: bfloat16 [2048], P(('dp', 'tensor')), may hold values from 0.25 to 1.75
- latent_gain: bfloat16 [512], P(('dp', 'tensor')), may hold values from 0.25 to 1.75
- feedforward_gain: bfloat16 [2048], P(('dp', 'tensor')), may hold values from 0.25 to 1.75
- query_weight: bfloat16 [2048, 3072], P('dp', 'tensor'), may hold values from -0.125 to 0.125
- latent_weight: bfloat16 [2048, 576], P(('dp', 'tensor')), may hold values from -0.125 to 0.125
- expand_weight: bfloat16 [512, 4096], P('dp', 'tensor'), may hold values from -0.25 to 0.25
- output_weight: bfloat16 [2048, 2048], P('tensor', 'dp'), may hold values from -0.5 to 0.5
- router_weight: bfloat16 [2048, 64], P(('dp', 'tensor')), may hold values from -0.125 to 0.125
- shared_in: bfloat16 [2048, 2, 2816], P('dp', None, 'tensor'), may hold values from -0.125 to 0.125
- shared_out: bfloat16 [2816, 2048], P('tensor', 'dp'), may hold values from -0.109375 to 0.109375
- expert_in: bfloat16 [64, 2048, 2, 1408], P('dp', None, None, 'tensor'), may hold values from -0.125 to 0.125
- expert_out: bfloat16 [64, 1408, 2048], P('dp', 'tensor'), may hold values from -0.15625 to 0.15625
Outputs:
- out_tokens: bfloat16 [4096, 2048], P(('dp', 'tensor'))
- tokens_grad: float32 [4096, 2048], P(('dp', 'tensor'))
- attention_gain_grad: float32 [2048], P(('dp', 'tensor'))
- latent_gain_grad: float32 [512], P(('dp', 'tensor'))
- feedforward_gain_grad: float32 [2048], P(('dp', 'tensor'))
- query_weight_grad: float32 [2048, 3072], P('dp', 'tensor')
- latent_weight_grad: float32 [2048, 576], P(('dp', 'tensor'))
- expand_weight_grad: float32 [512, 4096], P('dp', 'tensor')
- output_weight_grad: float32 [2048, 2048], P('tensor', 'dp')
- router_weight_grad: float32 [2048, 64], P(('dp', 'tensor'))
- shared_in_grad: float32 [2048, 2, 2816], P('dp', None, 'tensor')
- shared_out_grad: float32 [2816, 2048], P('tensor', 'dp')
- expert_in_grad: float32 [64, 2048, 2, 1408], P('dp', None, None, 'tensor')
- expert_out_grad: float32 [64, 1408, 2048], P('dp', 'tensor')
Inputs may be any that keep to these rules, and one draw needn't show every extreme that they name: `segments`: each row numbers the sequences of one group in order; a sequence holds at most 256 tokens and one holds exactly that many. `routes`: the 6 experts of a token differ. Within the 512 tokens of one index of dp, no expert is named more than 72 times, a bound that some block reaches.
All inputs are finite; a program needn't handle non-finite values.
Results may differ from a plain program's by a relative error of at most 0.024.
Values may be sent and summed in bfloat16 or wider, within the bound.
A program may use at most 512 MiB of HBM per device.

v0:
```python
import jax
import jax.numpy as jnp
from jax import lax
from jax.sharding import PartitionSpec as P

DN = 128
DR = 64
DV = 128
KVR = 512
EXPERTS = 64
TOPK = 6
CAP = 72


epsilon = 1e-06
route_scale = 2.446
rope_base = 50000.0
excluded = -1e30


def rms_scale(array_in):
    return lax.rsqrt(jnp.mean(array_in * array_in, axis=-1, keepdims=True) + epsilon)


def rope_tables(segment_row):
    places = jnp.arange(segment_row.shape[0], dtype=jnp.int32)
    boundary = jnp.concatenate([jnp.ones((1,), jnp.bool_), segment_row[1:] != segment_row[:-1]])
    begins = lax.cummax(jnp.where(boundary, places, 0), axis=0)
    position = (places - begins).astype(jnp.float32)
    freqs = rope_base ** (-jnp.arange(DR // 2, dtype=jnp.float32) * 2.0 / DR)
    angle = position[:, None] * freqs[None, :]
    return (jnp.cos(angle), jnp.sin(angle))


def rotate(array_in, cosine, sine):
    half_width = array_in.shape[-1] // 2
    first_half, second_half = (array_in[..., :half_width], array_in[..., half_width:])
    return jnp.concatenate(
        [first_half * cosine - second_half * sine, second_half * cosine + first_half * sine],
        axis=-1,
    )


def unrotate(array_in, cosine, sine):
    half_width = array_in.shape[-1] // 2
    first_half, second_half = (array_in[..., :half_width], array_in[..., half_width:])
    return jnp.concatenate(
        [first_half * cosine + second_half * sine, second_half * cosine - first_half * sine],
        axis=-1,
    )


def attention_tables(normed, query_weight, latent_weight, expand_weight, latent_gain, cosine, sine):
    row_count = normed.shape[0]
    head_count = query_weight.shape[1] // (DN + DR)
    query = jnp.dot(normed, query_weight, preferred_element_type=jnp.float32).reshape(
        row_count, head_count, DN + DR
    )
    query = jnp.concatenate(
        [query[..., :DN], rotate(query[..., DN:], cosine[:, None, :], sine[:, None, :])], axis=-1
    ).astype(jnp.bfloat16)
    latent = jnp.dot(normed, latent_weight, preferred_element_type=jnp.float32)
    compressed = latent[:, :KVR]
    latent_scale = rms_scale(compressed)
    latent_normed = (compressed * latent_scale * latent_gain.astype(jnp.float32)).astype(
        jnp.bfloat16
    )
    rope_key = rotate(latent[:, KVR:], cosine, sine)
    keyvalue = jnp.dot(latent_normed, expand_weight, preferred_element_type=jnp.float32).reshape(
        row_count, head_count, DN + DV
    )
    key_rows = jnp.concatenate(
        [keyvalue[..., :DN], jnp.broadcast_to(rope_key[:, None, :], (row_count, head_count, DR))],
        axis=-1,
    ).astype(jnp.bfloat16)
    value_rows = keyvalue[..., DN:].astype(jnp.bfloat16)
    return (query, key_rows, value_rows, compressed, latent_scale, latent_normed)


def masked_scores(query_block, key_rows, start, segment_row):
    block_rows = query_block.shape[0]
    head_depth = query_block.shape[-1]
    scores = jnp.einsum(
        "qhd,khd->hqk", query_block, key_rows, preferred_element_type=jnp.float32
    ) * head_depth ** (-0.5)
    row_index = start + jnp.arange(block_rows, dtype=jnp.int32)
    column_index = jnp.arange(key_rows.shape[0], dtype=jnp.int32)
    allowed = (segment_row[None, :] == segment_row[:, None]) & (
        column_index[None, :] <= row_index[:, None]
    )
    return jnp.where(allowed[None], scores, excluded)


def attend(query, key_rows, value_rows, segment_row):
    row_count, head_count, head_depth = query.shape
    block_rows = min(row_count, 512)
    blocks = row_count // block_rows
    starts = jnp.arange(blocks, dtype=jnp.int32) * block_rows

    def one_block(inputs):
        query_block, start = inputs
        scores = masked_scores(query_block, key_rows, start, segment_row)
        logsum = jnp.log(jnp.sum(jnp.exp(scores), axis=-1))
        weights_low = jnp.exp(scores - logsum[..., None]).astype(jnp.bfloat16)
        mixed = jnp.einsum(
            "hqk,khd->qhd", weights_low, value_rows, preferred_element_type=jnp.float32
        ).astype(jnp.bfloat16)
        return (mixed, logsum.T)

    mixed, logsum = lax.map(
        one_block, (query.reshape(blocks, block_rows, head_count, head_depth), starts)
    )
    return (mixed.reshape(row_count, head_count, -1), logsum.reshape(row_count, head_count))


def attend_back(query, key_rows, value_rows, segment_row, out_grad, logsum):
    row_count, head_count, head_depth = query.shape
    block_rows = min(row_count, 512)
    blocks = row_count // block_rows
    starts = jnp.arange(blocks, dtype=jnp.int32) * block_rows

    def one_block(carry, inputs):
        key_grad, value_grad = carry
        query_block, grad_block, logsum_block, start = inputs
        scores = masked_scores(query_block, key_rows, start, segment_row)
        weights_full = jnp.exp(scores - logsum_block.T[..., None])
        weights_low = weights_full.astype(jnp.bfloat16)
        prob_grad = jnp.einsum(
            "qhd,khd->hqk", grad_block, value_rows, preferred_element_type=jnp.float32
        )
        row_total = jnp.sum(weights_full * prob_grad, axis=-1, keepdims=True)
        score_grad = (weights_full * (prob_grad - row_total) * head_depth ** (-0.5)).astype(
            jnp.bfloat16
        )
        query_grad = jnp.einsum(
            "hqk,khd->qhd", score_grad, key_rows, preferred_element_type=jnp.float32
        )
        key_grad = key_grad + jnp.einsum(
            "hqk,qhd->khd", score_grad, query_block, preferred_element_type=jnp.float32
        )
        value_grad = value_grad + jnp.einsum(
            "hqk,qhd->khd", weights_low, grad_block, preferred_element_type=jnp.float32
        )
        return ((key_grad, value_grad), query_grad)

    initial = (
        jnp.zeros((row_count, head_count, head_depth), jnp.float32),
        jnp.zeros((row_count, head_count, value_rows.shape[-1]), jnp.float32),
    )
    (key_grad, value_grad), query_grad = lax.scan(
        one_block,
        initial,
        (
            query.reshape(blocks, block_rows, head_count, head_depth),
            out_grad.reshape(blocks, block_rows, head_count, -1),
            logsum.reshape(blocks, block_rows, head_count),
            starts,
        ),
    )
    return (query_grad.reshape(row_count, head_count, head_depth), key_grad, value_grad)


def expert_slots(route_group):
    route_flat = route_group.reshape(-1)
    onehot = (route_flat[:, None] == jnp.arange(EXPERTS, dtype=jnp.int32)[None, :]).astype(
        jnp.int32
    )
    before = jnp.cumsum(onehot, axis=0) - onehot
    return (route_flat, jnp.sum(before * onehot, axis=1))


def swiglu_grad(hidden_grad, gate_pre, up_pre):
    sigm = jax.nn.sigmoid(gate_pre)
    return (
        hidden_grad * up_pre * sigm * (1.0 + gate_pre * (1.0 - sigm)),
        hidden_grad * jax.nn.silu(gate_pre),
    )


def expert_compute(received, expert_in, expert_out):
    pre = jnp.einsum("sxkd,xdcf->sxkcf", received, expert_in, preferred_element_type=jnp.float32)
    activation = (jax.nn.silu(pre[..., 0, :]) * pre[..., 1, :]).astype(jnp.bfloat16)
    return jnp.einsum(
        "sxkf,xfd->sxkd", activation, expert_out, preferred_element_type=jnp.float32
    ).astype(jnp.bfloat16)


def body(
    tokens,
    segments,
    routes,
    cotangent,
    attention_gain,
    latent_gain,
    feedforward_gain,
    query_weight,
    latent_weight,
    expand_weight,
    output_weight,
    router_weight,
    shared_in,
    shared_out,
    expert_in,
    expert_out,
):
    query_full, expand_full, output_full, shared_in_full, shared_out_full = (
        lax.all_gather(query_weight, "dp", axis=0, tiled=True),
        lax.all_gather(expand_weight, "dp", axis=0, tiled=True),
        lax.all_gather(output_weight, "dp", axis=1, tiled=True),
        lax.all_gather(shared_in, "dp", axis=0, tiled=True),
        lax.all_gather(shared_out, "dp", axis=1, tiled=True),
    )
    gain_one_low, gain_lat_low, gain_two_low, latent_full, router_full = (
        lax.all_gather(attention_gain, ("dp", "tensor"), axis=0, tiled=True),
        lax.all_gather(latent_gain, ("dp", "tensor"), axis=0, tiled=True),
        lax.all_gather(feedforward_gain, ("dp", "tensor"), axis=0, tiled=True),
        lax.all_gather(latent_weight, ("dp", "tensor"), axis=0, tiled=True),
        lax.all_gather(router_weight, ("dp", "tensor"), axis=0, tiled=True),
    )
    gain_one = gain_one_low.astype(jnp.float32)
    gain_two = gain_two_low.astype(jnp.float32)
    own_rows = tokens.shape[0]
    width_model = tokens.shape[1]
    first_row = lax.axis_index("tensor") * own_rows
    dp_count = lax.axis_size("dp")
    local_experts = expert_in.shape[0]
    segment_row = segments[0]
    group_rows = lax.all_gather(tokens, "tensor", axis=0, tiled=True)
    row_count = group_rows.shape[0]
    wide = group_rows.astype(jnp.float32)
    scale_one = rms_scale(wide)
    normed = (wide * scale_one * gain_one).astype(jnp.bfloat16)
    cosine, sine = rope_tables(segment_row)
    query, key_rows, value_rows, compressed, latent_scale, latent_normed = attention_tables(
        normed, query_full, latent_full, expand_full, gain_lat_low, cosine, sine
    )
    mixed, logsum = attend(query, key_rows, value_rows, segment_row)
    mixed_flat = mixed.reshape(row_count, -1)
    attention_out = lax.psum(
        jnp.dot(mixed_flat, output_full, preferred_element_type=jnp.float32).astype(jnp.bfloat16),
        "tensor",
    ).astype(jnp.float32)
    hidden = wide + attention_out
    scale_two = rms_scale(hidden)
    normed_two = (hidden * scale_two * gain_two).astype(jnp.bfloat16)
    logits = jnp.dot(normed_two, router_full, preferred_element_type=jnp.float32)
    sigm = jax.nn.sigmoid(logits)
    chosen = routes[:, :, None] == jnp.arange(EXPERTS, dtype=jnp.int32)[None, None, :]
    picked = jnp.sum(jnp.where(chosen, sigm[:, None, :], 0.0), axis=-1)
    picked_total = jnp.sum(picked, axis=1, keepdims=True)
    gate_weights = route_scale * picked / picked_total
    shared_pre = jnp.einsum(
        "gd,dcf->gcf", normed_two, shared_in_full, preferred_element_type=jnp.float32
    )
    shared_act = (jax.nn.silu(shared_pre[:, 0]) * shared_pre[:, 1]).astype(jnp.bfloat16)
    shared_part = jnp.dot(shared_act, shared_out_full, preferred_element_type=jnp.float32)
    route_flat, slot_index = expert_slots(routes)
    pair_mask = jnp.ones((row_count, TOPK), jnp.float32)
    send_rows = (
        jnp.zeros((EXPERTS, CAP, width_model), jnp.bfloat16)
        .at[route_flat, slot_index]
        .set(jnp.repeat(normed_two, TOPK, axis=0))
    )
    send_rows = send_rows.reshape(dp_count, local_experts, CAP, width_model)
    result = expert_compute(
        lax.all_to_all(send_rows, "dp", split_axis=0, concat_axis=0, tiled=True),
        expert_in,
        expert_out,
    )
    returned = lax.all_to_all(result, "dp", split_axis=0, concat_axis=0, tiled=True)
    routed = (
        returned.reshape(EXPERTS, -1, width_model)[route_flat, slot_index]
        .reshape(row_count, TOPK, width_model)
        .astype(jnp.float32)
        * pair_mask[..., None]
    )
    feed_part = shared_part + jnp.sum(gate_weights[..., None] * routed, axis=1)
    feed_own = lax.psum_scatter(
        feed_part.astype(jnp.bfloat16), "tensor", scatter_dimension=0, tiled=True
    ).astype(jnp.float32)
    hidden_own = lax.dynamic_slice_in_dim(hidden, first_row, own_rows, 0)
    out_tokens = (hidden_own + feed_own).astype(jnp.bfloat16)
    grad_rows = lax.all_gather(cotangent, "tensor", axis=0, tiled=True)
    grad_wide = grad_rows.astype(jnp.float32)
    gate_grad = jnp.sum(routed * grad_wide[:, None, :], axis=-1)
    routed_grad = (gate_weights[..., None] * grad_wide[:, None, :]).astype(jnp.bfloat16)
    grad_send = (
        jnp.zeros((EXPERTS, CAP, width_model), jnp.bfloat16)
        .at[route_flat, slot_index]
        .set(routed_grad.reshape(row_count * TOPK, width_model))
    )
    grad_send = grad_send.reshape(dp_count, local_experts, CAP, width_model)
    payload = jnp.concatenate([grad_send, send_rows], axis=1)
    arrived = lax.all_to_all(payload, "dp", split_axis=0, concat_axis=0, tiled=True)
    grad_recv = arrived[:, :local_experts]
    rows_recv = arrived[:, local_experts:]
    expert_pre = jnp.einsum(
        "sxkd,xdcf->sxkcf", rows_recv, expert_in, preferred_element_type=jnp.float32
    )
    gate_pre, up_pre = (expert_pre[..., 0, :], expert_pre[..., 1, :])
    expert_act = (jax.nn.silu(gate_pre) * up_pre).astype(jnp.bfloat16)
    expert_hidden_grad = jnp.einsum(
        "sxkd,xfd->sxkf", grad_recv, expert_out, preferred_element_type=jnp.float32
    )
    gate_part, up_part = swiglu_grad(expert_hidden_grad, gate_pre, up_pre)
    expert_pre_grad = jnp.stack([gate_part, up_part], axis=-2).astype(jnp.bfloat16)
    expert_out_grad = jnp.einsum(
        "sxkf,sxkd->xfd", expert_act, grad_recv, preferred_element_type=jnp.float32
    )
    expert_in_grad = jnp.einsum(
        "sxkd,sxkcf->xdcf", rows_recv, expert_pre_grad, preferred_element_type=jnp.float32
    )
    expert_row_grad = jnp.einsum(
        "sxkcf,xdcf->sxkd", expert_pre_grad, expert_in, preferred_element_type=jnp.float32
    ).astype(jnp.bfloat16)
    back_rows = lax.all_to_all(expert_row_grad, "dp", split_axis=0, concat_axis=0, tiled=True)
    routed_back = jnp.sum(
        back_rows.reshape(EXPERTS, -1, width_model)[route_flat, slot_index]
        .reshape(row_count, TOPK, width_model)
        .astype(jnp.float32)
        * pair_mask[..., None],
        axis=1,
    )
    shared_hidden_grad = jnp.dot(grad_rows, shared_out_full.T, preferred_element_type=jnp.float32)
    shared_gate_part, shared_up_part = swiglu_grad(
        shared_hidden_grad, shared_pre[:, 0], shared_pre[:, 1]
    )
    shared_pre_grad = jnp.stack([shared_gate_part, shared_up_part], axis=1).astype(jnp.bfloat16)
    shared_out_grad = jnp.dot(shared_act.T, grad_rows, preferred_element_type=jnp.float32)
    shared_in_grad = jnp.einsum(
        "gd,gcf->dcf", normed_two, shared_pre_grad, preferred_element_type=jnp.float32
    )
    shared_back = jnp.einsum(
        "gcf,dcf->gd", shared_pre_grad, shared_in_full, preferred_element_type=jnp.float32
    )
    picked_grad = route_scale * (
        gate_grad / picked_total
        - jnp.sum(gate_grad * picked, axis=1, keepdims=True) / (picked_total * picked_total)
    )
    logit_part = picked_grad * picked * (1.0 - picked)
    logit_grad = jnp.sum(jnp.where(chosen, logit_part[..., None], 0.0), axis=1)
    router_grad = jnp.dot(
        normed_two.astype(jnp.float32).T, logit_grad, precision=lax.Precision.HIGHEST
    )
    router_back = jnp.dot(
        logit_grad, router_full.astype(jnp.float32).T, precision=lax.Precision.HIGHEST
    )
    normed_two_grad = lax.psum(
        (routed_back + shared_back + router_back).astype(jnp.bfloat16), "tensor"
    ).astype(jnp.float32)
    weighted_two = normed_two_grad * gain_two
    hidden_grad = (
        grad_wide
        + scale_two * weighted_two
        - hidden * scale_two**3 * jnp.mean(hidden * weighted_two, axis=-1, keepdims=True)
    )
    own_term = lax.dynamic_slice_in_dim(
        normed_two_grad * hidden * scale_two, first_row, own_rows, 0
    )
    gain_two_grad = jnp.sum(own_term, axis=0)
    hidden_low = hidden_grad.astype(jnp.bfloat16)
    output_grad = jnp.dot(mixed_flat.T, hidden_low, preferred_element_type=jnp.float32)
    mixed_grad = (
        jnp.dot(hidden_low, output_full.T, preferred_element_type=jnp.float32)
        .astype(jnp.bfloat16)
        .reshape(mixed.shape)
    )
    query_grad, key_grad, value_grad = attend_back(
        query, key_rows, value_rows, segment_row, mixed_grad, logsum
    )
    query_pre = (
        jnp.concatenate(
            [
                query_grad[..., :DN],
                unrotate(query_grad[..., DN:], cosine[:, None, :], sine[:, None, :]),
            ],
            axis=-1,
        )
        .astype(jnp.bfloat16)
        .reshape(row_count, -1)
    )
    query_grad_weight = jnp.dot(normed.T, query_pre, preferred_element_type=jnp.float32)
    normed_grad = jnp.dot(query_pre, query_full.T, preferred_element_type=jnp.float32)
    keyvalue_grad = (
        jnp.concatenate([key_grad[..., :DN], value_grad], axis=-1)
        .astype(jnp.bfloat16)
        .reshape(row_count, -1)
    )
    expand_grad = jnp.dot(latent_normed.T, keyvalue_grad, preferred_element_type=jnp.float32)
    latent_normed_grad = jnp.dot(keyvalue_grad, expand_full.T, preferred_element_type=jnp.float32)
    rope_grad = unrotate(jnp.sum(key_grad[..., DN:], axis=1), cosine, sine)
    lat_weighted = latent_normed_grad * gain_lat_low.astype(jnp.float32)
    gain_lat_grad = jnp.sum(latent_normed_grad * compressed * latent_scale, axis=0)
    compressed_grad = latent_scale * lat_weighted - compressed * latent_scale**3 * jnp.mean(
        compressed * lat_weighted, axis=-1, keepdims=True
    )
    latent_grad = jnp.concatenate([compressed_grad, rope_grad], axis=-1)
    latent_grad_weight = jnp.dot(
        normed.astype(jnp.float32).T, latent_grad, precision=lax.Precision.HIGHEST
    )
    normed_grad = normed_grad + jnp.dot(
        latent_grad, latent_full.astype(jnp.float32).T, precision=lax.Precision.HIGHEST
    )
    normed_own = lax.psum_scatter(
        normed_grad.astype(jnp.bfloat16), "tensor", scatter_dimension=0, tiled=True
    ).astype(jnp.float32)
    wide_own = lax.dynamic_slice_in_dim(wide, first_row, own_rows, 0)
    scale_own = lax.dynamic_slice_in_dim(scale_one, first_row, own_rows, 0)
    hidden_grad_own = lax.dynamic_slice_in_dim(hidden_grad, first_row, own_rows, 0)
    weighted_one = normed_own * gain_one
    gain_one_grad = jnp.sum(normed_own * wide_own * scale_own, axis=0)
    tokens_grad = (
        hidden_grad_own
        + scale_own * weighted_one
        - wide_own * scale_own**3 * jnp.mean(wide_own * weighted_one, axis=-1, keepdims=True)
    )
    query_out, expand_out, output_out, shared_in_out, shared_out_out = (
        lax.psum_scatter(
            query_grad_weight.astype(jnp.bfloat16), "dp", scatter_dimension=0, tiled=True
        ).astype(jnp.float32),
        lax.psum_scatter(
            expand_grad.astype(jnp.bfloat16), "dp", scatter_dimension=0, tiled=True
        ).astype(jnp.float32),
        lax.psum_scatter(
            output_grad.astype(jnp.bfloat16), "dp", scatter_dimension=1, tiled=True
        ).astype(jnp.float32),
        lax.psum_scatter(
            shared_in_grad.astype(jnp.bfloat16), "dp", scatter_dimension=0, tiled=True
        ).astype(jnp.float32),
        lax.psum_scatter(
            shared_out_grad.astype(jnp.bfloat16), "dp", scatter_dimension=1, tiled=True
        ).astype(jnp.float32),
    )
    gain_one_out, gain_lat_out, gain_two_out, latent_out, router_out = (
        lax.psum_scatter(gain_one_grad, ("dp", "tensor"), scatter_dimension=0, tiled=True),
        lax.psum_scatter(gain_lat_grad, ("dp", "tensor"), scatter_dimension=0, tiled=True),
        lax.psum_scatter(gain_two_grad, ("dp", "tensor"), scatter_dimension=0, tiled=True),
        lax.psum_scatter(latent_grad_weight, ("dp", "tensor"), scatter_dimension=0, tiled=True),
        lax.psum_scatter(router_grad, ("dp", "tensor"), scatter_dimension=0, tiled=True),
    )
    return (
        out_tokens,
        tokens_grad,
        gain_one_out,
        gain_lat_out,
        gain_two_out,
        query_out,
        latent_out,
        expand_out,
        output_out,
        router_out,
        shared_in_out,
        shared_out_out,
        expert_in_grad,
        expert_out_grad,
    )


def solution(mesh):
    placed = (
        P(("dp", "tensor"), None),
        P("dp", None),
        P("dp", None),
        P(("dp", "tensor"), None),
        P(("dp", "tensor")),
        P(("dp", "tensor")),
        P(("dp", "tensor")),
        P("dp", "tensor"),
        P(("dp", "tensor"), None),
        P("dp", "tensor"),
        P("tensor", "dp"),
        P(("dp", "tensor"), None),
        P("dp", None, "tensor"),
        P("tensor", "dp"),
        P("dp", None, None, "tensor"),
        P("dp", "tensor", None),
    )
    return jax.shard_map(
        body,
        mesh=mesh,
        in_specs=placed,
        out_specs=(
            P(("dp", "tensor"), None),
            P(("dp", "tensor"), None),
            P(("dp", "tensor")),
            P(("dp", "tensor")),
            P(("dp", "tensor")),
            P("dp", "tensor"),
            P(("dp", "tensor"), None),
            P("dp", "tensor"),
            P("tensor", "dp"),
            P(("dp", "tensor"), None),
            P("dp", None, "tensor"),
            P("tensor", "dp"),
            P("dp", None, None, "tensor"),
            P("dp", "tensor", None),
        ),
        check_vma=False,
    )
```

profile of v0, /device:TPU:0, one launch (start us, length us, event | category | flops | bytes accessed | tf_op | source)
XLA Modules:
  0.0 2332.7 jit_solution(10668653182762681979)
XLA Ops:
  14.7 45.7 %all-reduce.7 = (bf16[2048]{0:T(1024)(128)(2,1)S(1)}, bf16[2048]{0:T(1024)(128)(2,1)S(1)}, bf16[512]{0:T(512)(128)(2,1)S(1)}) all-reduce(bf16[2048]{0:T(1024)(128)(2,1)S(1)} %dynamic-update-slice.2, bf16[2048]{0:T(1024)(128)(2,1)S(1)} %dynamic-update-slice, ...), channel_id=1, replica_groups=mesh['dp'=8,'tensor'=4] {'dp','tensor'}, use_global_device_ids=true, to_apply=%add.2 | all-reduce | flops 4608 | bytes 18432
  64.5 54.0 %all-gather.11.cloned.1.call-done = bf16[2048,576]{1,0:T(8,128)(2,1)} async-done(((bf16[64,576]{1,0:T(8,128)(2,1)}), bf16[2048,576]{1,0:T(8,128)(2,1)}) %all-gather.11.cloned.1.call-update) | async-done | bytes 2359312 | tf_op jit(solution)/shard_map/all_gather | solution.py:217
  123.1 19.5 all-gather.13.cloned.1.call-done
  150.1 26.4 %all-gather.15.cloned.1.call-done = bf16[2048,768]{1,0:T(8,128)(2,1)} async-done(((bf16[256,768]{1,0:T(8,128)(2,1)}), bf16[2048,768]{1,0:T(8,128)(2,1)}) %all-gather.15.cloned.1.call-update) | async-done | bytes 3145744 | tf_op jit(solution)/shard_map/all_gather | solution.py:207
  184.3 6.9 convolution_convert_fusion.9
  191.1 15.3 all-gather.17.cloned.1.call-done
  206.4 4.4 convolution_convert_fusion.4
  212.4 32.2 %reduce-window.19 = s32[64,24,128]{2,1,0:T(8,128)S(1)} reduce-window(s32[64,24,128]{2,1,0:T(8,128)} %fusion.106, s32[]{:T(128)} %constant.58.clone.1), window={size=1x1x128 pad=0_0x0_0x127_0}, to_apply=%region_9.10 | reduce-window | flops 24969216 | bytes 1572868 | tf_op jit(solution)/shard_map/reduce-window.2
  249.0 48.1 %all-reduce.11.cloned.1.call-done = bf16[512,2048]{1,0:T(8,128)(2,1)} async-done(((bf16[512,2048]{1,0:T(8,128)(2,1)}), bf16[512,2048]{1,0:T(8,128)(2,1)}) %all-reduce.11.cloned.1.call-update) | async-done | bytes 2097168 | tf_op jit(solution)/shard_map/psum | solution.py:239
  302.7 7.2 broadcast_in_dim.81
  309.9 20.5 reshape.464
  330.4 29.6 %scatter_custom_fusion = bf16[4608,2048]{1,0:T(8,128)(2,1)} fusion(s32[3072]{0:T(1024)S(1)} %broadcast_select_fusion, bf16[3072,2048]{1,0:T(8,128)(2,1)} %reshape.464, bf16[]{:T(256)} %constant.105.clone.1), kind=kCustom, calls=%fused_computation.34 | custom fusion | bytes 18874880
  360.0 5.9 all-to-all-start
  366.6 78.1 %all_gather.46 = bf16[2048,64]{1,0:T(8,128)(2,1)S(1)} all-gather(bf16[64,64]{1,0:T(8,128)(2,1)S(1)} %copy-done.61), channel_id=1, replica_groups=mesh['dp'=8,'tensor'=4] {'dp','tensor'}, dimensions={0}, use_global_device_ids=true | all-gather | bytes 270336 | tf_op jit(solution)/shard_map/all_gather | solution.py:218
  444.7 12.6 mul.472
  457.3 29.7 %mul.473 = f32[3072,2048]{1,0:T(8,128)} reshape(f32[512,6,2048]{2,1,0:T(8,128)} %mul.472) | data formatting | bytes 50331648 | tf_op jit(solution)/shard_map/mul | solution.py:286
  489.0 10.6 mul.471
  499.6 33.3 %scatter_custom_fusion.1 = bf16[4608,2048]{1,0:T(8,128)(2,1)} fusion(s32[3072]{0:T(1024)S(1)} %broadcast_select_fusion, f32[3072,2048]{1,0:T(8,128)} %mul.471, f32[3072,2048]{1,0:T(8,128)} %mul.473, bf16[]{:T(256)} %constant.105.clone.1), kind=kCustom, calls=%fused_computation.30 | custom fusion | flops 12582912 | bytes 69206016
  532.8 25.9 %pad_maximum_fusion = bf16[8,16,72,2048]{3,2,1,0:T(8,128)(2,1)} fusion(bf16[8,8,72,2048]{3,2,1,0:T(8,128)(2,1)} %bitcast.234, bf16[8,8,72,2048]{3,2,1,0:T(8,128)(2,1)} %bitcast.236), kind=kLoop, calls=%fused_computation.6 | loop fusion | flops 18874368 | bytes 75497472 | tf_op jit(solution)/shard_map/concatenate | solution.py:293
  558.8 16.2 all-to-all-done
  575.0 7.5 all-to-all-start.2
  582.5 30.2 %fusion.28 = f32[8,8,72,2,352]{4,2,3,0,1:T(8,128)} fusion(bf16[8,2048,2,352]{1,3,2,0:T(8,128)(2,1)} %param.30, bf16[8,8,72,2048]{3,2,1,0:T(8,128)(2,1)} %all-to-all-done), kind=kOutput, calls=%fused_computation.36 | convolution fusion | flops 13287555072 | bytes 54919168 | tf_op jit(solution)/shard_map/sxkd,xdcf->sxkcf/dot_general | solution.py:181
  612.7 20.5 convert_bitcast_fusion
  633.2 16.9 copy.134
  650.1 341.0 %all-to-all-done.2 = bf16[8,16,72,2048]{3,2,1,0:T(8,128)(2,1)} async-done(((bf16[8,16,72,2048]{3,2,1,0:T(8,128)(2,1)}), bf16[8,16,72,2048]{3,2,1,0:T(8,128)(2,1)}, u32[]{:S(2)}, u32[]{:S(2)}) %all-to-all-start.2) | async-done | bytes 37748768 | tf_op jit(solution)/shard_map/all_to_all | solution.py:294
  991.1 6.0 all-to-all-start.1
  997.8 26.1 %fusion.162 = (bf16[8,8,72,2048]{3,2,1,0:T(8,128)(2,1)}, bf16[8,8,72,2048]{3,2,1,0:T(8,128)(2,1)}) fusion(bf16[8,16,72,2048]{3,2,1,0:T(8,128)(2,1)} %all-to-all-done.2), kind=kLoop, calls=%fused_computation.236 | loop fusion | bytes 75497472 | tf_op jit(solution)/shard_map/slice | solution.py:296
  1024.0 30.2 %fusion.44 = f32[8,8,72,2,352]{4,2,0,1,3:T(8,128)} fusion(bf16[8,8,72,2048]{3,2,1,0:T(8,128)(2,1)} %get-tuple-element.81, bf16[8,2048,2,352]{1,3,2,0:T(8,128)(2,1)} %param.30), kind=kOutput, calls=%fused_computation.55 | convolution fusion | flops 13287555072 | bytes 54919168 | tf_op jit(solution)/shard_map/sxkd,xdcf->sxkcf/dot_general | solution.py:297
  1054.2 23.9 %fusion.57 = (bf16[8,8,72,1,352]{4,2,0,1,3:T(8,128)(2,1)S(1)}, bf16[8,8,72,1,352]{4,2,0,1,3:T(8,128)(2,1)}) fusion(f32[8,8,72,2,352]{4,2,0,1,3:T(8,128)} %fusion.44, bf16[8,352,2048]{2,1,0:T(8,128)(2,1)} %param.31, bf16[8,8,72,2048]{3,2,1,0:T(8,128)(2,1)} %get-tuple-element.82), kind=kOutput, calls=%fused_computation.79 | convolution fusion | flops 6664863744 | bytes 49872896 | tf_op jit(solution)/shard_map/sxkd,xfd->sxkf/dot_general | solution.py:302
  1078.1 24.2 %fusion.4 = bf16[8,8,72,2048,1]{3,2,1,0,4:T(8,128)(2,1)} fusion(bf16[8,8,72,1,352]{4,2,0,1,3:T(8,128)(2,1)} %get-tuple-element.84, bf16[8,8,72,1,352]{4,2,0,1,3:T(8,128)(2,1)S(1)} %get-tuple-element.83, bf16[8,2048,2,352]{1,3,2,0:T(8,128)(2,1)} %param.30), kind=kOutput, calls=%fused_computation.13 | convolution fusion | flops 13290799104 | bytes 48431104 | tf_op jit(solution)/shard_map/sxkcf,xdcf->sxkd/dot_general | solution.py:313
  1102.3 16.9 copy.213
  1119.2 107.4 %all-to-all-done.1 = bf16[8,8,72,2048]{3,2,1,0:T(8,128)(2,1)} async-done(((bf16[8,8,72,2048]{3,2,1,0:T(8,128)(2,1)}), bf16[8,8,72,2048]{3,2,1,0:T(8,128)(2,1)}, u32[]{:S(2)}, u32[]{:S(2)}) %all-to-all-start.1) | async-done | bytes 18874400 | tf_op jit(solution)/shard_map/all_to_all | solution.py:270
  1226.7 6.3 all-to-all-start.3
  1237.9 7.5 fusion.69
  1245.4 114.3 %all-gather.21.cloned.1.call-done = bf16[704,2048]{1,0:T(8,128)(2,1)} async-done(((bf16[704,256]{1,0:T(8,128)(2,1)}), bf16[704,2048]{1,0:T(8,128)(2,1)}) %all-gather.21.cloned.1.call-update) | async-done | bytes 2883600 | tf_op jit(solution)/shard_map/all_gather | solution.py:211
  1359.7 6.8 fusion.108
  1366.6 75.4 %gather_fusion = bf16[3072,2048]{1,0:T(8,128)(2,1)} fusion(bf16[64,72,2048]{2,1,0:T(8,128)(2,1)} %bitcast.23, s32[3072]{0:T(1024)S(1)} %bitcast.231), kind=kCustom, calls=%fused_computation | custom fusion | bytes 25190400 | tf_op jit(solution)/shard_map/gather | solution.py:272
  1442.0 22.2 reshape.448
  1464.2 20.9 multiply_reduce_fusion
  1489.3 75.3 %gather_fusion.1 = bf16[3072,2048]{1,0:T(8,128)(2,1)} fusion(bf16[64,72,2048]{2,1,0:T(8,128)(2,1)} %bitcast.37, s32[3072]{0:T(1024)S(1)} %bitcast.232), kind=kCustom, calls=%fused_computation.1 | custom fusion | bytes 25190400 | tf_op jit(solution)/shard_map/gather | solution.py:318
  1564.6 22.1 reshape.449
  1586.7 18.0 reduce_sum.193
  1604.8 10.2 fusion.51
  1615.0 5.0 convolution_convert_fusion.2
  1620.1 6.0 convolution_convert_fusion
  1627.3 6.3 add_convert_fusion.1
  1633.6 7.7 fusion.49
  1641.3 57.2 %all-reduce.13.cloned.1.call-done = bf16[512,2048]{1,0:T(8,128)(2,1)} async-done(((bf16[512,2048]{1,0:T(8,128)(2,1)}), bf16[512,2048]{1,0:T(8,128)(2,1)}) %all-reduce.13.cloned.1.call-update) | async-done | bytes 2097168 | tf_op jit(solution)/shard_map/psum | solution.py:348
  1712.2 8.6 fusion.79
  1722.9 6.8 fusion.85
  1733.8 4.9 convolution_convert_fusion.3
  1739.3 8.7 fusion.76
  1756.1 9.7 add_convert_fusion
  1769.8 5.0 fusion.169
  1775.0 8.0 fusion.101
  1787.7 20.8 reduce-scatter.24.cloned.1.call-done
  1810.7 31.5 %fusion.19 = f32[8,2048,2,352]{1,3,2,0:T(8,128)} fusion(bf16[8,8,72,2048]{3,2,1,0:T(8,128)(2,1)} %get-tuple-element.81, bf16[8,8,72,1,352]{4,2,0,1,3:T(8,128)(2,1)} %get-tuple-element.84, bf16[8,8,72,1,352]{4,2,0,1,3:T(8,128)(2,1)} %copy-done.73), kind=kOutput, calls=%fused_computation.29 | convolution fusion | flops 13290799104 | bytes 71499776 | tf_op jit(solution)/shard_map/sxkd,sxkcf->xdcf/dot_general | solution.py:310
  1842.3 23.4 %fusion.33 = f32[8,352,2048]{2,1,0:T(8,128)} fusion(bf16[8,8,72,2048]{3,2,1,0:T(8,128)(2,1)} %get-tuple-element.82, f32[8,8,72,2,352]{4,2,0,1,3:T(8,128)} %fusion.44), kind=kOutput, calls=%fused_computation.37 | convolution fusion | flops 6653509632 | bytes 54919168 | tf_op jit(solution)/shard_map/sxkf,sxkd->xfd/dot_general | solution.py:307
  1870.9 21.7 reduce-scatter.18.cloned.1.call-done
  1894.2 42.6 %reduce-scatter.20.cloned.1.call-done = bf16[512,256]{1,0:T(8,128)(2,1)} async-done(((bf16[512,2048]{1,0:T(8,128)(2,1)}), bf16[512,256]{1,0:T(8,128)(2,1)}) %reduce-scatter.20.cloned.1.call-update) | async-done | bytes 262160 | tf_op jit(solution)/shard_map/reduce_scatter | solution.py:424
  1938.7 44.1 %reduce-scatter.12.cloned.1.call-done = bf16[128,2048]{1,0:T(8,128)(2,1)} async-done(((bf16[512,2048]{1,0:T(8,128)(2,1)}), bf16[128,2048]{1,0:T(8,128)(2,1)}) %reduce-scatter.12.cloned.1.call-update) | async-done | bytes 524304 | tf_op jit(solution)/shard_map/reduce_scatter | solution.py:404
  1984.4 39.7 %all-reduce.6 = (f32[2048]{0:T(1024)S(1)}, f32[512]{0:T(512)S(1)}, f32[2048]{0:T(1024)S(1)}) all-reduce(f32[2048]{0:T(1024)S(1)} %get-tuple-element.57, f32[512]{0:T(512)S(1)} %get-tuple-element.69, f32[2048]{0:T(1024)S(1)} %get-tuple-element.87), channel_id=4, replica_groups=mesh['dp'=8,'tensor'=4] {'dp','tensor'}, use_global_device_ids=true, to_apply=%region_28.29.clone | all-reduce | flops 4608 | bytes 36864
  2033.4 137.8 %reduce-scatter.22.cloned.1.call-done = f32[64,64]{1,0:T(8,128)} async-done(((f32[2048,64]{1,0:T(8,128)}), f32[64,64]{1,0:T(8,128)}) %reduce-scatter.22.cloned.1.call-update) | async-done | bytes 16400 | tf_op jit(solution)/shard_map/reduce_scatter | solution.py:439
  2171.2 154.8 %reduce-scatter.16.cloned.1.call-done = f32[64,576]{1,0:T(8,128)} async-done(((f32[2048,576]{1,0:T(8,128)}), f32[64,576]{1,0:T(8,128)}) %reduce-scatter.16.cloned.1.call-update) | async-done | bytes 147472 | tf_op jit(solution)/shard_map/reduce_scatter | solution.py:438
  (290 shorter events, 115.4 us)
Async XLA Ops:
  7.2 55.2 %all-gather.9.cloned.1.call-start = ((), (), s32[]{:S(2)}) async-start(), calls=%async_computation.13 | async-start | bytes 2621440 | tf_op jit(solution)/shard_map/all_gather | solution.py:228
  7.9 110.5 %all-gather.11.cloned.1.call-start = ((), (), s32[]{:S(2)}) async-start(), calls=%async_computation.14 | async-start | bytes 2703360 | tf_op jit(solution)/shard_map/all_gather | solution.py:217
  8.7 133.9 %all-gather.13.cloned.1.call-start = ((), (), s32[]{:S(2)}) async-start(), calls=%async_computation.15 | async-start | bytes 1179648 | tf_op jit(solution)/shard_map/all_gather | solution.py:208
  9.4 167.1 %all-gather.15.cloned.1.call-start = ((), (), s32[]{:S(2)}) async-start(), calls=%async_computation.16 | async-start | bytes 3538944 | tf_op jit(solution)/shard_map/all_gather | solution.py:207
  10.0 196.4 %all-gather.17.cloned.1.call-start = ((), (), s32[]{:S(2)}) async-start(), calls=%async_computation.17 | async-start | bytes 2359296 | tf_op jit(solution)/shard_map/all_gather | solution.py:209
  10.6 286.5 %all-reduce.11.cloned.1.call-start = ((), (), s32[]{:S(2)}) async-start(), calls=%async_computation.18 | async-start | bytes 4194304 | tf_op jit(solution)/shard_map/psum | solution.py:239
  12.1 137.6 %copy-start.49 = (f32[512]{0:T(512)}, f32[512]{0:T(512)S(1)}, u32[]{:S(2)}) copy-start(f32[512]{0:T(512)S(1)} %fusion.133) | copy-start | bytes 6148
  12.2 137.6 %copy-start.64 = (f32[32]{0:T(128)}, f32[32]{0:T(128)S(1)}, u32[]{:S(2)}) copy-start(f32[32]{0:T(128)S(1)} %multiply_power_fusion) | copy-start | bytes 388
  60.4 116.1 %copy-start.40 = (f32[2048]{0:T(1024)}, f32[2048]{0:T(1024)S(1)}, u32[]{:S(2)}) copy-start(f32[2048]{0:T(1024)S(1)} %convert_element_type.180) | copy-start | bytes 24580
  60.4 82.2 %copy-start.59 = (f32[512]{0:T(512)}, f32[512]{0:T(512)S(1)}, u32[]{:S(2)}) copy-start(f32[512]{0:T(512)S(1)} %convert_element_type.182) | copy-start | bytes 6148
  60.7 119.8 %copy-start.31 = (f32[512,32]{0,1:T(8,128)}, f32[512,32]{0,1:T(8,128)S(1)}, u32[]{:S(2)}) copy-start(f32[512,32]{0,1:T(8,128)S(1)} %get-tuple-element.103) | copy-start | bytes 196612
  60.7 119.8 %copy-start.33 = (f32[512,32]{0,1:T(8,128)}, f32[512,32]{0,1:T(8,128)S(1)}, u32[]{:S(2)}) copy-start(f32[512,32]{0,1:T(8,128)S(1)} %get-tuple-element.104) | copy-start | bytes 196612
  64.5 112.0 %copy-start.53 = (f32[512]{0:T(512)}, f32[512]{0:T(512)S(1)}, u32[]{:S(2)}) copy-start(f32[512]{0:T(512)S(1)} %add_rsqrt_fusion.2) | copy-start | bytes 6148
  122.4 58.1 %copy-start.11 = (f32[512,576]{0,1:T(8,128)}, f32[512,576]{0,1:T(8,128)S(1)}, u32[]{:S(2)}) copy-start(f32[512,576]{0,1:T(8,128)S(1)} %fusion.161) | copy-start | bytes 3538948
  122.4 54.2 %copy-start.1 = (bf16[512,2048]{1,0:T(8,128)(2,1)S(1)}, bf16[512,2048]{1,0:T(8,128)(2,1)}, u32[]{:S(2)}) copy-start(bf16[512,2048]{1,0:T(8,128)(2,1)} %all-gather.9.cloned.1.call-done) | copy-start | bytes 6291460
  123.1 27.0 %copy-start.57 = (f32[512]{0:T(512)}, f32[512]{0:T(512)S(1)}, u32[]{:S(2)}) copy-start(f32[512]{0:T(512)S(1)} %get-tuple-element.106) | copy-start | bytes 6148
  180.6 10.5 copy-start.36
  191.1 19.6 copy-start.45
  210.8 38.0 %copy-start.67 = (s32[2]{0:T(128)S(1)}, s32[2]{0:T(128)}, u32[]{:S(2)}) copy-start(s32[2]{0:T(128)} %constant.110) | copy-start | bytes 28
  210.8 38.1 %copy-start.66 = (s32[2]{0:T(128)S(1)}, s32[2]{0:T(128)}, u32[]{:S(2)}) copy-start(s32[2]{0:T(128)} %constant.113) | copy-start | bytes 28
  211.5 88.7 %copy-start.47 = (f32[2048]{0:T(1024)}, f32[2048]{0:T(1024)S(1)}, u32[]{:S(2)}) copy-start(f32[2048]{0:T(1024)S(1)} %convert_element_type.190) | copy-start | bytes 24580
  300.2 9.7 copy-start.55
  360.0 215.1 %all-to-all-start = ((bf16[8,8,72,2048]{3,2,1,0:T(8,128)(2,1)}), bf16[8,8,72,2048]{3,2,1,0:T(8,128)(2,1)}, u32[]{:S(2)}, u32[]{:S(2)}) async-start(bf16[8,8,72,2048]{3,2,1,0:T(8,128)(2,1)} %bitcast.233), calls=%async_computation | async-start | bytes 37748736 | tf_op jit(solution)/shard_map/all_to_all | solution.py:266
  365.9 78.9 %all-gather.23.cloned.1.call-start = ((), (), s32[]{:S(2)}) async-start(), calls=%async_computation.22 | async-start | bytes 2621440 | tf_op jit(solution)/shard_map/all_gather | solution.py:283
  444.7 42.4 %copy-start.14 = (bf16[2048,64]{1,0:T(8,128)(2,1)}, bf16[2048,64]{1,0:T(8,128)(2,1)S(1)}, u32[]{:S(2)}) copy-start(bf16[2048,64]{1,0:T(8,128)(2,1)S(1)} %all_gather.46) | copy-start | bytes 786436
  457.3 29.7 %copy-start.4 = (bf16[512,2048]{1,0:T(8,128)(2,1)S(1)}, bf16[512,2048]{1,0:T(8,128)(2,1)}, u32[]{:S(2)}) copy-start(bf16[512,2048]{1,0:T(8,128)(2,1)} %copy-done.3) | copy-start | bytes 6291460
  488.0 11.5 copy-start.51
  488.8 10.8 copy-start.22
  575.0 416.1 %all-to-all-start.2 = ((bf16[8,16,72,2048]{3,2,1,0:T(8,128)(2,1)}), bf16[8,16,72,2048]{3,2,1,0:T(8,128)(2,1)}, u32[]{:S(2)}, u32[]{:S(2)}) async-start(bf16[8,16,72,2048]{3,2,1,0:T(8,128)(2,1)} %pad_maximum_fusion), calls=%async_computation.3 | async-start | bytes 75497472 | tf_op jit(solution)/shard_map/all_to_all | solution.py:294
  991.1 235.5 %all-to-all-start.1 = ((bf16[8,8,72,2048]{3,2,1,0:T(8,128)(2,1)}), bf16[8,8,72,2048]{3,2,1,0:T(8,128)(2,1)}, u32[]{:S(2)}, u32[]{:S(2)}) async-start(bf16[8,8,72,2048]{3,2,1,0:T(8,128)(2,1)} %copy.134), calls=%async_computation.1 | async-start | bytes 37748736 | tf_op jit(solution)/shard_map/all_to_all | solution.py:270
  997.1 240.8 %all-gather.19.cloned.1.call-start = ((), (), s32[]{:S(2)}) async-start(), calls=%async_computation.19 | async-start | bytes 6488064 | tf_op jit(solution)/shard_map/all_gather | solution.py:210
  1078.1 24.2 %copy-start.73 = (bf16[8,8,72,1,352]{4,2,0,1,3:T(8,128)(2,1)}, bf16[8,8,72,1,352]{4,2,0,1,3:T(8,128)(2,1)S(1)}, u32[]{:S(2)}) copy-start(bf16[8,8,72,1,352]{4,2,0,1,3:T(8,128)(2,1)S(1)} %get-tuple-element.83) | copy-start | bytes 9732100
  1226.7 262.7 %all-to-all-start.3 = ((bf16[8,8,72,2048]{3,2,1,0:T(8,128)(2,1)}), bf16[8,8,72,2048]{3,2,1,0:T(8,128)(2,1)}, u32[]{:S(2)}, u32[]{:S(2)}) async-start(bf16[8,8,72,2048]{3,2,1,0:T(8,128)(2,1)} %bitcast.235), calls=%async_computation.4 | async-start | bytes 37748736 | tf_op jit(solution)/shard_map/all_to_all | solution.py:316
  1233.0 126.7 %all-gather.21.cloned.1.call-start = ((), (), s32[]{:S(2)}) async-start(), calls=%async_computation.20 | async-start | bytes 3244032 | tf_op jit(solution)/shard_map/all_gather | solution.py:211
  1233.8 464.7 %all-reduce.13.cloned.1.call-start = ((), (), s32[]{:S(2)}) async-start(), calls=%async_computation.23 | async-start | bytes 4194304 | tf_op jit(solution)/shard_map/psum | solution.py:348
  1245.4 121.2 %copy-start = (s32[3072,1]{0,1:T(1,128)S(1)}, s32[3072,1]{0,1:T(1,128)}, u32[]{:S(2)}) copy-start(s32[3072,1]{0,1:T(1,128)} %get-tuple-element.100) | copy-start | bytes 36868
  1442.0 22.2 copy-start.23
  1464.1 21.0 copy-start.44
  1464.1 21.1 copy-start.52
  1464.1 21.1 copy-start.46
  1464.1 21.2 copy-start.15
  1586.7 18.0 copy-start.30
  1614.9 170.8 %reduce-scatter.26.cloned.1.call-start = ((), (), s32[]{:S(2)}) async-start(), calls=%async_computation.31 | async-start | bytes 3244032 | tf_op jit(solution)/shard_map/reduce_scatter | solution.py:430
  1620.1 188.4 %reduce-scatter.24.cloned.1.call-start = ((), (), s32[]{:S(2)}) async-start(), calls=%async_computation.30 | async-start | bytes 6488064 | tf_op jit(solution)/shard_map/reduce_scatter | solution.py:427
  1626.2 242.0 %reduce-scatter.10.cloned.1.call-start = ((), (), s32[]{:S(2)}) async-start(), calls=%async_computation.21 | async-start | bytes 2621440 | tf_op jit(solution)/shard_map/reduce_scatter | solution.py:278
  1633.6 64.9 %copy-start.2 = (bf16[512,2048]{1,0:T(8,128)(2,1)S(1)}, bf16[512,2048]{1,0:T(8,128)(2,1)}, u32[]{:S(2)}) copy-start(bf16[512,2048]{1,0:T(8,128)(2,1)} %all-gather.9.cloned.1.call-done) | copy-start | bytes 6291460
  1633.6 64.9 %copy-start.48 = (f32[2048]{0:T(1024)S(1)}, f32[2048]{0:T(1024)}, u32[]{:S(2)}) copy-start(f32[2048]{0:T(1024)} %copy-done.47) | copy-start | bytes 24580
  1633.6 259.0 %reduce-scatter.18.cloned.1.call-start = ((), (), s32[]{:S(2)}) async-start(), calls=%async_computation.27 | async-start | bytes 1179648 | tf_op jit(solution)/shard_map/reduce_scatter | solution.py:421
  1641.3 60.6 %copy-start.56 = (f32[512]{0:T(512)S(1)}, f32[512]{0:T(512)}, u32[]{:S(2)}) copy-start(f32[512]{0:T(512)} %copy-done.55) | copy-start | bytes 6148
  1641.3 60.6 %copy-start.63 = (f32[512]{0:T(512)S(1)}, f32[512]{0:T(512)}, u32[]{:S(2)}) copy-start(f32[512]{0:T(512)} %get-tuple-element.107) | copy-start | bytes 6148
  1709.2 11.5 copy-start.35
  1722.8 9.1 copy-start.58
  1722.9 9.1 copy-start.60
  1733.8 203.1 %reduce-scatter.20.cloned.1.call-start = ((), (), s32[]{:S(2)}) async-start(), calls=%async_computation.28 | async-start | bytes 2359296 | tf_op jit(solution)/shard_map/reduce_scatter | solution.py:424
  1738.8 11.7 copy-start.32
  1738.8 11.7 copy-start.34
  1738.8 243.9 %reduce-scatter.12.cloned.1.call-start = ((), (), s32[]{:S(2)}) async-start(), calls=%async_computation.24 | async-start | bytes 2621440 | tf_op jit(solution)/shard_map/reduce_scatter | solution.py:404
  1756.1 9.8 copy-start.29
  1756.1 9.8 copy-start.41
  1756.1 9.8 copy-start.54
  1765.9 265.5 %reduce-scatter.14.cloned.1.call-start = ((), (), s32[]{:S(2)}) async-start(), calls=%async_computation.25 | async-start | bytes 3538944 | tf_op jit(solution)/shard_map/reduce_scatter | solution.py:418
  1769.7 401.5 %reduce-scatter.22.cloned.1.call-start = ((), (), s32[]{:S(2)}) async-start(), calls=%async_computation.29 | async-start | bytes 1081344 | tf_op jit(solution)/shard_map/reduce_scatter | solution.py:439
  1774.8 551.2 %reduce-scatter.16.cloned.1.call-start = ((), (), s32[]{:S(2)}) async-start(), calls=%async_computation.26 | async-start | bytes 5406720 | tf_op jit(solution)/shard_map/reduce_scatter | solution.py:438
  1842.3 23.5 %copy-start.9 = (bf16[512,2048]{1,0:T(8,128)(2,1)S(1)}, bf16[512,2048]{1,0:T(8,128)(2,1)}, u32[]{:S(2)}) copy-start(bf16[512,2048]{1,0:T(8,128)(2,1)} %all-reduce.13.cloned.1.call-done) | copy-start | bytes 6291460
  (33 other events, 109.7 us)
Sparse Core Ops, SparseCore 0:
  9.6 49.4 all-gather.8
  61.9 56.5 all-gather.10
  120.4 22.1 all-gather.12
  144.3 32.1 all-gather.14
  178.3 28.0 all-gather.16
  210.9 86.1 all-reduce.10
  368.3 50.7 all-gather.22
  999.8 144.0 all-gather.18
  1235.7 123.9 all-gather.20
  1615.1 83.3 all-reduce.12
  1701.9 43.7 reduce-scatter.25
  1749.5 58.8 reduce-scatter.23
  1810.7 43.6 reduce-scatter.9
  1857.4 35.1 reduce-scatter.17
  1895.7 41.0 reduce-scatter.19
  1939.0 43.6 reduce-scatter.11
  1986.0 45.4 reduce-scatter.13
  2034.1 137.0 reduce-scatter.21
  2174.1 151.8 reduce-scatter.15
where the time goes:
time: 2350 us; the launch traced here: 2330 us
  waiting for transfers between devices  1230 us (52%)
  local copies, waits for them, and re-layouts  390 us (17%)
  matrix products  320 us (14%)
  other arithmetic  189 us (8%)
  blocking collectives  163 us (7%)
  starting transfers between devices  27.2 us (1%)
    all_to_all x1, waiting for transfers between devices, body(): lax.all_to_all(payload, 'dp', split_axis=0, concat_axis=0, tiled=True)  341 us
    reduce_scatter x1, waiting for transfers between devices, body(): lax.psum_scatter(latent_grad_weight, ('dp', 'tensor'), scatter_dimension=...  155 us
    reduce_scatter x1, waiting for transfers between devices, body(): lax.psum_scatter(router_grad, ('dp', 'tensor'), scatter_dimension=0, tile...  138 us
    all_gather x1, waiting for transfers between devices, body(): lax.all_gather(shared_out, 'dp', axis=1, tiled=True)  114 us
    all_to_all x1, waiting for transfers between devices, body(): lax.all_to_all(result, 'dp', split_axis=0, concat_axis=0, tiled=True)  107 us
    unnamed x2, blocking collectives  85.3 us
    all_gather x1, blocking collectives, body(): lax.all_gather(router_weight, ('dp', 'tensor'), axis=0, tiled=True)  78.1 us
    gather x1, local copies, waits for them, and re-layouts, body(): returned.reshape(EXPERTS, -1, width_model)[route_flat, slot_index]  75.4 us
  transfers between devices with their start and end apart: 23, of which 17 were waited for; matrix products, arithmetic and copies ran while one was open for 30% of the time, Pallas kernels for 0%

commit v1 on v0

v1 whole, which is shorter than its diff:
```python
import jax
import jax.numpy as jnp
from jax import lax
from jax.sharding import PartitionSpec as P

DN = 128
DR = 64
DV = 128
KVR = 512
EXPERTS = 64
TOPK = 6
CAP = 72
BOTH = ("dp", "tensor")


epsilon = 1e-06
route_scale = 2.446
rope_base = 50000.0
excluded = -1e30


def rms_scale(array_in):
    return lax.rsqrt(jnp.mean(array_in * array_in, axis=-1, keepdims=True) + epsilon)


def rope_tables(segment_row):
    places = jnp.arange(segment_row.shape[0], dtype=jnp.int32)
    begins = jnp.sum((segment_row[None, :] < segment_row[:, None]).astype(jnp.int32), axis=1)
    position = (places - begins).astype(jnp.float32)
    freqs = rope_base ** (-jnp.arange(DR // 2, dtype=jnp.float32) * 2.0 / DR)
    angle = position[:, None] * freqs[None, :]
    return (jnp.cos(angle), jnp.sin(angle))


def rotate(array_in, cosine, sine):
    half_width = array_in.shape[-1] // 2
    first_half, second_half = (array_in[..., :half_width], array_in[..., half_width:])
    return jnp.concatenate(
        [first_half * cosine - second_half * sine, second_half * cosine + first_half * sine],
        axis=-1,
    )


def unrotate(array_in, cosine, sine):
    half_width = array_in.shape[-1] // 2
    first_half, second_half = (array_in[..., :half_width], array_in[..., half_width:])
    return jnp.concatenate(
        [first_half * cosine + second_half * sine, second_half * cosine - first_half * sine],
        axis=-1,
    )


def attention_tables(normed, query_weight, latent_weight, expand_weight, latent_gain, cosine, sine):
    row_count = normed.shape[0]
    head_count = query_weight.shape[1] // (DN + DR)
    query = jnp.dot(normed, query_weight, preferred_element_type=jnp.float32).reshape(
        row_count, head_count, DN + DR
    )
    query = jnp.concatenate(
        [query[..., :DN], rotate(query[..., DN:], cosine[:, None, :], sine[:, None, :])], axis=-1
    ).astype(jnp.bfloat16)
    latent = jnp.dot(normed, latent_weight, preferred_element_type=jnp.float32)
    compressed = latent[:, :KVR]
    latent_scale = rms_scale(compressed)
    latent_normed = (compressed * latent_scale * latent_gain.astype(jnp.float32)).astype(
        jnp.bfloat16
    )
    rope_key = rotate(latent[:, KVR:], cosine, sine)
    keyvalue = jnp.dot(latent_normed, expand_weight, preferred_element_type=jnp.float32).reshape(
        row_count, head_count, DN + DV
    )
    key_rows = jnp.concatenate(
        [keyvalue[..., :DN], jnp.broadcast_to(rope_key[:, None, :], (row_count, head_count, DR))],
        axis=-1,
    ).astype(jnp.bfloat16)
    value_rows = keyvalue[..., DN:].astype(jnp.bfloat16)
    return (query, key_rows, value_rows, compressed, latent_scale, latent_normed)


def masked_scores(query, key_rows, segment_row):
    scores = jnp.einsum(
        "qhd,khd->hqk", query, key_rows, preferred_element_type=jnp.float32
    ) * query.shape[-1] ** (-0.5)
    places = jnp.arange(key_rows.shape[0], dtype=jnp.int32)
    allowed = (segment_row[None, :] == segment_row[:, None]) & (places[None, :] <= places[:, None])
    return jnp.where(allowed[None], scores, excluded)


def attend(query, key_rows, value_rows, segment_row):
    scores = masked_scores(query, key_rows, segment_row)
    logsum = jnp.log(jnp.sum(jnp.exp(scores), axis=-1))
    weights_low = jnp.exp(scores - logsum[..., None]).astype(jnp.bfloat16)
    mixed = jnp.einsum(
        "hqk,khd->qhd", weights_low, value_rows, preferred_element_type=jnp.float32
    ).astype(jnp.bfloat16)
    return (mixed, logsum)


def attend_back(query, key_rows, value_rows, segment_row, out_grad, logsum):
    scores = masked_scores(query, key_rows, segment_row)
    weights_full = jnp.exp(scores - logsum[..., None])
    weights_low = weights_full.astype(jnp.bfloat16)
    prob_grad = jnp.einsum("qhd,khd->hqk", out_grad, value_rows, preferred_element_type=jnp.float32)
    row_total = jnp.sum(weights_full * prob_grad, axis=-1, keepdims=True)
    score_grad = (weights_full * (prob_grad - row_total) * query.shape[-1] ** (-0.5)).astype(
        jnp.bfloat16
    )
    query_grad = jnp.einsum("hqk,khd->qhd", score_grad, key_rows, preferred_element_type=jnp.float32)
    key_grad = jnp.einsum("hqk,qhd->khd", score_grad, query, preferred_element_type=jnp.float32)
    value_grad = jnp.einsum("hqk,qhd->khd", weights_low, out_grad, preferred_element_type=jnp.float32)
    return (query_grad, key_grad, value_grad)


def swiglu_grad(hidden_grad, gate_pre, up_pre):
    sigm = jax.nn.sigmoid(gate_pre)
    return (
        hidden_grad * up_pre * sigm * (1.0 + gate_pre * (1.0 - sigm)),
        hidden_grad * jax.nn.silu(gate_pre),
    )


def gather(array_in, axis_name, axis=0):
    return lax.all_gather(array_in, axis_name, axis=axis, tiled=True)


def scatter_sum(array_in, axis_name, axis=0):
    return lax.psum_scatter(array_in, axis_name, scatter_dimension=axis, tiled=True)


def own_slice(array_in, first_row, own_rows):
    return lax.dynamic_slice_in_dim(array_in, first_row, own_rows, 0)


def body(
    tokens,
    segments,
    routes,
    cotangent,
    attention_gain,
    latent_gain,
    feedforward_gain,
    query_weight,
    latent_weight,
    expand_weight,
    output_weight,
    router_weight,
    shared_in,
    shared_out,
    expert_in,
    expert_out,
):
    own_rows, width = tokens.shape
    groups = lax.axis_size("dp")
    place_dp = lax.axis_index("dp")
    first_row = lax.axis_index("tensor") * own_rows
    local_experts = expert_in.shape[0]
    segment_row = segments[0]
    group_rows = gather(tokens, "tensor")
    row_count = group_rows.shape[0]
    gain_one_low, gain_lat_low, gain_two_low = (
        gather(attention_gain, BOTH),
        gather(latent_gain, BOTH),
        gather(feedforward_gain, BOTH),
    )
    latent_full = gather(latent_weight, BOTH)
    expand_full = gather(expand_weight, "dp")
    query_full = gather(query_weight, "dp")
    output_full = gather(output_weight, "dp", 1)
    router_full = gather(router_weight, BOTH)
    routes_all = gather(routes, "dp")
    shared_in_full = gather(shared_in, "dp")
    shared_out_full = gather(shared_out, "dp", 1)
    gain_one = gain_one_low.astype(jnp.float32)
    gain_two = gain_two_low.astype(jnp.float32)

    wide = group_rows.astype(jnp.float32)
    scale_one = rms_scale(wide)
    normed = (wide * scale_one * gain_one).astype(jnp.bfloat16)
    cosine, sine = rope_tables(segment_row)
    query, key_rows, value_rows, compressed, latent_scale, latent_normed = attention_tables(
        normed, query_full, latent_full, expand_full, gain_lat_low, cosine, sine
    )
    mixed, logsum = attend(query, key_rows, value_rows, segment_row)
    mixed_flat = mixed.reshape(row_count, -1)
    attention_own = scatter_sum(
        jnp.dot(mixed_flat, output_full, preferred_element_type=jnp.float32).astype(jnp.bfloat16),
        "tensor",
    )
    wide_own = tokens.astype(jnp.float32)
    hidden = wide_own + attention_own.astype(jnp.float32)
    scale_two = rms_scale(hidden)
    normed_two_own = (hidden * scale_two * gain_two).astype(jnp.bfloat16)

    cot_group = gather(cotangent, "tensor")
    cot_all = gather(cot_group, "dp").reshape(groups, row_count, width)
    normed_two = gather(normed_two_own, "tensor")
    normed_all = gather(normed_two, "dp").reshape(groups, row_count, width)

    expert_ids = jnp.arange(EXPERTS, dtype=jnp.int32)
    chosen = jnp.any(routes_all[:, :, None] == expert_ids[None, None, :], axis=1)
    logits = jnp.dot(
        normed_all.reshape(groups * row_count, width),
        router_full,
        preferred_element_type=jnp.float32,
    )
    sigm = jnp.where(chosen, jax.nn.sigmoid(logits), 0.0)
    picked_total = jnp.sum(sigm, axis=1, keepdims=True)
    gate_dense = route_scale * sigm / picked_total
    first_expert = place_dp * local_experts
    gate_local = lax.dynamic_slice_in_dim(gate_dense, first_expert, local_experts, 1)
    chosen_local = lax.dynamic_slice_in_dim(
        chosen.astype(jnp.bfloat16), first_expert, local_experts, 1
    ).reshape(groups, row_count, local_experts)
    gate_local = jnp.swapaxes(gate_local.reshape(groups, row_count, local_experts), 1, 2)
    places = jnp.arange(row_count, dtype=jnp.int32)
    below = (places[None, :] < places[:, None]).astype(jnp.bfloat16)
    rank = jnp.einsum("ts,gse->get", below, chosen_local, preferred_element_type=jnp.float32)
    slot = jnp.where(jnp.swapaxes(chosen_local, 1, 2) > 0, rank, -1.0).astype(jnp.int32)
    is_slot = slot[:, :, None, :] == jnp.arange(CAP, dtype=jnp.int32)[None, None, :, None]
    pick = is_slot.astype(jnp.bfloat16).reshape(groups, local_experts * CAP, row_count)
    gate_slot = jnp.sum(jnp.where(is_slot, gate_local[:, :, None, :], 0.0), axis=-1)

    rows = jnp.einsum(
        "gst,gtd->gsd", pick, normed_all, preferred_element_type=jnp.float32
    ).astype(jnp.bfloat16).reshape(groups, local_experts, CAP, width)
    cots = jnp.einsum(
        "gst,gtd->gsd", pick, cot_all, preferred_element_type=jnp.float32
    ).astype(jnp.bfloat16).reshape(groups, local_experts, CAP, width)
    expert_pre = jnp.einsum(
        "sxkd,xdcf->sxkcf", rows, expert_in, preferred_element_type=jnp.float32
    )
    gate_pre, up_pre = (expert_pre[..., 0, :], expert_pre[..., 1, :])
    act = jax.nn.silu(gate_pre) * up_pre
    hid_raw = jnp.einsum("sxkd,xfd->sxkf", cots, expert_out, preferred_element_type=jnp.float32)
    gate_grad_slot = jnp.sum(act * hid_raw, axis=-1)
    act_gated = (act * gate_slot[..., None]).astype(jnp.bfloat16)
    gate_part, up_part = swiglu_grad(hid_raw * gate_slot[..., None], gate_pre, up_pre)
    expert_pre_grad = jnp.stack([gate_part, up_part], axis=-2).astype(jnp.bfloat16)
    back_slots = jnp.einsum(
        "sxkcf,xdcf->sxkd", expert_pre_grad, expert_in, preferred_element_type=jnp.float32
    ).astype(jnp.bfloat16).reshape(groups, local_experts * CAP, width)
    out_slots = jnp.einsum(
        "sxkf,xfd->sxkd", act_gated, expert_out, preferred_element_type=jnp.float32
    ).astype(jnp.bfloat16).reshape(groups, local_experts * CAP, width)
    expert_out_grad = jnp.einsum(
        "sxkf,sxkd->xfd", act_gated, cots, preferred_element_type=jnp.float32
    )
    expert_in_grad = jnp.einsum(
        "sxkd,sxkcf->xdcf", rows, expert_pre_grad, preferred_element_type=jnp.float32
    )
    gate_grad_local = jnp.sum(jnp.where(is_slot, gate_grad_slot[..., None], 0.0), axis=2)
    gate_grad_all = lax.dynamic_update_slice_in_dim(
        jnp.zeros((groups * row_count, 2 * EXPERTS), jnp.bfloat16),
        jnp.swapaxes(gate_grad_local, 1, 2)
        .reshape(groups * row_count, local_experts)
        .astype(jnp.bfloat16),
        first_expert,
        1,
    )

    shared_pre = jnp.einsum(
        "gd,dcf->gcf", normed_two, shared_in_full, preferred_element_type=jnp.float32
    )
    shared_act = (jax.nn.silu(shared_pre[:, 0]) * shared_pre[:, 1]).astype(jnp.bfloat16)
    shared_part = jnp.dot(shared_act, shared_out_full, preferred_element_type=jnp.float32)
    shared_hidden_grad = jnp.dot(cot_group, shared_out_full.T, preferred_element_type=jnp.float32)
    shared_gate_part, shared_up_part = swiglu_grad(
        shared_hidden_grad, shared_pre[:, 0], shared_pre[:, 1]
    )
    shared_pre_grad = jnp.stack([shared_gate_part, shared_up_part], axis=1).astype(jnp.bfloat16)
    shared_out_grad = jnp.dot(shared_act.T, cot_group, preferred_element_type=jnp.float32)
    shared_in_grad = jnp.einsum(
        "gd,gcf->dcf", normed_two, shared_pre_grad, preferred_element_type=jnp.float32
    )
    shared_back = jnp.einsum(
        "gcf,dcf->gd", shared_pre_grad, shared_in_full, preferred_element_type=jnp.float32
    )
    mine = (jnp.arange(groups, dtype=jnp.int32) == place_dp)[:, None, None]

    def combine(slots, shared):
        total = jnp.einsum("gst,gsd->gtd", pick, slots, preferred_element_type=jnp.float32)
        total = total + jnp.where(mine, shared[None], 0.0)
        return total.astype(jnp.bfloat16).reshape(groups * row_count, width)

    back_sum = combine(back_slots, shared_back)
    back_sum = jnp.concatenate([back_sum, gate_grad_all], axis=1)
    back_own = scatter_sum(scatter_sum(back_sum, "dp"), "tensor").astype(jnp.float32)
    out_sum = combine(out_slots, shared_part)
    out_own = scatter_sum(scatter_sum(out_sum, "dp"), "tensor").astype(jnp.float32)
    out_tokens = (hidden + out_own).astype(jnp.bfloat16)

    first_token = place_dp * row_count + first_row
    sigm_own = own_slice(sigm, first_token, own_rows)
    total_own = own_slice(picked_total, first_token, own_rows)
    gate_grad = back_own[:, width : width + EXPERTS]
    picked_grad = route_scale * (
        gate_grad / total_own
        - jnp.sum(gate_grad * sigm_own, axis=1, keepdims=True) / (total_own * total_own)
    )
    logit_grad = picked_grad * sigm_own * (1.0 - sigm_own)
    router_grad = jnp.dot(
        normed_two_own.astype(jnp.float32).T, logit_grad, precision=lax.Precision.HIGHEST
    )
    router_back = jnp.dot(
        logit_grad, router_full.astype(jnp.float32).T, precision=lax.Precision.HIGHEST
    )
    normed_two_grad = back_own[:, :width] + router_back
    weighted_two = normed_two_grad * gain_two
    hidden_grad = (
        cotangent.astype(jnp.float32)
        + scale_two * weighted_two
        - hidden * scale_two**3 * jnp.mean(hidden * weighted_two, axis=-1, keepdims=True)
    )
    gain_two_grad = jnp.sum(normed_two_grad * hidden * scale_two, axis=0)
    hidden_low = gather(hidden_grad.astype(jnp.bfloat16), "tensor")

    output_grad = jnp.dot(mixed_flat.T, hidden_low, preferred_element_type=jnp.float32)
    mixed_grad = (
        jnp.dot(hidden_low, output_full.T, preferred_element_type=jnp.float32)
        .astype(jnp.bfloat16)
        .reshape(mixed.shape)
    )
    query_grad, key_grad, value_grad = attend_back(
        query, key_rows, value_rows, segment_row, mixed_grad, logsum
    )
    query_pre = (
        jnp.concatenate(
            [
                query_grad[..., :DN],
                unrotate(query_grad[..., DN:], cosine[:, None, :], sine[:, None, :]),
            ],
            axis=-1,
        )
        .astype(jnp.bfloat16)
        .reshape(row_count, -1)
    )
    query_grad_weight = jnp.dot(normed.T, query_pre, preferred_element_type=jnp.float32)
    normed_grad = jnp.dot(query_pre, query_full.T, preferred_element_type=jnp.float32)
    keyvalue_grad = (
        jnp.concatenate([key_grad[..., :DN], value_grad], axis=-1)
        .astype(jnp.bfloat16)
        .reshape(row_count, -1)
    )
    expand_grad = jnp.dot(latent_normed.T, keyvalue_grad, preferred_element_type=jnp.float32)
    latent_normed_grad = jnp.dot(keyvalue_grad, expand_full.T, preferred_element_type=jnp.float32)
    rope_grad = unrotate(jnp.sum(key_grad[..., DN:], axis=1), cosine, sine)
    lat_weighted = latent_normed_grad * gain_lat_low.astype(jnp.float32)
    gain_lat_grad = jnp.sum(latent_normed_grad * compressed * latent_scale, axis=0)
    compressed_grad = latent_scale * lat_weighted - compressed * latent_scale**3 * jnp.mean(
        compressed * lat_weighted, axis=-1, keepdims=True
    )
    latent_grad = jnp.concatenate([compressed_grad, rope_grad], axis=-1).astype(jnp.bfloat16)
    latent_grad_weight = jnp.dot(normed.T, latent_grad, preferred_element_type=jnp.float32)
    normed_grad = normed_grad + jnp.dot(
        latent_grad, latent_full.T, preferred_element_type=jnp.float32
    )
    normed_own = scatter_sum(normed_grad.astype(jnp.bfloat16), "tensor").astype(jnp.float32)
    scale_own = own_slice(scale_one, first_row, own_rows)
    weighted_one = normed_own * gain_one
    gain_one_grad = jnp.sum(normed_own * wide_own * scale_own, axis=0)
    tokens_grad = (
        hidden_grad
        + scale_own * weighted_one
        - wide_own * scale_own**3 * jnp.mean(wide_own * weighted_one, axis=-1, keepdims=True)
    )

    shared_out_out = scatter_sum(shared_out_grad.astype(jnp.bfloat16), "dp", 1).astype(jnp.float32)
    shared_in_out = scatter_sum(shared_in_grad.astype(jnp.bfloat16), "dp").astype(jnp.float32)
    output_out = scatter_sum(output_grad.astype(jnp.bfloat16), "dp", 1).astype(jnp.float32)
    expand_out = scatter_sum(expand_grad.astype(jnp.bfloat16), "dp").astype(jnp.float32)
    query_out = scatter_sum(query_grad_weight.astype(jnp.bfloat16), "dp").astype(jnp.float32)
    lat_rows = latent_gain.shape[0]
    gain_rows = attention_gain.shape[0]
    lat_column = jnp.pad(
        gain_lat_grad.reshape(-1, lat_rows), ((0, 0), (0, gain_rows - lat_rows))
    ).reshape(-1)
    columns = jnp.stack([gain_one_grad, gain_two_grad, lat_column], axis=1)
    latent_columns = latent_grad_weight.shape[1]
    small = jnp.concatenate([latent_grad_weight, router_grad, columns], axis=1)
    small = jnp.pad(small, ((0, 0), (0, -small.shape[1] % 128))).astype(jnp.bfloat16)
    small = scatter_sum(scatter_sum(small, "dp"), "tensor").astype(jnp.float32)
    latent_out = small[:, :latent_columns]
    router_out = small[:, latent_columns : latent_columns + EXPERTS]
    last = latent_columns + EXPERTS
    gain_one_out = small[:, last]
    gain_two_out = small[:, last + 1]
    gain_lat_out = small[:lat_rows, last + 2]
    return (
        out_tokens,
        tokens_grad,
        gain_one_out,
        gain_lat_out,
        gain_two_out,
        query_out,
        latent_out,
        expand_out,
        output_out,
        router_out,
        shared_in_out,
        shared_out_out,
        expert_in_grad,
        expert_out_grad,
    )


def solution(mesh):
    placed = (
        P(("dp", "tensor"), None),
        P("dp", None),
        P("dp", None),
        P(("dp", "tensor"), None),
        P(("dp", "tensor")),
        P(("dp", "tensor")),
        P(("dp", "tensor")),
        P("dp", "tensor"),
        P(("dp", "tensor"), None),
        P("dp", "tensor"),
        P("tensor", "dp"),
        P(("dp", "tensor"), None),
        P("dp", None, "tensor"),
        P("tensor", "dp"),
        P("dp", None, None, "tensor"),
        P("dp", "tensor", None),
    )
    return jax.shard_map(
        body,
        mesh=mesh,
        in_specs=placed,
        out_specs=(
            P(("dp", "tensor"), None),
            P(("dp", "tensor"), None),
            P(("dp", "tensor")),
            P(("dp", "tensor")),
            P(("dp", "tensor")),
            P("dp", "tensor"),
            P(("dp", "tensor"), None),
            P("dp", "tensor"),
            P("tensor", "dp"),
            P(("dp", "tensor"), None),
            P("dp", None, "tensor"),
            P("tensor", "dp"),
            P("dp", None, None, "tensor"),
            P("dp", "tensor", None),
        ),
        check_vma=False,
    )
```

time: 2350 us -> 1630 us (0.69)
  local copies, waits for them, and re-layouts: 390 us -> 67.6 us
  waiting for transfers between devices: 1230 us -> 969 us
  other arithmetic: 189 us -> 74.5 us
  matrix products: 320 us -> 364 us
  blocking collectives: 163 us -> 125 us
  starting transfers between devices: 27.2 us -> 1.74 us
    all_to_all x4 -> x0, waiting for transfers between devices: 465 us -> none  [the longest x1 341 us: body(): lax.all_to_all(payload, 'dp', split_axis=0, concat_axis=0, tiled=True)]
    all_gather x8 -> x12, waiting for transfers between devices: 229 us -> 381 us  [gather(): return lax.all_gather(array_in, axis_name, axis=axis, tiled=True)]
    gather x2 -> x0, local copies, waits for them, and re-layouts: 151 us -> none  [the longest x1 75.4 us: body(): returned.reshape(EXPERTS, -1, width_model)[route_flat, slot_index]]
    reduce_scatter x9 -> x12, waiting for transfers between devices: 424 us -> 562 us  [scatter_sum(): lax.psum_scatter(array_in, axis_name, scatter_dimension=axis, tiled=True)]
    psum x2 -> x0, waiting for transfers between devices: 105 us -> none  [the longest x1 57.2 us: body(): lax.psum((routed_back + shared_back + router_back).astype(jnp.bfloat16),...]
    mul x3 -> x0, local copies, waits for them, and re-layouts: 53 us -> none  [the longest x2 42.3 us: body(): gate_weights[..., None] * grad_wide[:, None, :]]
    dot_general x18 -> x22, matrix products: 232 us -> 274 us  [the longest x2 50.5 us: combine(): jnp.einsum('gst,gsd->gtd', pick, slots, preferred_element_type=jnp.float32)]
    unnamed x2 -> x1, blocking collectives: 85.3 us -> 44.6 us
  transfers between devices with their start and end apart: 23 -> 25, of which waited for: 17 -> 20; matrix products, arithmetic and copies ran while one was open for 30% -> 16% of each run, Pallas kernels for 0% -> 0%
where the time goes in v1:
time: 1630 us; the launch traced here: 1620 us
  waiting for transfers between devices  969 us (59%)
  matrix products  364 us (22%)
  blocking collectives  125 us (8%)
  other arithmetic  74.5 us (5%)
  local copies, waits for them, and re-layouts  67.6 us (4%)
    reduce_scatter x12, waiting for transfers between devices, scatter_sum(): lax.psum_scatter(array_in, axis_name, scatter_dimension=axis, tiled=True)  562 us
    all_gather x12, waiting for transfers between devices, gather(): return lax.all_gather(array_in, axis_name, axis=axis, tiled=True)  381 us
    all_gather x2, blocking collectives, gather(): return lax.all_gather(array_in, axis_name, axis=axis, tiled=True)  79.9 us
    dot_general x2, matrix products, combine(): jnp.einsum('gst,gsd->gtd', pick, slots, preferred_element_type=jnp.float32)  50.5 us
    unnamed x1, blocking collectives  44.6 us
  transfers between devices with their start and end apart: 25, of which 20 were waited for; matrix products, arithmetic and copies ran while one was open for 16% of the time, Pallas kernels for 0%

profile of v1, /device:TPU:0, one launch (start us, length us, event | category | flops | bytes accessed | tf_op | source)
XLA Modules:
  0.0 1616.8 jit_solution(15007705718040744759)
XLA Ops:
  14.2 44.6 %all-reduce.5 = (bf16[2048]{0:T(1024)(128)(2,1)S(1)}, bf16[512]{0:T(512)(128)(2,1)S(1)}, bf16[2048]{0:T(1024)(128)(2,1)S(1)}) all-reduce(bf16[2048]{0:T(1024)(128)(2,1)S(1)} %dynamic-update-slice, bf16[512]{0:T(512)(128)(2,1)S(1)} %dynamic-update-slice.1, ...), channel_id=1, replica_groups=mesh['dp'=8,'tensor'=4] {'dp','tensor'}, use_global_device_ids=true, to_apply=%add.2 | all-reduce | flops 4608 | bytes 18432
  62.9 55.6 %all-gather.15.cloned.1.call-done = bf16[2048,576]{1,0:T(8,128)(2,1)} async-done(((bf16[64,576]{1,0:T(8,128)(2,1)}), bf16[2048,576]{1,0:T(8,128)(2,1)}) %all-gather.15.cloned.1.call-update) | async-done | bytes 2359312 | tf_op jit(solution)/shard_map/all_gather | solution.py:123
  118.5 3.9 fusion.142
  123.2 19.4 %all-gather.17.cloned.1.call-done = bf16[512,1024]{1,0:T(8,128)(2,1)} async-done(((bf16[64,1024]{1,0:T(8,128)(2,1)}), bf16[512,1024]{1,0:T(8,128)(2,1)}) %all-gather.17.cloned.1.call-update) | async-done | bytes 1048592 | tf_op jit(solution)/shard_map/all_gather | solution.py:123
  145.6 30.9 %all-gather.19.cloned.1.call-done = bf16[2048,768]{1,0:T(8,128)(2,1)} async-done(((bf16[256,768]{1,0:T(8,128)(2,1)}), bf16[2048,768]{1,0:T(8,128)(2,1)}) %all-gather.19.cloned.1.call-update) | async-done | bytes 3145744 | tf_op jit(solution)/shard_map/all_gather | solution.py:123
  176.5 4.4 fusion.140
  182.0 2.8 fusion.87
  184.8 6.0 convolution_convert_fusion.13
  190.8 15.6 all-gather.21.cloned.1.call-done
  206.4 4.2 convolution_convert_fusion.7
  211.5 42.9 %reduce-scatter.16.cloned.1.call-done = bf16[128,2048]{1,0:T(8,128)(2,1)} async-done(((bf16[512,2048]{1,0:T(8,128)(2,1)}), bf16[128,2048]{1,0:T(8,128)(2,1)}) %reduce-scatter.16.cloned.1.call-update) | async-done | bytes 524304 | tf_op jit(solution)/shard_map/reduce_scatter | solution.py:127
  260.2 40.7 %all-gather.31.cloned.1.call-done = bf16[512,2048]{1,0:T(8,128)(2,1)} async-done(((bf16[128,2048]{1,0:T(8,128)(2,1)}), bf16[512,2048]{1,0:T(8,128)(2,1)}) %all-gather.31.cloned.1.call-update) | async-done | bytes 2097168 | tf_op jit(solution)/shard_map/all_gather | solution.py:123
  301.0 46.6 %all-gather.23.cloned.1.call-done = bf16[512,2048]{1,0:T(8,128)(2,1)} async-done(((bf16[128,2048]{1,0:T(8,128)(2,1)}), bf16[512,2048]{1,0:T(8,128)(2,1)}) %all-gather.23.cloned.1.call-update) | async-done | bytes 2097168 | tf_op jit(solution)/shard_map/all_gather | solution.py:123
  347.7 9.6 all_gather.58
  361.1 70.3 %all_gather.62 = bf16[2048,64]{1,0:T(8,128)(2,1)S(1)} all-gather(bf16[64,64]{1,0:T(8,128)(2,1)S(1)} %copy-done.55), channel_id=1, replica_groups=mesh['dp'=8,'tensor'=4] {'dp','tensor'}, dimensions={0}, use_global_device_ids=true | all-gather | bytes 270336 | tf_op jit(solution)/shard_map/all_gather | solution.py:123
  431.4 8.0 fusion.57
  439.5 7.0 fusion.86
  447.5 5.1 convolution_bitcast_fusion
  452.7 66.3 %all-gather.33.cloned.1.call-done = bf16[4096,2048]{1,0:T(8,128)(2,1)} async-done(((bf16[512,2048]{1,0:T(8,128)(2,1)}), bf16[4096,2048]{1,0:T(8,128)(2,1)}) %all-gather.33.cloned.1.call-update) | async-done | bytes 16777232 | tf_op jit(solution)/shard_map/all_gather | solution.py:123
  518.9 18.8 %convolution_convert_fusion = bf16[8,576,2048]{2,1,0:T(8,128)(2,1)} fusion(pred[8,576,512]{2,1,0:T(32,128)(4,1)S(1)} %bitcast_compare_fusion, bf16[8,512,2048]{2,1,0:T(8,128)(2,1)} %bitcast.232), kind=kOutput, calls=%fused_computation.20 | convolution fusion | flops 9673113600 | bytes 38010880 | tf_op jit(solution)/shard_map/gst,gtd->gsd/dot_general | solution.py:226
  537.7 72.7 %all-gather.25.cloned.1.call-done = bf16[4096,2048]{1,0:T(8,128)(2,1)} async-done(((bf16[512,2048]{1,0:T(8,128)(2,1)}), bf16[4096,2048]{1,0:T(8,128)(2,1)}) %all-gather.25.cloned.1.call-update) | async-done | bytes 16777232 | tf_op jit(solution)/shard_map/all_gather | solution.py:123
  610.4 18.8 %convolution_convert_fusion.1 = bf16[8,576,2048]{2,1,0:T(8,128)(2,1)} fusion(pred[8,576,512]{2,1,0:T(32,128)(4,1)S(1)} %bitcast_compare_fusion, bf16[8,512,2048]{2,1,0:T(8,128)(2,1)} %bitcast.231), kind=kOutput, calls=%fused_computation.21 | convolution fusion | flops 9673113600 | bytes 38010880 | tf_op jit(solution)/shard_map/gst,gtd->gsd/dot_general | solution.py:223
  629.2 30.5 %fusion.19 = f32[8,8,72,2,352]{4,2,3,0,1:T(8,128)} fusion(bf16[8,2048,2,352]{1,3,2,0:T(8,128)(2,1)} %param.30, bf16[8,8,72,2048,1]{3,2,1,0,4:T(8,128)(2,1)} %bitcast.235), kind=kOutput, calls=%fused_computation.28 | convolution fusion | flops 13287555072 | bytes 54919168 | tf_op jit(solution)/shard_map/sxkd,xdcf->sxkcf/dot_general | solution.py:229
  659.7 23.5 %fusion.27 = (f32[8,8,72]{2,0,1:T(8,128)S(1)}, f32[8,8,72,352]{3,2,1,0:T(8,128)}) fusion(f32[8,8,72,2,352]{4,2,3,0,1:T(8,128)} %fusion.19, bf16[8,352,2048]{2,1,0:T(8,128)(2,1)} %param.31, bf16[8,8,72,2048]{3,2,1,0:T(8,128)(2,1)} %bitcast.233), kind=kOutput, calls=%fused_computation.35 | convolution fusion | flops 6655127040 | bytes 49891328 | tf_op jit(solution)/shard_map/sxkd,xfd->sxkf/dot_general | solution.py:234
  683.1 8.4 fusion.144
  694.7 4.3 select_reduce_fusion
  699.0 11.1 fusion.44
  710.1 28.5 %fusion.4 = bf16[8,8,72,2048,1]{3,2,0,1,4:T(8,128)(2,1)} fusion(bf16[8,2048,2,352]{1,3,2,0:T(8,128)(2,1)} %param.30, bf16[8,8,72,1,352]{4,2,0,1,3:T(8,128)(2,1)S(1)} %get-tuple-element.88, bf16[8,8,72,1,352]{4,2,0,1,3:T(8,128)(2,1)S(1)} %get-tuple-element.87), kind=kOutput, calls=%fused_computation.7 | convolution fusion | flops 13290799104 | bytes 48431104 | tf_op jit(solution)/shard_map/sxkcf,xdcf->sxkd/dot_general | solution.py:239
  738.6 9.2 copy.184
  747.8 6.7 copy.119
  754.9 24.7 %add_convert_fusion = bf16[8,512,2048]{2,1,0:T(8,128)(2,1)} fusion(pred[8,576,512]{2,1,0:T(32,128)(4,1)} %copy-done.18, bf16[8,576,2048]{2,1,0:T(8,128)(2,1)} %bitcast.209, f32[512,2048]{1,0:T(8,128)} %convolution_bitcast_fusion, pred[8]{0:T(512)(128)(4,1)S(1)} %copy-done.77), kind=kOutput, calls=%fused_computation.3 | convolution fusion | flops 9688842240 | bytes 42205192 | tf_op jit(solution)/shard_map/gst,gsd->gtd/dot_general | solution.py:281
  779.7 3.9 dynamic_update_slice.3
  783.6 15.6 pad_maximum_fusion
  799.4 124.6 %reduce-scatter.22.cloned.1.call-done = bf16[512,2176]{1,0:T(8,128)(2,1)} async-done(((bf16[4096,2176]{1,0:T(8,128)(2,1)}), bf16[512,2176]{1,0:T(8,128)(2,1)}) %reduce-scatter.22.cloned.1.call-update) | async-done | bytes 2228240 | tf_op jit(solution)/shard_map/reduce_scatter | solution.py:127
  924.1 47.8 %reduce-scatter.24.cloned.1.call-done = bf16[128,2176]{1,0:T(8,128)(2,1)} async-done(((bf16[512,2176]{1,0:T(8,128)(2,1)}), bf16[128,2176]{1,0:T(8,128)(2,1)}) %reduce-scatter.24.cloned.1.call-update) | async-done | bytes 557072 | tf_op jit(solution)/shard_map/reduce_scatter | solution.py:127
  978.5 7.8 fusion.40
  986.3 3.8 fusion.145
  990.1 33.3 %all-gather.35.cloned.1.call-done = bf16[512,2048]{1,0:T(8,128)(2,1)} async-done(((bf16[128,2048]{1,0:T(8,128)(2,1)}), bf16[512,2048]{1,0:T(8,128)(2,1)}) %all-gather.35.cloned.1.call-update) | async-done | bytes 2097168 | tf_op jit(solution)/shard_map/all_gather | solution.py:123
  1023.4 3.5 convolution_convert_fusion.11
  1029.7 6.7 fusion.72
  1036.4 8.5 fusion.67
  1047.4 8.5 fusion.64
  1059.5 2.8 multiply_reduce_fusion.1
  1065.1 3.2 add_convert_fusion.2
  1068.4 17.6 %convert_bitcast_fusion = bf16[8,8,72,2048]{3,2,0,1:T(8,128)(2,1)} fusion(bf16[8,8,72,352]{3,2,0,1:T(8,128)(2,1)} %get-tuple-element.89, bf16[8,352,2048]{2,1,0:T(8,128)(2,1)} %param.31), kind=kOutput, calls=%fused_computation.13 | convolution fusion | flops 6653214720 | bytes 33652736 | tf_op jit(solution)/shard_map/sxkf,xfd->sxkd/dot_general | solution.py:242
  1086.0 17.9 %copy.116 = bf16[8,8,72,2048]{3,2,1,0:T(8,128)(2,1)} copy(bf16[8,8,72,2048]{3,2,0,1:T(8,128)(2,1)} %convert_bitcast_fusion) | data formatting | bytes 37748736 | tf_op jit(solution)/shard_map/convert_element_type | solution.py:244
  1103.9 25.9 %add_convert_fusion.1 = bf16[8,512,2048]{2,1,0:T(8,128)(2,1)} fusion(pred[8,576,512]{2,1,0:T(32,128)(4,1)S(1)} %copy-done.19, bf16[8,576,2048]{2,1,0:T(8,128)(2,1)} %bitcast.210, f32[512,2048]{1,0:T(8,128)S(1)} %copy-done.11, pred[8]{0:T(512)(128)(4,1)S(1)} %copy-done.78), kind=kOutput, calls=%fused_computation.4 | convolution fusion | flops 9688842240 | bytes 42205192 | tf_op jit(solution)/shard_map/gst,gsd->gtd/dot_general | solution.py:281
  1130.9 4.9 convolution_convert_fusion.4
  1135.9 9.1 convolution_convert_fusion.2
  1146.9 5.0 convolution_convert_fusion.6
  1153.7 4.0 convolution_convert_fusion.5
  1159.1 8.7 concatenate.37
  1169.9 75.1 %reduce-scatter.18.cloned.1.call-done = bf16[512,2048]{1,0:T(8,128)(2,1)} async-done(((bf16[4096,2048]{1,0:T(8,128)(2,1)}), bf16[512,2048]{1,0:T(8,128)(2,1)}) %reduce-scatter.18.cloned.1.call-update) | async-done | bytes 2097168 | tf_op jit(solution)/shard_map/reduce_scatter | solution.py:127
  1245.1 3.6 convolution_convert_fusion.3
  1249.0 44.0 %reduce-scatter.38.cloned.1.call-done = bf16[704,256]{1,0:T(8,128)(2,1)} async-done(((bf16[704,2048]{1,0:T(8,128)(2,1)}), bf16[704,256]{1,0:T(8,128)(2,1)}) %reduce-scatter.38.cloned.1.call-update) | async-done | bytes 360464 | tf_op jit(solution)/shard_map/reduce_scatter | solution.py:127
  1294.9 60.4 %reduce-scatter.36.cloned.1.call-done = bf16[256,2,704]{0,2,1:T(8,128)(2,1)} async-done(((bf16[2048,2,704]{0,2,1:T(8,128)(2,1)}), bf16[256,2,704]{0,2,1:T(8,128)(2,1)}) %reduce-scatter.36.cloned.1.call-update) | async-done | bytes 720912 | tf_op jit(solution)/shard_map/reduce_scatter | solution.py:127
  1357.7 18.0 %fusion.24 = f32[8,352,2048]{2,1,0:T(8,128)} fusion(bf16[8,8,72,352]{3,2,0,1:T(8,128)(2,1)} %get-tuple-element.89, bf16[8,8,72,2048]{3,2,1,0:T(8,128)(2,1)} %bitcast.234), kind=kOutput, calls=%fused_computation.29 | convolution fusion | flops 6643777536 | bytes 45187072 | tf_op jit(solution)/shard_map/sxkf,sxkd->xfd/dot_general | solution.py:245
  1375.8 31.8 %fusion.14 = f32[8,2048,2,352]{1,3,2,0:T(8,128)} fusion(bf16[8,8,72,2048,1]{3,2,1,0,4:T(8,128)(2,1)} %bitcast.236, bf16[8,8,72,1,352]{4,2,0,1,3:T(8,128)(2,1)} %copy-done.15, bf16[8,8,72,1,352]{4,2,0,1,3:T(8,128)(2,1)} %copy-done.14), kind=kOutput, calls=%fused_computation.19 | convolution fusion | flops 13290799104 | bytes 71499776 | tf_op jit(solution)/shard_map/sxkd,sxkcf->xdcf/dot_general | solution.py:248
  1409.2 30.1 %reduce-scatter.34.cloned.1.call-done = bf16[512,256]{1,0:T(8,128)(2,1)} async-done(((bf16[512,2048]{1,0:T(8,128)(2,1)}), bf16[512,256]{1,0:T(8,128)(2,1)}) %reduce-scatter.34.cloned.1.call-update) | async-done | bytes 262160 | tf_op jit(solution)/shard_map/reduce_scatter | solution.py:127
  1441.1 47.7 %reduce-scatter.28.cloned.1.call-done = bf16[256,768]{0,1:T(8,128)(2,1)} async-done(((bf16[2048,768]{0,1:T(8,128)(2,1)}), bf16[256,768]{0,1:T(8,128)(2,1)}) %reduce-scatter.28.cloned.1.call-update) | async-done | bytes 393232 | tf_op jit(solution)/shard_map/reduce_scatter | solution.py:127
  1490.8 44.0 %reduce-scatter.20.cloned.1.call-done = bf16[128,2048]{1,0:T(8,128)(2,1)} async-done(((bf16[512,2048]{1,0:T(8,128)(2,1)}), bf16[128,2048]{1,0:T(8,128)(2,1)}) %reduce-scatter.20.cloned.1.call-update) | async-done | bytes 524304 | tf_op jit(solution)/shard_map/reduce_scatter | solution.py:127
  1534.9 3.0 fusion.75
  1537.9 45.5 %reduce-scatter.30.cloned.1.call-done = bf16[256,768]{1,0:T(8,128)(2,1)} async-done(((bf16[2048,768]{1,0:T(8,128)(2,1)}), bf16[256,768]{1,0:T(8,128)(2,1)}) %reduce-scatter.30.cloned.1.call-update) | async-done | bytes 393232 | tf_op jit(solution)/shard_map/reduce_scatter | solution.py:127
  1585.3 21.2 %reduce-scatter.40.cloned.1.call-done = bf16[64,768]{1,0:T(8,128)(2,1)} async-done(((bf16[256,768]{1,0:T(8,128)(2,1)}), bf16[64,768]{1,0:T(8,128)(2,1)}) %reduce-scatter.40.cloned.1.call-update) | async-done | bytes 98320
  (302 shorter events, 73.0 us)
Async XLA Ops:
  7.2 53.6 %all-gather.13.cloned.1.call-start = ((), (), s32[]{:S(2)}) async-start(), calls=%async_computation.13 | async-start | bytes 2621440 | tf_op jit(solution)/shard_map/all_gather | solution.py:123
  7.9 110.6 %all-gather.15.cloned.1.call-start = ((), (), s32[]{:S(2)}) async-start(), calls=%async_computation.14 | async-start | bytes 2703360 | tf_op jit(solution)/shard_map/all_gather | solution.py:123
  8.7 133.9 %all-gather.17.cloned.1.call-start = ((), (), s32[]{:S(2)}) async-start(), calls=%async_computation.15 | async-start | bytes 1179648 | tf_op jit(solution)/shard_map/all_gather | solution.py:123
  9.4 167.1 %all-gather.19.cloned.1.call-start = ((), (), s32[]{:S(2)}) async-start(), calls=%async_computation.16 | async-start | bytes 3538944 | tf_op jit(solution)/shard_map/all_gather | solution.py:123
  10.0 196.4 %all-gather.21.cloned.1.call-start = ((), (), s32[]{:S(2)}) async-start(), calls=%async_computation.17 | async-start | bytes 2359296 | tf_op jit(solution)/shard_map/all_gather | solution.py:123
  10.6 243.9 %reduce-scatter.16.cloned.1.call-start = ((), (), s32[]{:S(2)}) async-start(), calls=%async_computation.18 | async-start | bytes 2621440 | tf_op jit(solution)/shard_map/reduce_scatter | solution.py:127
  11.6 133.7 %copy-start.48 = (f32[512]{0:T(512)}, f32[512]{0:T(512)S(1)}, u32[]{:S(2)}) copy-start(f32[512]{0:T(512)S(1)} %subtract_convert_fusion.3) | copy-start | bytes 6148
  11.6 133.7 %copy-start.57 = (f32[32]{0:T(128)}, f32[32]{0:T(128)S(1)}, u32[]{:S(2)}) copy-start(f32[32]{0:T(128)S(1)} %multiply_power_fusion) | copy-start | bytes 388
  58.8 117.7 %copy-start.46 = (f32[2048]{0:T(1024)}, f32[2048]{0:T(1024)S(1)}, u32[]{:S(2)}) copy-start(f32[2048]{0:T(1024)S(1)} %convert_element_type.183) | copy-start | bytes 24580
  58.8 83.8 %copy-start.52 = (f32[512]{0:T(512)}, f32[512]{0:T(512)S(1)}, u32[]{:S(2)}) copy-start(f32[512]{0:T(512)S(1)} %convert_element_type.185) | copy-start | bytes 6148
  59.1 122.0 %copy-start.34 = (f32[512,32]{0,1:T(8,128)}, f32[512,32]{0,1:T(8,128)S(1)}, u32[]{:S(2)}) copy-start(f32[512,32]{0,1:T(8,128)S(1)} %get-tuple-element.105) | copy-start | bytes 196612
  59.1 122.0 %copy-start.36 = (f32[512,32]{0,1:T(8,128)}, f32[512,32]{0,1:T(8,128)S(1)}, u32[]{:S(2)}) copy-start(f32[512,32]{0,1:T(8,128)S(1)} %get-tuple-element.106) | copy-start | bytes 196612
  62.9 113.6 %copy-start.62 = (f32[512]{0:T(512)}, f32[512]{0:T(512)S(1)}, u32[]{:S(2)}) copy-start(f32[512]{0:T(512)S(1)} %add_rsqrt_fusion.1) | copy-start | bytes 6148
  122.4 58.6 %copy-start.2 = (f32[512,576]{0,1:T(8,128)}, f32[512,576]{0,1:T(8,128)S(1)}, u32[]{:S(2)}) copy-start(f32[512,576]{0,1:T(8,128)S(1)} %fusion.142) | copy-start | bytes 3538948
  123.2 19.4 %copy-start.50 = (f32[512]{0:T(512)}, f32[512]{0:T(512)S(1)}, u32[]{:S(2)}) copy-start(f32[512]{0:T(512)S(1)} %get-tuple-element.108) | copy-start | bytes 6148
  145.2 39.6 %copy-start.9 = (bf16[512,1024]{0,1:T(8,128)(2,1)}, bf16[512,1024]{0,1:T(8,128)(2,1)S(1)}, u32[]{:S(2)}) copy-start(bf16[512,1024]{0,1:T(8,128)(2,1)S(1)} %copy.157) | copy-start | bytes 3145732
  145.3 36.0 %copy-start.23 = (bf16[512,4,128]{0,2,1:T(8,128)(2,1)}, bf16[512,4,128]{0,2,1:T(8,128)(2,1)S(1)}, u32[]{:S(2)}) copy-start(bf16[512,4,128]{0,2,1:T(8,128)(2,1)S(1)} %slice.125) | copy-start | bytes 1572868
  190.8 20.6 %copy-start.76 = (bf16[4,128,512]{2,1,0:T(8,128)(2,1)}, bf16[4,128,512]{2,1,0:T(8,128)(2,1)S(1)}, u32[]{:S(2)}) copy-start(bf16[4,128,512]{2,1,0:T(8,128)(2,1)S(1)} %convolution_convert_fusion.13) | copy-start | bytes 1572868
  206.4 48.1 %copy-start = (bf16[128,2048]{1,0:T(8,128)(2,1)S(1)}, bf16[128,2048]{1,0:T(8,128)(2,1)}, u32[]{:S(2)}) copy-start(bf16[128,2048]{1,0:T(8,128)(2,1)} %param.16) | copy-start | bytes 1572868
  210.7 90.2 %all-gather.31.cloned.1.call-start = ((), (), s32[]{:S(2)}) async-start(), calls=%async_computation.25 | async-start | bytes 2621440 | tf_op jit(solution)/shard_map/all_gather | solution.py:123
  211.4 136.1 %all-gather.23.cloned.1.call-start = ((), (), s32[]{:S(2)}) async-start(), calls=%async_computation.19 | async-start | bytes 2621440 | tf_op jit(solution)/shard_map/all_gather | solution.py:123
  211.5 136.1 %copy-start.43 = (f32[2048]{0:T(1024)}, f32[2048]{0:T(1024)S(1)}, u32[]{:S(2)}) copy-start(f32[2048]{0:T(1024)S(1)} %convert_element_type.196) | copy-start | bytes 24580
  211.5 136.2 %copy-start.54 = (s32[512,6]{0,1:T(8,128)S(1)}, s32[512,6]{0,1:T(8,128)}, u32[]{:S(2)}) copy-start(s32[512,6]{0,1:T(8,128)} %param.18) | copy-start | bytes 36868
  258.8 172.6 %all-gather.27.cloned.1.call-start = ((), (), s32[]{:S(2)}) async-start(), calls=%async_computation.21 | async-start | bytes 6488064 | tf_op jit(solution)/shard_map/all_gather | solution.py:123
  259.6 179.9 %all-gather.29.cloned.1.call-start = ((), (), s32[]{:S(2)}) async-start(), calls=%async_computation.22 | async-start | bytes 3244032 | tf_op jit(solution)/shard_map/all_gather | solution.py:123
  260.2 258.7 %all-gather.33.cloned.1.call-start = ((), (), s32[]{:S(2)}) async-start(), calls=%async_computation.26 | async-start | bytes 18874368 | tf_op jit(solution)/shard_map/all_gather | solution.py:123
  300.9 60.2 %copy-start.55 = (bf16[64,64]{1,0:T(8,128)(2,1)S(1)}, bf16[64,64]{1,0:T(8,128)(2,1)}, u32[]{:S(2)}) copy-start(bf16[64,64]{1,0:T(8,128)(2,1)} %param.27) | copy-start | bytes 24580
  300.9 309.5 %all-gather.25.cloned.1.call-start = ((), (), s32[]{:S(2)}) async-start(), calls=%async_computation.20 | async-start | bytes 18874368 | tf_op jit(solution)/shard_map/all_gather | solution.py:123
  347.6 576.4 %reduce-scatter.22.cloned.1.call-start = ((), (), s32[]{:S(2)}) async-start(), calls=%async_computation.27 | async-start | bytes 20054016 | tf_op jit(solution)/shard_map/reduce_scatter | solution.py:127
  360.5 249.9 %copy-start.18 = (pred[8,576,512]{2,1,0:T(32,128)(4,1)}, pred[8,576,512]{2,1,0:T(32,128)(4,1)S(1)}, u32[]{:S(2)}) copy-start(pred[8,576,512]{2,1,0:T(32,128)(4,1)S(1)} %bitcast_compare_fusion) | copy-start | bytes 7077892
  710.1 28.5 %copy-start.14 = (bf16[8,8,72,1,352]{4,2,0,1,3:T(8,128)(2,1)}, bf16[8,8,72,1,352]{4,2,0,1,3:T(8,128)(2,1)S(1)}, u32[]{:S(2)}) copy-start(bf16[8,8,72,1,352]{4,2,0,1,3:T(8,128)(2,1)S(1)} %get-tuple-element.87) | copy-start | bytes 9732100
  710.1 28.5 %copy-start.15 = (bf16[8,8,72,1,352]{4,2,0,1,3:T(8,128)(2,1)}, bf16[8,8,72,1,352]{4,2,0,1,3:T(8,128)(2,1)S(1)}, u32[]{:S(2)}) copy-start(bf16[8,8,72,1,352]{4,2,0,1,3:T(8,128)(2,1)S(1)} %get-tuple-element.88) | copy-start | bytes 9732100
  799.3 174.8 %copy-start.1 = (bf16[128,2048]{1,0:T(8,128)(2,1)S(1)}, bf16[128,2048]{1,0:T(8,128)(2,1)}, u32[]{:S(2)}) copy-start(bf16[128,2048]{1,0:T(8,128)(2,1)} %param.16) | copy-start | bytes 1572868
  799.3 174.8 %copy-start.4 = (bf16[128,2048]{1,0:T(8,128)(2,1)S(1)}, bf16[128,2048]{1,0:T(8,128)(2,1)}, u32[]{:S(2)}) copy-start(bf16[128,2048]{1,0:T(8,128)(2,1)} %reduce-scatter.16.cloned.1.call-done) | copy-start | bytes 1572868
  799.3 174.8 %copy-start.44 = (f32[2048]{0:T(1024)S(1)}, f32[2048]{0:T(1024)}, u32[]{:S(2)}) copy-start(f32[2048]{0:T(1024)} %copy-done.43) | copy-start | bytes 24580
  799.3 174.8 %copy-start.60 = (f32[128]{0:T(128)S(1)}, f32[128]{0:T(128)}, u32[]{:S(2)}) copy-start(f32[128]{0:T(128)} %copy-done.59) | copy-start | bytes 1540
  799.3 177.7 %copy-start.7 = (bf16[128,2048]{1,0:T(8,128)(2,1)S(1)}, bf16[128,2048]{1,0:T(8,128)(2,1)}, u32[]{:S(2)}) copy-start(bf16[128,2048]{1,0:T(8,128)(2,1)} %param.19) | copy-start | bytes 1572868
  799.3 177.7 %copy-start.68 = (f32[128]{0:T(128)S(1)}, f32[128]{0:T(128)}, u32[]{:S(2)}) copy-start(f32[128]{0:T(128)} %get-tuple-element.109) | copy-start | bytes 1540
  799.3 172.5 %reduce-scatter.24.cloned.1.call-start = ((), (), s32[]{:S(2)}) async-start(), calls=%async_computation.28 | async-start | bytes 2785280 | tf_op jit(solution)/shard_map/reduce_scatter | solution.py:127
  924.0 99.4 %all-gather.35.cloned.1.call-start = ((), (), s32[]{:S(2)}) async-start(), calls=%async_computation.29 | async-start | bytes 2621440 | tf_op jit(solution)/shard_map/all_gather | solution.py:123
  978.3 179.4 %reduce-scatter.26.cloned.1.call-start = ((), (), s32[]{:S(2)}) async-start(), calls=%async_computation.30 | async-start | bytes 2621440 | tf_op jit(solution)/shard_map/reduce_scatter | solution.py:127
  990.1 36.8 %copy-start.10 = (bf16[512,1024]{0,1:T(8,128)(2,1)S(1)}, bf16[512,1024]{0,1:T(8,128)(2,1)}, u32[]{:S(2)}) copy-start(bf16[512,1024]{0,1:T(8,128)(2,1)} %copy-done.9) | copy-start | bytes 3145732
  1068.3 176.7 %reduce-scatter.18.cloned.1.call-start = ((), (), s32[]{:S(2)}) async-start(), calls=%async_computation.23 | async-start | bytes 18874368 | tf_op jit(solution)/shard_map/reduce_scatter | solution.py:127
  1086.0 17.9 %copy-start.11 = (f32[512,2048]{1,0:T(8,128)S(1)}, f32[512,2048]{1,0:T(8,128)}, u32[]{:S(2)}) copy-start(f32[512,2048]{1,0:T(8,128)} %fusion.145) | copy-start | bytes 12582916
  1086.0 17.9 %copy-start.19 = (pred[8,576,512]{2,1,0:T(32,128)(4,1)S(1)}, pred[8,576,512]{2,1,0:T(32,128)(4,1)}, u32[]{:S(2)}) copy-start(pred[8,576,512]{2,1,0:T(32,128)(4,1)} %copy-done.18) | copy-start | bytes 7077892
  1086.0 17.9 %copy-start.78 = (pred[8]{0:T(512)(128)(4,1)S(1)}, pred[8]{0:T(512)(128)(4,1)}, u32[]{:S(2)}) copy-start(pred[8]{0:T(512)(128)(4,1)} %iota_compare_fusion.4) | copy-start | bytes 28
  1129.8 163.2 %reduce-scatter.38.cloned.1.call-start = ((), (), s32[]{:S(2)}) async-start(), calls=%async_computation.36 | async-start | bytes 3244032 | tf_op jit(solution)/shard_map/reduce_scatter | solution.py:127
  1135.8 219.5 %reduce-scatter.36.cloned.1.call-start = ((), (), s32[]{:S(2)}) async-start(), calls=%async_computation.35 | async-start | bytes 6488064 | tf_op jit(solution)/shard_map/reduce_scatter | solution.py:127
  1144.9 262.7 %reduce-scatter.32.cloned.1.call-start = ((), (), s32[]{:S(2)}) async-start(), calls=%async_computation.33 | async-start | bytes 1179648 | tf_op jit(solution)/shard_map/reduce_scatter | solution.py:127
  1146.8 292.5 %reduce-scatter.34.cloned.1.call-start = ((), (), s32[]{:S(2)}) async-start(), calls=%async_computation.34 | async-start | bytes 2359296 | tf_op jit(solution)/shard_map/reduce_scatter | solution.py:127
  1151.9 336.9 %reduce-scatter.28.cloned.1.call-start = ((), (), s32[]{:S(2)}) async-start(), calls=%async_computation.31 | async-start | bytes 3538944 | tf_op jit(solution)/shard_map/reduce_scatter | solution.py:127
  1169.8 75.2 %copy-start.21 = (bf16[512,2048]{1,0:T(8,128)(2,1)S(1)}, bf16[512,2048]{1,0:T(8,128)(2,1)}, u32[]{:S(2)}) copy-start(bf16[512,2048]{1,0:T(8,128)(2,1)} %all-gather.13.cloned.1.call-done) | copy-start | bytes 6291460
  1169.8 75.2 %copy-start.31 = (bf16[512,4,192]{0,2,1:T(8,128)(2,1)S(1)}, bf16[512,4,192]{0,2,1:T(8,128)(2,1)}, u32[]{:S(2)}) copy-start(bf16[512,4,192]{0,2,1:T(8,128)(2,1)} %copy-done.30) | copy-start | bytes 2359300
  1169.9 364.9 %reduce-scatter.20.cloned.1.call-start = ((), (), s32[]{:S(2)}) async-start(), calls=%async_computation.24 | async-start | bytes 2621440 | tf_op jit(solution)/shard_map/reduce_scatter | solution.py:127
  1245.0 338.3 %reduce-scatter.30.cloned.1.call-start = ((), (), s32[]{:S(2)}) async-start(), calls=%async_computation.32 | async-start | bytes 3538944 | tf_op jit(solution)/shard_map/reduce_scatter | solution.py:127
  1248.8 357.7 %reduce-scatter.40.cloned.1.call-start = ((), (), s32[]{:S(2)}) async-start(), calls=%async_computation.37 | async-start | bytes 491520
  1375.7 159.1 %copy-start.5 = (bf16[128,2048]{1,0:T(8,128)(2,1)S(1)}, bf16[128,2048]{1,0:T(8,128)(2,1)}, u32[]{:S(2)}) copy-start(bf16[128,2048]{1,0:T(8,128)(2,1)} %reduce-scatter.16.cloned.1.call-done) | copy-start | bytes 1572868
  1375.7 159.1 %copy-start.8 = (bf16[128,2048]{1,0:T(8,128)(2,1)S(1)}, bf16[128,2048]{1,0:T(8,128)(2,1)}, u32[]{:S(2)}) copy-start(bf16[128,2048]{1,0:T(8,128)(2,1)} %param.19) | copy-start | bytes 1572868
  1375.7 159.1 %copy-start.13 = (f32[128,2048]{1,0:T(8,128)S(1)}, f32[128,2048]{1,0:T(8,128)}, u32[]{:S(2)}) copy-start(f32[128,2048]{1,0:T(8,128)} %copy-done.12) | copy-start | bytes 3145732
  1375.7 159.1 %copy-start.22 = (bf16[128,2048]{1,0:T(8,128)(2,1)S(1)}, bf16[128,2048]{1,0:T(8,128)(2,1)}, u32[]{:S(2)}) copy-start(bf16[128,2048]{1,0:T(8,128)(2,1)} %reduce-scatter.26.cloned.1.call-done) | copy-start | bytes 1572868
  1375.7 159.1 %copy-start.45 = (f32[2048]{0:T(1024)S(1)}, f32[2048]{0:T(1024)}, u32[]{:S(2)}) copy-start(f32[2048]{0:T(1024)} %copy-done.43) | copy-start | bytes 24580
  1375.7 159.1 %copy-start.61 = (f32[128]{0:T(128)S(1)}, f32[128]{0:T(128)}, u32[]{:S(2)}) copy-start(f32[128]{0:T(128)} %copy-done.59) | copy-start | bytes 1540
  1375.7 159.1 %copy-start.69 = (f32[128]{0:T(128)S(1)}, f32[128]{0:T(128)}, u32[]{:S(2)}) copy-start(f32[128]{0:T(128)} %get-tuple-element.109) | copy-start | bytes 1540
  1375.7 159.1 %copy-start.71 = (f32[128]{0:T(128)S(1)}, f32[128]{0:T(128)}, u32[]{:S(2)}) copy-start(f32[128]{0:T(128)} %copy-done.70) | copy-start | bytes 1540
  (42 other events, 235.3 us)
Sparse Core Ops, SparseCore 0:
  9.6 49.4 all-gather.12
  61.9 56.5 all-gather.14
  120.4 22.1 all-gather.16
  144.3 32.1 all-gather.18
  178.3 28.0 all-gather.20
  210.8 43.6 reduce-scatter.15
  256.0 44.8 all-gather.30
  303.1 44.4 all-gather.22
  349.4 43.7 all-gather.26
  395.0 32.2 all-gather.28
  429.2 89.7 all-gather.32
  520.7 89.7 all-gather.24
  799.4 124.4 reduce-scatter.21
  926.1 45.6 reduce-scatter.23
  978.4 44.9 all-gather.34
  1068.4 42.4 reduce-scatter.25
  1130.0 114.9 reduce-scatter.17
  1248.2 44.7 reduce-scatter.37
  1296.4 58.8 reduce-scatter.35
  1358.9 35.9 reduce-scatter.31
  1398.2 41.0 reduce-scatter.33
  1442.7 46.0 reduce-scatter.27
  1491.1 43.6 reduce-scatter.19
  1538.0 45.2 reduce-scatter.29
  1585.6 20.7 reduce-scatter.39

commit v2 on v1

--- a/solution.py
+++ b/solution.py
@@ -1,6 +1,8 @@
 import jax
 import jax.numpy as jnp
 from jax import lax
+from jax.experimental import pallas as pl
+from jax.experimental.pallas import tpu as pltpu
 from jax.sharding import PartitionSpec as P
 
 DN = 128
@@ -129,6 +131,334 @@
 
 def own_slice(array_in, first_row, own_rows):
     return lax.dynamic_slice_in_dim(array_in, first_row, own_rows, 0)
+
+
+class Cube:
+    def __init__(self, axes):
+        self.axes = axes
+        self.sizes = {a: lax.axis_size(a) for a in axes}
+        self.total = 1
+        for a in axes:
+            self.total *= self.sizes[a]
+
+    def flat(self, pos):
+        index = 0
+        for a in self.axes:
+            index = index * self.sizes[a] + pos[a]
+        return index
+
+
+def flipped(pos, name, bit):
+    value = pos[name]
+    has = (value // (1 << bit)) % 2
+    new = dict(pos)
+    new[name] = value + (1 - 2 * has) * (1 << bit)
+    return new
+
+
+def moved(pos, order, pattern):
+    for step, (name, bit) in enumerate(order):
+        if (pattern >> step) & 1:
+            pos = flipped(pos, name, bit)
+    return pos
+
+
+def axis_bits(name):
+    return range(lax.axis_size(name).bit_length() - 1)
+
+
+def gather_orders(axes):
+    far = [("tensor", b) for b in reversed(axis_bits("tensor"))] if "tensor" in axes else []
+    if "dp" not in axes:
+        return [far, far]
+    middle = [("dp", b) for b in list(axis_bits("dp"))[1:]]
+    low = [("dp", 0)]
+    return [far + middle + low, far + middle[::-1] + low]
+
+
+def greet(coords, orders):
+    partners = sorted({bit for order in orders for bit in order})
+    barrier = pltpu.get_barrier_semaphore()
+    for name, bit in partners:
+        pl.semaphore_signal(
+            barrier,
+            inc=1,
+            device_id={name: flipped(coords, name, bit)[name]},
+            device_id_type=pl.DeviceIdType.MESH,
+        )
+    pl.semaphore_wait(barrier, len(partners))
+
+
+def part_of(ref, item, part, index):
+    rows, cols = item["rows"] // item["parts"], item["cols"]
+    if index is None:
+        return ref.at[pl.ds(part * rows, rows), :]
+    if item["lanes"]:
+        return ref.at[pl.ds(part * rows, rows), pl.ds(pl.multiple_of(index * cols, 128), cols)]
+    start = index * item["rows"] + part * rows
+    return ref.at[pl.ds(pl.multiple_of(start, 8), rows), :]
+
+
+def side_by_side(stacked, n):
+    rows = stacked.shape[0] // n
+    return jnp.swapaxes(stacked.reshape(n, rows, -1), 0, 1).reshape(rows, -1)
+
+
+def stacked_blocks(wide_array, n):
+    rows = wide_array.shape[0]
+    return jnp.swapaxes(wide_array.reshape(rows, n, -1), 0, 1).reshape(n * rows, -1)
+
+
+def size_of(axes):
+    return Cube(axes).total
+
+
+def gather_blocks(blocks, collective_id):
+    narrow = [lanes and array.shape[1] % 128 != 0 for array, _, lanes, _ in blocks]
+    done = cube_gather(
+        [(a, axes, lanes and not thin, parts) for (a, axes, lanes, parts), thin in zip(blocks, narrow)],
+        collective_id,
+    )
+    return [
+        side_by_side(out, size_of(block[1])) if thin else out
+        for out, block, thin in zip(done, blocks, narrow)
+    ]
+
+
+def reduce_blocks(blocks, collective_id):
+    ready = []
+    for array, axes, lanes, parts in blocks:
+        if lanes and (array.shape[1] // size_of(axes)) % 128 != 0:
+            array, lanes = stacked_blocks(array, size_of(axes)), False
+        ready.append((array, axes, lanes, parts))
+    return cube_reduce(ready, collective_id)
+
+
+def cube_gather(blocks, collective_id):
+    items = []
+    for array, axes, lanes, parts in blocks:
+        cube = Cube(axes)
+        items.append(
+            dict(
+                rows=array.shape[0], cols=array.shape[1], lanes=lanes, parts=parts,
+                cube=cube, orders=gather_orders(axes), dtype=array.dtype,
+            )
+        )
+    count = len(items)
+    names = [a for a in BOTH if any(a in item["cube"].axes for item in items)]
+
+    def kernel(*refs):
+        ins, outs = refs[:count], refs[count : 2 * count]
+        sems = refs[2 * count :]
+        coords = {a: lax.axis_index(a) for a in names}
+        greet(coords, [order for item in items for order in item["orders"]])
+        pending = []
+
+        def copy(i, part, step, slot, src, dst):
+            name, bit = items[i]["orders"][part][step]
+            return pltpu.make_async_remote_copy(
+                src_ref=src,
+                dst_ref=dst,
+                send_sem=sems[3 * i].at[part, slot],
+                recv_sem=sems[3 * i + 1].at[part, slot],
+                device_id={name: flipped(coords, name, bit)[name]},
+                device_id_type=pl.DeviceIdType.MESH,
+            )
+
+        def send(i, part, step, pattern, src, pos):
+            dst = part_of(outs[i], items[i], part, items[i]["cube"].flat(pos))
+            one = copy(i, part, step, (1 << step) - 1 + pattern, src, dst)
+            one.start()
+            pending.append(one.wait_send)
+
+        depth = [len(item["orders"][0]) for item in items]
+        for step in range(max(depth)):
+            for i, item in enumerate(items):
+                for part in range(item["parts"]):
+                    if step < depth[i]:
+                        send(i, part, step, 0, part_of(ins[i], item, part, None), coords)
+        for i, item in enumerate(items):
+            for part in range(item["parts"]):
+                own = part_of(outs[i], item, part, item["cube"].flat(coords))
+                one = pltpu.make_async_copy(
+                    part_of(ins[i], item, part, None), own, sems[3 * i + 2].at[part]
+                )
+                one.start()
+                pending.append(one.wait)
+        for step in range(max(depth)):
+            for k in range(1 << step):
+                for i, item in enumerate(items):
+                    if step >= depth[i]:
+                        continue
+                    for part in range(item["parts"]):
+                        pattern = k + (1 << step)
+                        pos = moved(coords, item["orders"][part], pattern)
+                        here = part_of(outs[i], item, part, item["cube"].flat(pos))
+                        copy(i, part, step, pattern - 1, here, here).wait_recv()
+                        for later in range(step + 1, depth[i]):
+                            send(i, part, later, pattern, here, pos)
+        for wait in pending:
+            wait()
+
+    shapes, scratch = [], []
+    for item in items:
+        n = item["cube"].total
+        whole = (item["rows"], item["cols"] * n) if item["lanes"] else (item["rows"] * n, item["cols"])
+        shapes.append(jax.ShapeDtypeStruct(whole, item["dtype"]))
+        scratch += [pltpu.SemaphoreType.DMA((item["parts"], n - 1))] * 2
+        scratch.append(pltpu.SemaphoreType.DMA((item["parts"],)))
+    moved_bytes = sum(s.size * s.dtype.itemsize for s in shapes)
+    return pl.pallas_call(
+        kernel,
+        out_shape=shapes,
+        in_specs=[pl.BlockSpec(memory_space=pltpu.VMEM)] * count,
+        out_specs=[pl.BlockSpec(memory_space=pl.ANY)] * count,
+        scratch_shapes=scratch,
+        compiler_params=pltpu.CompilerParams(collective_id=collective_id, has_side_effects=True),
+        cost_estimate=pl.CostEstimate(flops=0, bytes_accessed=8 * moved_bytes, transcendentals=0),
+        name="cube_gather",
+    )(*[block[0] for block in blocks])
+
+
+def cube_reduce(blocks, collective_id):
+    items = []
+    for array, axes, lanes, parts in blocks:
+        cube = Cube(axes)
+        rows, cols = array.shape
+        rows, cols = (rows, cols // cube.total) if lanes else (rows // cube.total, cols)
+        orders = [order[::-1] for order in gather_orders(axes)]
+        items.append(
+            dict(rows=rows, cols=cols, lanes=lanes, parts=parts, cube=cube, orders=orders, dtype=array.dtype)
+        )
+    count = len(items)
+    names = [a for a in BOTH if any(a in item["cube"].axes for item in items)]
+
+    def kernel(*refs):
+        ins, outs = refs[:count], refs[count : 2 * count]
+        scratch = refs[2 * count :]
+        coords = {a: lax.axis_index(a) for a in names}
+        held = [scratch[5 * i] for i in range(count)]
+        came = [scratch[5 * i + 1] for i in range(count)]
+        send_sem = [scratch[5 * i + 2] for i in range(count)]
+        recv_sem = [scratch[5 * i + 3] for i in range(count)]
+        load_sem = [scratch[5 * i + 4] for i in range(count)]
+        depth = [len(item["orders"][0]) for item in items]
+        pending = []
+
+        def load(i, part, k):
+            item = items[i]
+            pos = moved(coords, item["orders"][part], k << 1)
+            return pltpu.make_async_copy(
+                part_of(ins[i], item, part, item["cube"].flat(pos)),
+                held[i].at[part, k],
+                load_sem[i].at[part, k],
+            )
+
+        for i, item in enumerate(items):
+            for part in range(item["parts"]):
+                for k in range(1 << (depth[i] - 1)):
+                    load(i, part, k).start()
+        greet(coords, [order for item in items for order in item["orders"]])
+
+        def base(i, step):
+            return (1 << depth[i]) - (1 << (depth[i] - step))
+
+        def copy(i, part, step, k, src):
+            name, bit = items[i]["orders"][part][step]
+            slot = base(i, step) + k
+            return pltpu.make_async_remote_copy(
+                src_ref=src,
+                dst_ref=came[i].at[part, slot],
+                send_sem=send_sem[i].at[part, slot],
+                recv_sem=recv_sem[i].at[part, slot],
+                device_id={name: flipped(coords, name, bit)[name]},
+                device_id_type=pl.DeviceIdType.MESH,
+            )
+
+        def first(count_bits):
+            return sorted(range(1 << count_bits), key=lambda k: -(k & 1))
+
+        for i, item in enumerate(items):
+            for k in first(depth[i] - 1):
+                for part in range(item["parts"]):
+                    pos = moved(coords, item["orders"][part], (k << 1) | 1)
+                    one = copy(i, part, 0, k, part_of(ins[i], item, part, item["cube"].flat(pos)))
+                    one.start()
+                    pending.append(one.wait_send)
+
+        def add_up(i, part, pattern, steps, store):
+            item = items[i]
+            rows = item["rows"] // item["parts"]
+            load(i, part, pattern >> 1).wait()
+            for step in range(steps):
+                k = pattern >> (step + 1)
+                copy(i, part, step, k, came[i].at[part, base(i, step) + k]).wait_recv()
+            chunk = 16 if rows % 16 == 0 else 8
+
+            def one_chunk(c, carry):
+                where = pl.ds(pl.multiple_of(c * chunk, chunk), chunk)
+                total = held[i][part, pattern >> 1, where, :].astype(jnp.float32)
+                for step in range(steps):
+                    slot = base(i, step) + (pattern >> (step + 1))
+                    total = total + came[i][part, slot, where, :].astype(jnp.float32)
+                store(where, total)
+                return carry
+
+            lax.fori_loop(0, rows // chunk, one_chunk, 0)
+
+        for step in range(1, max(depth)):
+            for i, item in enumerate(items):
+                if step >= depth[i]:
+                    continue
+                for k in first(depth[i] - step - 1):
+                    for part in range(item["parts"]):
+                        pattern = ((k << 1) | 1) << step
+
+                        def keep(where, total, i=i, part=part, pattern=pattern):
+                            held[i][part, pattern >> 1, where, :] = total.astype(held[i].dtype)
+
+                        add_up(i, part, pattern, step, keep)
+                        one = copy(i, part, step, k, held[i].at[part, pattern >> 1])
+                        one.start()
+                        pending.append(one.wait_send)
+        for i, item in enumerate(items):
+            rows = item["rows"] // item["parts"]
+            for part in range(item["parts"]):
+
+                def put(where, total, i=i, part=part, rows=rows):
+                    whole = pl.ds(pl.multiple_of(part * rows + where.start, 8), where.size)
+                    outs[i][whole, :] = total
+
+                add_up(i, part, 0, depth[i], put)
+        for wait in pending:
+            wait()
+
+    shapes, scratch = [], []
+    for item in items:
+        n = item["cube"].total
+        block = (item["rows"] // item["parts"], item["cols"])
+        shapes.append(jax.ShapeDtypeStruct((item["rows"], item["cols"]), jnp.float32))
+        scratch.append(pltpu.VMEM((item["parts"], n // 2) + block, item["dtype"]))
+        scratch.append(pltpu.VMEM((item["parts"], n - 1) + block, item["dtype"]))
+        scratch += [pltpu.SemaphoreType.DMA((item["parts"], n - 1))] * 2
+        scratch.append(pltpu.SemaphoreType.DMA((item["parts"], n // 2)))
+    moved_bytes = sum(block[0].size * block[0].dtype.itemsize for block in blocks)
+    return pl.pallas_call(
+        kernel,
+        out_shape=shapes,
+        in_specs=[pl.BlockSpec(memory_space=pl.ANY)] * count,
+        out_specs=[pl.BlockSpec(memory_space=pltpu.VMEM)] * count,
+        scratch_shapes=scratch,
+        compiler_params=pltpu.CompilerParams(
+            collective_id=collective_id, has_side_effects=True, vmem_limit_bytes=60 << 20
+        ),
+        cost_estimate=pl.CostEstimate(flops=0, bytes_accessed=8 * moved_bytes, transcendentals=0),
+        name="cube_reduce",
+    )(*[block[0] for block in blocks])
+
+
+def halves(rows):
+    return 2 if rows % 32 == 0 else 1
 
 
 def body(
@@ -155,23 +485,42 @@
     first_row = lax.axis_index("tensor") * own_rows
     local_experts = expert_in.shape[0]
     segment_row = segments[0]
-    group_rows = gather(tokens, "tensor")
+    gain_rows, lat_rows = attention_gain.shape[0], latent_gain.shape[0]
+    columns = jnp.stack(
+        [attention_gain, feedforward_gain, jnp.pad(latent_gain, (0, gain_rows - lat_rows))], axis=1
+    )
+    router_block = jnp.concatenate([router_weight, columns], axis=1)
+    router_block = jnp.pad(router_block, ((0, 0), (0, -router_block.shape[1] % 128)))
+    routes_block = jnp.pad(routes.T, ((0, -routes.shape[1] % 8), (0, 0)), constant_values=-1)
+    (
+        group_rows,
+        cot_group,
+        latent_full,
+        query_full,
+        expand_full,
+        router_block_full,
+        routes_full,
+        output_full,
+    ) = gather_blocks(
+        [
+            (tokens, ("tensor",), False, halves(own_rows)),
+            (cotangent, ("tensor",), False, halves(own_rows)),
+            (latent_weight, BOTH, False, halves(latent_weight.shape[0])),
+            (query_weight, ("dp",), False, halves(query_weight.shape[0])),
+            (expand_weight, ("dp",), False, halves(expand_weight.shape[0])),
+            (router_block, BOTH, False, halves(router_block.shape[0])),
+            (routes_block, ("dp",), True, 1),
+            (output_weight, ("dp",), True, halves(output_weight.shape[0])),
+        ],
+        0,
+    )
     row_count = group_rows.shape[0]
-    gain_one_low, gain_lat_low, gain_two_low = (
-        gather(attention_gain, BOTH),
-        gather(latent_gain, BOTH),
-        gather(feedforward_gain, BOTH),
-    )
-    latent_full = gather(latent_weight, BOTH)
-    expand_full = gather(expand_weight, "dp")
-    query_full = gather(query_weight, "dp")
-    output_full = gather(output_weight, "dp", 1)
-    router_full = gather(router_weight, BOTH)
-    routes_all = gather(routes, "dp")
-    shared_in_full = gather(shared_in, "dp")
-    shared_out_full = gather(shared_out, "dp", 1)
-    gain_one = gain_one_low.astype(jnp.float32)
-    gain_two = gain_two_low.astype(jnp.float32)
+    router_full = router_block_full[:, :EXPERTS]
+    gain_one = router_block_full[:, EXPERTS].astype(jnp.float32)
+    gain_two = router_block_full[:, EXPERTS + 1].astype(jnp.float32)
+    gain_lat_low = router_block_full[:, EXPERTS + 2].reshape(-1, gain_rows)[:, :lat_rows].reshape(-1)
+    routes_all = routes_full[: routes.shape[1]]
+    cot_all = gather(cot_group, "dp").reshape(groups, row_count, width)
 
     wide = group_rows.astype(jnp.float32)
     scale_one = rms_scale(wide)
@@ -182,27 +531,28 @@
     )
     mixed, logsum = attend(query, key_rows, value_rows, segment_row)
     mixed_flat = mixed.reshape(row_count, -1)
-    attention_own = scatter_sum(
-        jnp.dot(mixed_flat, output_full, preferred_element_type=jnp.float32).astype(jnp.bfloat16),
-        "tensor",
+    attention_part = jnp.dot(mixed_flat, output_full, preferred_element_type=jnp.float32)
+    (attention_own,) = reduce_blocks(
+        [(attention_part.astype(jnp.bfloat16), ("tensor",), False, halves(own_rows))], 1
     )
     wide_own = tokens.astype(jnp.float32)
-    hidden = wide_own + attention_own.astype(jnp.float32)
+    hidden = wide_own + attention_own
     scale_two = rms_scale(hidden)
     normed_two_own = (hidden * scale_two * gain_two).astype(jnp.bfloat16)
 
-    cot_group = gather(cotangent, "tensor")
-    cot_all = gather(cot_group, "dp").reshape(groups, row_count, width)
-    normed_two = gather(normed_two_own, "tensor")
-    normed_all = gather(normed_two, "dp").reshape(groups, row_count, width)
+    normed_two_own, cot_all = lax.optimization_barrier((normed_two_own, cot_all))
+    (normed_flat,) = gather_blocks([(normed_two_own, BOTH, False, halves(own_rows))], 2)
+    normed_flat, shared_in, shared_out = lax.optimization_barrier(
+        (normed_flat, shared_in, shared_out)
+    )
+    shared_in_full = gather(shared_in, "dp")
+    shared_out_full = gather(shared_out, "dp", 1)
+    normed_all = normed_flat.reshape(groups, row_count, width)
+    normed_two = lax.dynamic_index_in_dim(normed_all, place_dp, 0, keepdims=False)
 
     expert_ids = jnp.arange(EXPERTS, dtype=jnp.int32)
-    chosen = jnp.any(routes_all[:, :, None] == expert_ids[None, None, :], axis=1)
-    logits = jnp.dot(
-        normed_all.reshape(groups * row_count, width),
-        router_full,
-        preferred_element_type=jnp.float32,
-    )
+    chosen = jnp.any(routes_all[:, :, None] == expert_ids[None, None, :], axis=0)
+    logits = jnp.dot(normed_flat, router_full, preferred_element_type=jnp.float32)
     sigm = jnp.where(chosen, jax.nn.sigmoid(logits), 0.0)
     picked_total = jnp.sum(sigm, axis=1, keepdims=True)
     gate_dense = route_scale * sigm / picked_total
@@ -268,10 +618,12 @@
         shared_hidden_grad, shared_pre[:, 0], shared_pre[:, 1]
     )
     shared_pre_grad = jnp.stack([shared_gate_part, shared_up_part], axis=1).astype(jnp.bfloat16)
-    shared_out_grad = jnp.dot(shared_act.T, cot_group, preferred_element_type=jnp.float32)
+    shared_out_grad = jnp.dot(
+        shared_act.T, cot_group, preferred_element_type=jnp.float32
+    ).astype(jnp.bfloat16)
     shared_in_grad = jnp.einsum(
-        "gd,gcf->dcf", normed_two, shared_pre_grad, preferred_element_type=jnp.float32
-    )
+        "gcf,gd->cfd", shared_pre_grad, normed_two, preferred_element_type=jnp.float32
+    ).astype(jnp.bfloat16)
     shared_back = jnp.einsum(
         "gcf,dcf->gd", shared_pre_grad, shared_in_full, preferred_element_type=jnp.float32
     )
@@ -283,16 +635,40 @@
         return total.astype(jnp.bfloat16).reshape(groups * row_count, width)
 
     back_sum = combine(back_slots, shared_back)
-    back_sum = jnp.concatenate([back_sum, gate_grad_all], axis=1)
-    back_own = scatter_sum(scatter_sum(back_sum, "dp"), "tensor").astype(jnp.float32)
+    back_group = scatter_sum(back_sum, "dp")
     out_sum = combine(out_slots, shared_part)
-    out_own = scatter_sum(scatter_sum(out_sum, "dp"), "tensor").astype(jnp.float32)
-    out_tokens = (hidden + out_own).astype(jnp.bfloat16)
+    (
+        back_group,
+        out_sum,
+        expert_out_grad,
+        expert_in_grad,
+        shared_out_grad,
+        shared_in_grad,
+        gate_grad_all,
+    ) = lax.optimization_barrier(
+        (
+            back_group,
+            out_sum,
+            expert_out_grad,
+            expert_in_grad,
+            shared_out_grad,
+            shared_in_grad,
+            gate_grad_all,
+        )
+    )
+    back_own, gate_grad_own = reduce_blocks(
+        [
+            (back_group, ("tensor",), False, halves(own_rows)),
+            (gate_grad_all, BOTH, False, 1),
+        ],
+        3,
+    )
+    out_group = scatter_sum(out_sum, "dp")
 
     first_token = place_dp * row_count + first_row
     sigm_own = own_slice(sigm, first_token, own_rows)
     total_own = own_slice(picked_total, first_token, own_rows)
-    gate_grad = back_own[:, width : width + EXPERTS]
+    gate_grad = gate_grad_own[:, :EXPERTS]
     picked_grad = route_scale * (
         gate_grad / total_own
         - jnp.sum(gate_grad * sigm_own, axis=1, keepdims=True) / (total_own * total_own)
@@ -304,7 +680,7 @@
     router_back = jnp.dot(
         logit_grad, router_full.astype(jnp.float32).T, precision=lax.Precision.HIGHEST
     )
-    normed_two_grad = back_own[:, :width] + router_back
+    normed_two_grad = back_own + router_back
     weighted_two = normed_two_grad * gain_two
     hidden_grad = (
         cotangent.astype(jnp.float32)
@@ -312,7 +688,9 @@
         - hidden * scale_two**3 * jnp.mean(hidden * weighted_two, axis=-1, keepdims=True)
     )
     gain_two_grad = jnp.sum(normed_two_grad * hidden * scale_two, axis=0)
-    hidden_low = gather(hidden_grad.astype(jnp.bfloat16), "tensor")
+    (hidden_low,) = gather_blocks(
+        [(hidden_grad.astype(jnp.bfloat16), ("tensor",), False, halves(own_rows))], 4
+    )
 
     output_grad = jnp.dot(mixed_flat.T, hidden_low, preferred_element_type=jnp.float32)
     mixed_grad = (
@@ -334,6 +712,8 @@
         .astype(jnp.bfloat16)
         .reshape(row_count, -1)
     )
+    query_pre, out_group = lax.optimization_barrier((query_pre, out_group))
+    out_own = scatter_sum(out_group, "tensor").astype(jnp.float32)
     query_grad_weight = jnp.dot(normed.T, query_pre, preferred_element_type=jnp.float32)
     normed_grad = jnp.dot(query_pre, query_full.T, preferred_element_type=jnp.float32)
     keyvalue_grad = (
@@ -354,37 +734,57 @@
     normed_grad = normed_grad + jnp.dot(
         latent_grad, latent_full.T, preferred_element_type=jnp.float32
     )
-    normed_own = scatter_sum(normed_grad.astype(jnp.bfloat16), "tensor").astype(jnp.float32)
-    scale_own = own_slice(scale_one, first_row, own_rows)
-    weighted_one = normed_own * gain_one
-    gain_one_grad = jnp.sum(normed_own * wide_own * scale_own, axis=0)
-    tokens_grad = (
-        hidden_grad
-        + scale_own * weighted_one
-        - wide_own * scale_own**3 * jnp.mean(wide_own * weighted_one, axis=-1, keepdims=True)
-    )
-
-    shared_out_out = scatter_sum(shared_out_grad.astype(jnp.bfloat16), "dp", 1).astype(jnp.float32)
-    shared_in_out = scatter_sum(shared_in_grad.astype(jnp.bfloat16), "dp").astype(jnp.float32)
-    output_out = scatter_sum(output_grad.astype(jnp.bfloat16), "dp", 1).astype(jnp.float32)
-    expand_out = scatter_sum(expand_grad.astype(jnp.bfloat16), "dp").astype(jnp.float32)
-    query_out = scatter_sum(query_grad_weight.astype(jnp.bfloat16), "dp").astype(jnp.float32)
-    lat_rows = latent_gain.shape[0]
-    gain_rows = attention_gain.shape[0]
+    gain_one_grad = jnp.sum(normed_grad * wide * scale_one, axis=0)
+
     lat_column = jnp.pad(
         gain_lat_grad.reshape(-1, lat_rows), ((0, 0), (0, gain_rows - lat_rows))
     ).reshape(-1)
-    columns = jnp.stack([gain_one_grad, gain_two_grad, lat_column], axis=1)
+    columns = jnp.stack([gain_one_grad, gain_two_grad, lat_column], axis=1).astype(jnp.bfloat16)
     latent_columns = latent_grad_weight.shape[1]
-    small = jnp.concatenate([latent_grad_weight, router_grad, columns], axis=1)
-    small = jnp.pad(small, ((0, 0), (0, -small.shape[1] % 128))).astype(jnp.bfloat16)
-    small = scatter_sum(scatter_sum(small, "dp"), "tensor").astype(jnp.float32)
+    small = jnp.concatenate(
+        [latent_grad_weight.astype(jnp.bfloat16), router_grad.astype(jnp.bfloat16), columns], axis=1
+    )
+    small = jnp.pad(small, ((0, 0), (0, -small.shape[1] % 128)))
+    hidden_units = shared_in.shape[2]
+    normed_own, query_out, expand_out, output_out, shared_in_out, shared_out_out, small = (
+        reduce_blocks(
+            [
+                (normed_grad.astype(jnp.bfloat16), ("tensor",), False, halves(own_rows)),
+                (
+                    query_grad_weight.astype(jnp.bfloat16),
+                    ("dp",),
+                    False,
+                    halves(query_weight.shape[0]),
+                ),
+                (expand_grad.astype(jnp.bfloat16), ("dp",), False, halves(expand_weight.shape[0])),
+                (output_grad.astype(jnp.bfloat16), ("dp",), True, halves(output_weight.shape[0])),
+                (
+                    shared_in_grad.reshape(2 * hidden_units, width),
+                    ("dp",),
+                    True,
+                    halves(2 * hidden_units),
+                ),
+                (shared_out_grad, ("dp",), True, halves(hidden_units)),
+                (small, BOTH, False, 1),
+            ],
+            5,
+        )
+    )
+    shared_in_out = jnp.moveaxis(shared_in_out.reshape(2, hidden_units, -1), 2, 0)
     latent_out = small[:, :latent_columns]
     router_out = small[:, latent_columns : latent_columns + EXPERTS]
     last = latent_columns + EXPERTS
     gain_one_out = small[:, last]
     gain_two_out = small[:, last + 1]
     gain_lat_out = small[:lat_rows, last + 2]
+    scale_own = own_slice(scale_one, first_row, own_rows)
+    weighted_one = normed_own * gain_one
+    tokens_grad = (
+        hidden_grad
+        + scale_own * weighted_one
+        - wide_own * scale_own**3 * jnp.mean(wide_own * weighted_one, axis=-1, keepdims=True)
+    )
+    out_tokens = (hidden + out_own).astype(jnp.bfloat16)
     return (
         out_tokens,
         tokens_grad,

time: 1630 us -> 950 us (0.58)
  waiting for transfers between devices: 969 us -> 4.53 us
  Pallas kernels: 0 us -> 406 us
  blocking collectives: 125 us -> 0 us
  local copies, waits for them, and re-layouts: 67.6 us -> 94.8 us
    reduce_scatter x12 -> x3, waiting for transfers between devices: 562 us -> 0.02 us  [scatter_sum(): lax.psum_scatter(array_in, axis_name, scatter_dimension=axis, tiled=True)]
    pallas_call x0 -> x6, Pallas kernels: none -> 406 us  [the longest x3 212 us: cube_gather(): pl.pallas_call(kernel, out_shape=shapes, in_specs=[pl.BlockSpec(memory_sp...]
    all_gather x12 -> x3, waiting for transfers between devices: 381 us -> 4.4 us  [gather(): return lax.all_gather(array_in, axis_name, axis=axis, tiled=True)]
    all_gather x2 -> x0, blocking collectives: 79.9 us -> none  [gather(): return lax.all_gather(array_in, axis_name, axis=axis, tiled=True)]
    unnamed x1 -> x0, blocking collectives: 44.6 us -> none
    unnamed x26 -> x6, waiting for transfers between devices: 26.5 us -> 0.1 us
  transfers between devices with their start and end apart: 25 -> 6, of which waited for: 20 -> 1; matrix products, arithmetic and copies ran while one was open for 16% -> 49% of each run, Pallas kernels for 0% -> 24%
where the time goes in v2:
time: 950 us; the launch traced here: 940 us
  Pallas kernels  406 us (43%)
  matrix products  360 us (38%)
  local copies, waits for them, and re-layouts  94.8 us (10%)
  other arithmetic  58.8 us (6%)
  between operations  15.2 us (2%)
    pallas_call x3, Pallas kernels, cube_gather(): pl.pallas_call(kernel, out_shape=shapes, in_specs=[pl.BlockSpec(memory_sp...  212 us
    pallas_call x3, Pallas kernels, cube_reduce(): pl.pallas_call(kernel, out_shape=shapes, in_specs=[pl.BlockSpec(memory_sp...  194 us
    dot_general x2, matrix products, combine(): jnp.einsum('gst,gsd->gtd', pick, slots, preferred_element_type=jnp.float32)  52.2 us
    dot_general x1, matrix products, body(): jnp.einsum('sxkd,sxkcf->xdcf', rows, expert_pre_grad, preferred_element_t...  32.4 us
    dot_general x1, matrix products, body(): jnp.einsum('sxkd,xdcf->sxkcf', rows, expert_in, preferred_element_type=jn...  30.3 us
    dot_general x1, matrix products, body(): jnp.einsum('sxkcf,xdcf->sxkd', expert_pre_grad, expert_in, preferred_elem...  24.4 us
    dot_general x1, matrix products, body(): jnp.einsum('sxkd,xfd->sxkf', cots, expert_out, preferred_element_type=jnp...  23.5 us
    dot_general x1, matrix products, body(): jnp.einsum('gst,gtd->gsd', pick, cot_all, preferred_element_type=jnp.floa...  19.2 us
  transfers between devices with their start and end apart: 6, of which 1 were waited for; matrix products, arithmetic and copies ran while one was open for 49% of the time, Pallas kernels for 24%

profile of v2, /device:TPU:0, one launch (start us, length us, event | category | flops | bytes accessed | tf_op | source)
XLA Modules:
  0.0 939.7 jit_solution(16436518513294988034)
XLA Ops:
  12.3 94.4 %cube_gather.3 = (bf16[512,2048]{1,0:T(8,128)(2,1)}, bf16[512,2048]{1,0:T(8,128)(2,1)}, bf16[2048,576]{1,0:T(8,128)(2,1)}, bf16[2048,768]{1,0:T(8,128)(2,1)}, bf...) custom-call(bf16[128,2048]{1,0:T(8,128)(2,1)} %refs_0_.1, ...), custom_call_target="tpu_custom_call" | custom-call | bytes 108003328 | tf_op jit(solution)/shard_map/cube_gather/pallas_call | solution.py:311
  109.1 1.9 fusion.26
  112.3 2.5 fusion.36
  115.4 3.8 fusion.151
  120.6 1.8 convolution_convert_fusion.10
  122.5 1.7 copy.203
  124.2 5.0 fusion.149
  131.0 2.9 fusion.86
  134.2 5.9 convolution_convert_fusion.13
  140.9 4.2 convolution_convert_fusion.7.refs_0_
  145.1 38.3 %cube_reduce.3 = f32[128,2048]{1,0:T(8,128)} custom-call(bf16[512,2048]{1,0:T(8,128)(2,1)} %convolution_convert_fusion.7.refs_0_), custom_call_target="tpu_custom_call" | custom-call | bytes 16777216 | tf_op jit(solution)/shard_map/cube_reduce/pallas_call | solution.py:446
  183.7 2.7 bitcast_compare_fusion
  190.3 4.4 all-gather.4.cloned.1.call-done
  194.7 84.3 %cube_gather.4 = bf16[4096,2048]{1,0:T(8,128)(2,1)} custom-call(bf16[128,2048]{1,0:T(8,128)(2,1)} %multiply_convert_fusion.7.refs_0_), custom_call_target="tpu_custom_call" | custom-call | bytes 134217728 | tf_op jit(solution)/shard_map/cube_gather/pallas_call | solution.py:311
  279.1 8.8 fusion.154
  291.1 19.2 %convolution_convert_fusion.1 = bf16[8,576,2048]{2,1,0:T(8,128)(2,1)} fusion(pred[8,576,512]{2,1,0:T(32,128)(4,1)} %bitcast_compare_fusion, bf16[8,512,2048]{2,1,0:T(8,128)(2,1)} %bitcast.237), kind=kOutput, calls=%fused_computation.20 | convolution fusion | flops 9673113600 | bytes 38010880 | tf_op jit(solution)/shard_map/gst,gtd->gsd/dot_general | solution.py:576
  310.3 19.0 %convolution_convert_fusion = bf16[8,576,2048]{2,1,0:T(8,128)(2,1)} fusion(pred[8,576,512]{2,1,0:T(32,128)(4,1)S(1)} %copy-done.16, bf16[8,512,2048]{2,1,0:T(8,128)(2,1)} %bitcast.209), kind=kOutput, calls=%fused_computation.19 | convolution fusion | flops 9673113600 | bytes 38010880 | tf_op jit(solution)/shard_map/gst,gtd->gsd/dot_general | solution.py:573
  329.2 30.3 %fusion.27 = f32[8,8,72,2,352]{4,2,0,1,3:T(8,128)} fusion(bf16[8,8,72,2048]{3,2,1,0:T(8,128)(2,1)} %bitcast.238, bf16[8,2048,2,352]{1,3,2,0:T(8,128)(2,1)} %param.30), kind=kOutput, calls=%fused_computation.46 | convolution fusion | flops 13287555072 | bytes 54919168 | tf_op jit(solution)/shard_map/sxkd,xdcf->sxkcf/dot_general | solution.py:579
  359.5 23.5 %fusion.22 = (f32[8,8,72]{2,0,1:T(8,128)S(1)}, f32[8,8,72,352]{3,2,1,0:T(8,128)}) fusion(f32[8,8,72,2,352]{4,2,0,1,3:T(8,128)} %fusion.27, bf16[8,352,2048]{2,1,0:T(8,128)(2,1)} %param.31, bf16[8,8,72,2048]{3,2,1,0:T(8,128)(2,1)} %bitcast.240), kind=kOutput, calls=%fused_computation.33 | convolution fusion | flops 6655127040 | bytes 49891328 | tf_op jit(solution)/shard_map/sxkd,xfd->sxkf/dot_general | solution.py:584
  383.1 4.7 select_reduce_fusion
  388.4 12.9 %fusion.45 = (bf16[8,8,72,1,352]{4,2,0,1,3:T(8,128)(2,1)S(1)}, bf16[8,8,72,1,352]{4,2,0,1,3:T(8,128)(2,1)}, bf16[8,8,72,352]{3,2,0,1:T(8,128)(2,1)}) fusion(f32[8,8,72,2,352]{4,2,0,1,3:T(8,128)} %fusion.27, f32[8,8,72]{2,0,1:T(8,128)} %copy.161, f32[8,8,72,352]{3,2,1,0:T(8,128)} %get-tuple-element.119), kind=kLoop, calls=%fused_computation.67 | loop fusion | flops 27574272 | bytes 29214720 | tf_op jit(solution)/shard_map/stack | solution.py:588
  401.3 24.4 %fusion.2 = bf16[8,8,72,2048,1]{3,2,1,0,4:T(8,128)(2,1)} fusion(bf16[8,8,72,1,352]{4,2,0,1,3:T(8,128)(2,1)} %get-tuple-element.97, bf16[8,8,72,1,352]{4,2,0,1,3:T(8,128)(2,1)S(1)} %get-tuple-element.96, bf16[8,2048,2,352]{1,3,2,0:T(8,128)(2,1)} %param.30), kind=kOutput, calls=%fused_computation.5 | convolution fusion | flops 13290799104 | bytes 48431104 | tf_op jit(solution)/shard_map/sxkcf,xdcf->sxkd/dot_general | solution.py:589
  425.7 17.0 %copy.231 = bf16[8,8,72,2048,1]{3,2,0,1,4:T(8,128)(2,1)} copy(bf16[8,8,72,2048,1]{3,2,1,0,4:T(8,128)(2,1)} %fusion.2) | data formatting | bytes 37748736 | tf_op jit(solution)/shard_map/sxkcf,xdcf->sxkd/dot_general | solution.py:589
  442.7 8.2 fusion.58
  450.9 5.0 fusion.85
  456.0 3.6 convolution_bitcast_fusion
  459.7 25.9 %add_convert_fusion.1 = bf16[8,512,2048]{2,1,0:T(8,128)(2,1)} fusion(pred[8,576,512]{2,1,0:T(32,128)(4,1)S(1)} %copy-done.17, bf16[8,576,2048]{2,1,0:T(8,128)(2,1)} %bitcast.207, f32[512,2048]{1,0:T(8,128)S(1)} %convolution_bitcast_fusion, pred[8]{0:T(512)(128)(4,1)S(1)} %copy-done.79), kind=kOutput, calls=%fused_computation.4 | convolution fusion | flops 9688842240 | bytes 42205192 | tf_op jit(solution)/shard_map/gst,gsd->gtd/dot_general | solution.py:633
  486.9 19.0 %convert_bitcast_fusion = bf16[8,8,72,2048]{3,2,0,1:T(8,128)(2,1)} fusion(bf16[8,8,72,352]{3,2,0,1:T(8,128)(2,1)} %get-tuple-element.98, bf16[8,352,2048]{2,1,0:T(8,128)(2,1)} %param.31), kind=kOutput, calls=%fused_computation.13 | convolution fusion | flops 6653214720 | bytes 33652736 | tf_op jit(solution)/shard_map/sxkf,xfd->sxkd/dot_general | solution.py:592
  505.8 17.9 %copy.166 = bf16[8,8,72,2048]{3,2,1,0:T(8,128)(2,1)} copy(bf16[8,8,72,2048]{3,2,0,1:T(8,128)(2,1)} %convert_bitcast_fusion) | data formatting | bytes 37748736 | tf_op jit(solution)/shard_map/convert_element_type | solution.py:594
  523.9 3.9 dynamic_update_slice.3.refs_1_
  527.8 18.7 %fusion.19 = f32[8,352,2048]{2,1,0:T(8,128)} fusion(bf16[8,8,72,352]{3,2,0,1:T(8,128)(2,1)} %get-tuple-element.98, bf16[8,8,72,2048]{3,2,1,0:T(8,128)(2,1)} %bitcast.241), kind=kOutput, calls=%fused_computation.27 | convolution fusion | flops 6643777536 | bytes 45187072 | tf_op jit(solution)/shard_map/sxkf,sxkd->xfd/dot_general | solution.py:595
  546.5 32.4 %fusion.14 = f32[8,2048,2,352]{1,3,2,0:T(8,128)} fusion(bf16[8,8,72,2048,1]{3,2,1,0,4:T(8,128)(2,1)} %bitcast.239, bf16[8,8,72,1,352]{4,2,0,1,3:T(8,128)(2,1)} %get-tuple-element.97, bf16[8,8,72,1,352]{4,2,0,1,3:T(8,128)(2,1)} %copy-done.13), kind=kOutput, calls=%fused_computation.18 | convolution fusion | flops 13290799104 | bytes 71499776 | tf_op jit(solution)/shard_map/sxkd,sxkcf->xdcf/dot_general | solution.py:598
  579.0 3.2 convolution_convert_fusion.4.refs_5_
  582.2 6.7 convolution_convert_fusion.2
  588.8 1.9 fusion.155
  590.7 26.4 %add_convert_fusion = bf16[8,512,2048]{2,1,0:T(8,128)(2,1)} fusion(pred[8,576,512]{2,1,0:T(32,128)(4,1)S(1)} %copy-done.18, bf16[8,576,2048]{2,1,0:T(8,128)(2,1)} %bitcast.206, f32[512,2048]{1,0:T(8,128)S(1)} %fusion.155, pred[8]{0:T(512)(128)(4,1)S(1)} %copy-done.79), kind=kOutput, calls=%fused_computation.3 | convolution fusion | flops 9688842240 | bytes 42205192 | tf_op jit(solution)/shard_map/gst,gsd->gtd/dot_general | solution.py:633
  618.4 7.8 fusion.41
  626.2 50.4 %cube_reduce.4 = (f32[128,2048]{1,0:T(8,128)}, f32[128,128]{1,0:T(8,128)}) custom-call(bf16[512,2048]{1,0:T(8,128)(2,1)} %reduce-scatter.4.cloned.1.call-done.refs_0_, bf16[4096,128]{1,0:T(8,128)(2,1)} %copy-done.9), custom_call_target="tpu_custom_call" | custom-call | bytes 25165824 | tf_op jit(solution)/shard_map/cube_reduce/pallas_call | solution.py:446
  680.8 2.4 multiply_reduce_fusion.2
  685.5 33.3 %cube_gather.5 = bf16[512,2048]{1,0:T(8,128)(2,1)} custom-call(bf16[128,2048]{1,0:T(8,128)(2,1)} %get-tuple-element.88.refs_0_), custom_call_target="tpu_custom_call" | custom-call | bytes 16777216 | tf_op jit(solution)/shard_map/cube_gather/pallas_call | solution.py:311
  718.8 3.7 convolution_convert_fusion.11
  723.4 2.8 fusion.87
  726.1 8.9 fusion.70
  735.1 2.1 slice.248
  737.2 7.0 fusion.74
  746.6 3.5 multiply_reduce_fusion.1
  750.8 8.6 fusion.67
  759.4 2.1 slice.249
  761.5 2.6 stack_reshape.5
  766.3 2.0 pad_maximum_fusion.7
  771.0 4.8 convolution_convert_fusion.5
  775.8 4.4 copy.177
  780.2 3.0 convolution_convert_fusion.9.refs_2_
  783.2 4.5 convolution_convert_fusion.6.refs_3_
  787.7 1.8 fusion.156
  790.2 3.7 fusion.40
  795.0 6.7 concatenate.37
  801.7 4.0 pad.25.refs_6_
  805.7 3.7 convolution_convert_fusion.3.refs_1_
  809.4 105.5 %cube_reduce.5 = (f32[128,2048]{1,0:T(8,128)}, f32[256,768]{1,0:T(8,128)}, f32[64,1024]{1,0:T(8,128)}, f32[512,256]{1,0:T(8,128)}, f32[1408,256]{1,0:T(8,128)}, /*index=5*/f32[704,256]{1,0:T(8,128)}, f32[64,768]{1,0:T(8,128)}) custom-call(bf16[512,2048]{1,0:T(8,128)(2,1)} %get-tuple-element.102.refs_0_, bf16[2048,768]{1,0:T(8,128)(2,1)} %convolution_convert_fusion.3.refs_1_, ...), custom_call_target="tpu_custom_call" | custom-call | bytes 161480704 | tf_op jit(solution)/shard_map/cube_reduce/pallas_call | solution.py:446
  916.4 1.6 slice.138
  922.4 2.5 fusion.77
  925.0 2.1 add_convert_fusion.2
  927.1 2.1 copy.244
  (251 shorter events, 50.7 us)
Async XLA Ops:
  7.2 187.5 %all-gather.4.cloned.1.call-start = ((), (), s32[]{:S(2)}) async-start(), calls=%async_computation.3 | async-start | bytes 18874368 | tf_op jit(solution)/shard_map/all_gather | solution.py:125
  106.7 4.9 copy-start.4
  106.7 336.0 %all-gather.8.cloned.1.call-start = ((), (), s32[]{:S(2)}) async-start(), calls=%async_computation.5 | async-start | bytes 6488064 | tf_op jit(solution)/shard_map/all_gather | solution.py:125
  109.1 11.0 %copy-start.56 = (f32[512]{0:T(512)}, f32[512]{0:T(512)S(1)}, u32[]{:S(2)}) copy-start(f32[512]{0:T(512)S(1)} %reshape.321) | copy-start | bytes 6148
  109.1 6.3 copy-start.19
  112.2 12.0 %copy-start.51 = (f32[2048]{0:T(1024)}, f32[2048]{0:T(1024)S(1)}, u32[]{:S(2)}) copy-start(f32[2048]{0:T(1024)S(1)} %get-tuple-element.81) | copy-start | bytes 24580
  112.3 76.7 %copy-start.49 = (f32[2048]{0:T(1024)}, f32[2048]{0:T(1024)S(1)}, u32[]{:S(2)}) copy-start(f32[2048]{0:T(1024)S(1)} %get-tuple-element.80) | copy-start | bytes 24580
  115.4 5.3 copy-start.77
  119.2 10.3 %copy-start.2 = (f32[512,576]{0,1:T(8,128)}, f32[512,576]{0,1:T(8,128)S(1)}, u32[]{:S(2)}) copy-start(f32[512,576]{0,1:T(8,128)S(1)} %fusion.151) | copy-start | bytes 3538948
  124.1 10.0 %copy-start.10 = (bf16[512,1024]{0,1:T(8,128)(2,1)}, bf16[512,1024]{0,1:T(8,128)(2,1)S(1)}, u32[]{:S(2)}) copy-start(bf16[512,1024]{0,1:T(8,128)(2,1)S(1)} %copy.203) | copy-start | bytes 3145732
  124.2 6.8 copy-start.25
  124.2 5.1 copy-start.55
  129.3 4.6 copy-start.26
  134.2 5.9 copy-start.45
  140.9 42.8 %copy-start.62 = (s32[576]{0:T(1024)S(1)}, s32[576]{0:T(1024)}, u32[]{:S(2)}) copy-start(s32[576]{0:T(1024)} %eq.80) | copy-start | bytes 6916
  145.1 41.9 %copy-start.6 = (bf16[128,2048]{1,0:T(8,128)(2,1)S(1)}, bf16[128,2048]{1,0:T(8,128)(2,1)}, u32[]{:S(2)}) copy-start(bf16[128,2048]{1,0:T(8,128)(2,1)} %refs_0_.1) | copy-start | bytes 1572868
  189.0 90.1 %copy-start.66 = (f32[128]{0:T(128)}, f32[128]{0:T(128)S(1)}, u32[]{:S(2)}) copy-start(f32[128]{0:T(128)S(1)} %get-tuple-element.117) | copy-start | bytes 1540
  279.1 171.8 %all-gather.6.cloned.1.call-start = ((), (), s32[]{:S(2)}) async-start(), calls=%async_computation.4 | async-start | bytes 3244032 | tf_op jit(solution)/shard_map/all_gather | solution.py:125
  291.1 19.2 %copy-start.16 = (pred[8,576,512]{2,1,0:T(32,128)(4,1)S(1)}, pred[8,576,512]{2,1,0:T(32,128)(4,1)}, u32[]{:S(2)}) copy-start(pred[8,576,512]{2,1,0:T(32,128)(4,1)} %bitcast_compare_fusion) | copy-start | bytes 7077892
  388.4 228.7 %reduce-scatter.4.cloned.1.call-start = ((), (), s32[]{:S(2)}) async-start(), calls=%async_computation.6 | async-start | bytes 18874368 | tf_op jit(solution)/shard_map/reduce_scatter | solution.py:129
  401.3 24.4 %copy-start.13 = (bf16[8,8,72,1,352]{4,2,0,1,3:T(8,128)(2,1)}, bf16[8,8,72,1,352]{4,2,0,1,3:T(8,128)(2,1)S(1)}, u32[]{:S(2)}) copy-start(bf16[8,8,72,1,352]{4,2,0,1,3:T(8,128)(2,1)S(1)} %get-tuple-element.96) | copy-start | bytes 9732100
  442.7 8.2 copy-start.22
  450.9 5.1 copy-start.74
  456.0 3.7 copy-start.80
  456.0 3.7 copy-start.82
  456.0 3.7 copy-start.17
  456.0 3.7 copy-start.79
  485.6 283.1 %reduce-scatter.6.cloned.1.call-start = ((), (), s32[]{:S(2)}) async-start(), calls=%async_computation.7 | async-start | bytes 18874368 | tf_op jit(solution)/shard_map/reduce_scatter | solution.py:129
  527.8 18.7 %copy-start.9 = (bf16[4096,128]{1,0:T(8,128)(2,1)}, bf16[4096,128]{1,0:T(8,128)(2,1)S(1)}, u32[]{:S(2)}) copy-start(bf16[4096,128]{1,0:T(8,128)(2,1)S(1)} %dynamic_update_slice.3.refs_1_) | copy-start | bytes 3145732
  546.5 32.4 %copy-start.23 = (bf16[512,2048]{1,0:T(8,128)(2,1)S(1)}, bf16[512,2048]{1,0:T(8,128)(2,1)}, u32[]{:S(2)}) copy-start(bf16[512,2048]{1,0:T(8,128)(2,1)} %get-tuple-element.52) | copy-start | bytes 6291460
  582.2 6.7 copy-start.14
  617.1 307.8 %reduce-scatter.8.cloned.1.call-start = ((), (), s32[]{:S(2)}) async-start(), calls=%async_computation.8 | async-start | bytes 2621440 | tf_op jit(solution)/shard_map/reduce_scatter | solution.py:129
  618.4 60.0 %copy-start.8 = (bf16[128,2048]{1,0:T(8,128)(2,1)S(1)}, bf16[128,2048]{1,0:T(8,128)(2,1)}, u32[]{:S(2)}) copy-start(bf16[128,2048]{1,0:T(8,128)(2,1)} %multiply_convert_fusion.7.refs_0_) | copy-start | bytes 1572868
  626.2 54.6 %copy-start.1 = (f32[128,2048]{1,0:T(8,128)S(1)}, f32[128,2048]{1,0:T(8,128)}, u32[]{:S(2)}) copy-start(f32[128,2048]{1,0:T(8,128)} %copy-done) | copy-start | bytes 3145732
  626.2 54.6 %copy-start.5 = (bf16[2048,128]{1,0:T(8,128)(2,1)S(1)}, bf16[2048,128]{1,0:T(8,128)(2,1)}, u32[]{:S(2)}) copy-start(bf16[2048,128]{1,0:T(8,128)(2,1)} %get-tuple-element.46) | copy-start | bytes 1572868
  626.2 54.6 %copy-start.50 = (f32[2048]{0:T(1024)S(1)}, f32[2048]{0:T(1024)}, u32[]{:S(2)}) copy-start(f32[2048]{0:T(1024)} %copy-done.49) | copy-start | bytes 24580
  626.2 54.6 %copy-start.67 = (f32[128]{0:T(128)S(1)}, f32[128]{0:T(128)}, u32[]{:S(2)}) copy-start(f32[128]{0:T(128)} %copy-done.66) | copy-start | bytes 1540
  626.2 58.1 %copy-start.24 = (bf16[128,2048]{1,0:T(8,128)(2,1)S(1)}, bf16[128,2048]{1,0:T(8,128)(2,1)}, u32[]{:S(2)}) copy-start(bf16[128,2048]{1,0:T(8,128)(2,1)} %refs_1_.1) | copy-start | bytes 1572868
  626.2 58.1 %copy-start.73 = (f32[128]{0:T(128)S(1)}, f32[128]{0:T(128)}, u32[]{:S(2)}) copy-start(f32[128]{0:T(128)} %get-tuple-element.116) | copy-start | bytes 1540
  718.8 4.6 copy-start.11
  737.2 9.4 copy-start.3
  737.2 9.4 copy-start.57
  737.2 9.4 copy-start.59
  744.2 6.6 copy-start.31
  750.8 17.5 %copy-start.54 = (f32[512]{0:T(512)S(1)}, f32[512]{0:T(512)}, u32[]{:S(2)}) copy-start(f32[512]{0:T(512)} %copy-done.53) | copy-start | bytes 6148
  759.4 8.9 copy-start.65
  759.4 9.3 copy-start.72
  759.4 9.3 copy-start.60
  759.4 9.3 copy-start.63
  761.5 9.5 %copy-start.52 = (f32[2048]{0:T(1024)S(1)}, f32[2048]{0:T(1024)}, u32[]{:S(2)}) copy-start(f32[2048]{0:T(1024)} %copy-done.51) | copy-start | bytes 24580
  761.5 9.5 %copy-start.69 = (f32[512]{0:T(512)S(1)}, f32[512]{0:T(512)}, u32[]{:S(2)}) copy-start(f32[512]{0:T(512)} %copy-done.68) | copy-start | bytes 6148
  783.2 4.5 copy-start.32
  783.2 4.5 copy-start.75
  790.2 4.8 copy-start.27
  790.2 4.8 copy-start.28
  801.7 4.0 copy-start.21
  801.7 4.0 copy-start.33
  809.4 111.5 %copy-start.7 = (bf16[128,2048]{1,0:T(8,128)(2,1)S(1)}, bf16[128,2048]{1,0:T(8,128)(2,1)}, u32[]{:S(2)}) copy-start(bf16[128,2048]{1,0:T(8,128)(2,1)} %refs_0_.1) | copy-start | bytes 1572868
  809.4 113.0 %copy-start.70 = (f32[128]{0:T(128)S(1)}, f32[128]{0:T(128)}, u32[]{:S(2)}) copy-start(f32[128]{0:T(128)} %get-tuple-element.86) | copy-start | bytes 1540
  809.4 113.0 %copy-start.71 = (f32[128]{0:T(128)S(1)}, f32[128]{0:T(128)}, u32[]{:S(2)}) copy-start(f32[128]{0:T(128)} %get-tuple-element.87) | copy-start | bytes 1540
  920.9 8.2 copy-start.47
  924.9 5.7 copy-start.29
  924.9 6.8 copy-start.34
  925.0 4.9 copy-start.44
  (26 other events, 44.0 us)
Sparse Core Ops, SparseCore 0:
  106.8 87.8 all-gather.3
  279.2 43.7 all-gather.7
  388.5 31.0 all-gather.5
  485.7 115.7 reduce-scatter.3
  617.2 122.8 reduce-scatter.5
  768.8 43.6 reduce-scatter.7

commit v3 on v2

--- a/solution.py
+++ b/solution.py
@@ -457,6 +457,147 @@
     )(*[block[0] for block in blocks])
 
 
+def rows_dot(left, right):
+    return lax.dot_general(left, right, (((1,), (1,)), ((), ())), preferred_element_type=jnp.float32)
+
+
+def columns_dot(left, right):
+    return lax.dot_general(left, right, (((0,), (0,)), ((), ())), preferred_element_type=jnp.float32)
+
+
+def tile_groups(groups, slots):
+    tile = groups
+    while tile % 2 == 0 and tile * slots > 1024:
+        tile //= 2
+    return tile
+
+
+def expert_calls(rows):
+    groups, experts, slots, width = rows.shape
+    tile = tile_groups(groups, slots)
+    height = tile * slots
+    grid = (experts, groups // tile)
+    token_spec = pl.BlockSpec((tile, None, slots, width), lambda e, m: (m, e, 0, 0))
+    params = pltpu.CompilerParams(
+        dimension_semantics=("arbitrary", "arbitrary"), vmem_limit_bytes=60 << 20
+    )
+    return groups, experts, slots, width, height, grid, token_spec, params
+
+
+def expert_first(rows, cots, gate, weight_in, weight_out):
+    groups, experts, slots, width, height, grid, token_spec, params = expert_calls(rows)
+    units = weight_out.shape[1]
+
+    def kernel(rows_ref, cots_ref, gate_ref, in_ref, out_ref, back_ref, act_ref, pre_ref, grad_ref):
+        picked = rows_ref[...].reshape(height, width)
+        gate_pre = rows_dot(picked, in_ref[0])
+        up_pre = rows_dot(picked, in_ref[1])
+        raw = rows_dot(cots_ref[...].reshape(height, width), out_ref[...])
+        weight = gate_ref[...]
+        sigm = jax.nn.sigmoid(gate_pre)
+        silu = gate_pre * sigm
+        act = silu * up_pre
+        grad_ref[...] = jnp.sum(act * raw, axis=1, keepdims=True)
+        act_ref[...] = (act * weight).astype(jnp.bfloat16)
+        hidden_grad = raw * weight
+        gate_part = (hidden_grad * up_pre * sigm * (1.0 + gate_pre * (1.0 - sigm))).astype(
+            jnp.bfloat16
+        )
+        up_part = (hidden_grad * silu).astype(jnp.bfloat16)
+        pre_ref[0] = gate_part
+        pre_ref[1] = up_part
+        back = jnp.dot(gate_part, in_ref[0], preferred_element_type=jnp.float32)
+        back = back + jnp.dot(up_part, in_ref[1], preferred_element_type=jnp.float32)
+        back_ref[...] = back.astype(jnp.bfloat16).reshape(back_ref.shape)
+
+    count = groups * slots
+    column = pl.BlockSpec((None, height, 1), lambda e, m: (e, m, 0))
+    work = experts * count * width * units
+    return pl.pallas_call(
+        kernel,
+        grid=grid,
+        out_shape=[
+            jax.ShapeDtypeStruct(rows.shape, jnp.bfloat16),
+            jax.ShapeDtypeStruct((experts, count, units), jnp.bfloat16),
+            jax.ShapeDtypeStruct((experts, 2, count, units), jnp.bfloat16),
+            jax.ShapeDtypeStruct((experts, count, 1), jnp.float32),
+        ],
+        in_specs=[
+            token_spec,
+            token_spec,
+            column,
+            pl.BlockSpec((None, 2, units, width), lambda e, m: (e, 0, 0, 0)),
+            pl.BlockSpec((None, units, width), lambda e, m: (e, 0, 0)),
+        ],
+        out_specs=[
+            token_spec,
+            pl.BlockSpec((None, height, units), lambda e, m: (e, m, 0)),
+            pl.BlockSpec((None, 2, height, units), lambda e, m: (e, 0, m, 0)),
+            column,
+        ],
+        compiler_params=params,
+        cost_estimate=pl.CostEstimate(
+            flops=10 * work, bytes_accessed=6 * rows.size + 6 * experts * units * width, transcendentals=0
+        ),
+        name="expert_first",
+    )(rows, cots, gate, weight_in, weight_out)
+
+
+def expert_second(rows, cots, act, pre_grad, weight_out):
+    groups, experts, slots, width, height, grid, token_spec, params = expert_calls(rows)
+    units = weight_out.shape[1]
+
+    def kernel(rows_ref, cots_ref, act_ref, pre_ref, out_ref, rows_out_ref, in_grad_ref, out_grad_ref):
+        act_low = act_ref[...]
+        result = jnp.dot(act_low, out_ref[...], preferred_element_type=jnp.float32)
+        rows_out_ref[...] = result.astype(jnp.bfloat16).reshape(rows_out_ref.shape)
+        picked = rows_ref[...].reshape(height, width)
+        out_part = columns_dot(act_low, cots_ref[...].reshape(height, width))
+        gate_part = columns_dot(pre_ref[0], picked)
+        up_part = columns_dot(pre_ref[1], picked)
+
+        @pl.when(pl.program_id(1) == 0)
+        def _():
+            out_grad_ref[...] = out_part
+            in_grad_ref[0] = gate_part
+            in_grad_ref[1] = up_part
+
+        @pl.when(pl.program_id(1) != 0)
+        def _():
+            out_grad_ref[...] += out_part
+            in_grad_ref[0] += gate_part
+            in_grad_ref[1] += up_part
+
+    count = groups * slots
+    work = experts * count * width * units
+    return pl.pallas_call(
+        kernel,
+        grid=grid,
+        out_shape=[
+            jax.ShapeDtypeStruct(rows.shape, jnp.bfloat16),
+            jax.ShapeDtypeStruct((experts, 2, units, width), jnp.float32),
+            jax.ShapeDtypeStruct((experts, units, width), jnp.float32),
+        ],
+        in_specs=[
+            token_spec,
+            token_spec,
+            pl.BlockSpec((None, height, units), lambda e, m: (e, m, 0)),
+            pl.BlockSpec((None, 2, height, units), lambda e, m: (e, 0, m, 0)),
+            pl.BlockSpec((None, units, width), lambda e, m: (e, 0, 0)),
+        ],
+        out_specs=[
+            token_spec,
+            pl.BlockSpec((None, 2, units, width), lambda e, m: (e, 0, 0, 0)),
+            pl.BlockSpec((None, units, width), lambda e, m: (e, 0, 0)),
+        ],
+        compiler_params=params,
+        cost_estimate=pl.CostEstimate(
+            flops=8 * work, bytes_accessed=6 * rows.size + 14 * experts * units * width, transcendentals=0
+        ),
+        name="expert_second",
+    )(rows, cots, act, pre_grad, weight_out)
+
+
 def halves(rows):
     return 2 if rows % 32 == 0 else 1
 
@@ -540,10 +681,9 @@
     scale_two = rms_scale(hidden)
     normed_two_own = (hidden * scale_two * gain_two).astype(jnp.bfloat16)
 
-    normed_two_own, cot_all = lax.optimization_barrier((normed_two_own, cot_all))
     (normed_flat,) = gather_blocks([(normed_two_own, BOTH, False, halves(own_rows))], 2)
-    normed_flat, shared_in, shared_out = lax.optimization_barrier(
-        (normed_flat, shared_in, shared_out)
+    normed_flat, shared_in, shared_out, cot_all = lax.optimization_barrier(
+        (normed_flat, shared_in, shared_out, cot_all)
     )
     shared_in_full = gather(shared_in, "dp")
     shared_out_full = gather(shared_out, "dp", 1)
@@ -566,38 +706,28 @@
     below = (places[None, :] < places[:, None]).astype(jnp.bfloat16)
     rank = jnp.einsum("ts,gse->get", below, chosen_local, preferred_element_type=jnp.float32)
     slot = jnp.where(jnp.swapaxes(chosen_local, 1, 2) > 0, rank, -1.0).astype(jnp.int32)
-    is_slot = slot[:, :, None, :] == jnp.arange(CAP, dtype=jnp.int32)[None, None, :, None]
-    pick = is_slot.astype(jnp.bfloat16).reshape(groups, local_experts * CAP, row_count)
+    slots = CAP + -CAP % 16
+    is_slot = slot[:, :, None, :] == jnp.arange(slots, dtype=jnp.int32)[None, None, :, None]
+    pick = is_slot.astype(jnp.bfloat16).reshape(groups, local_experts * slots, row_count)
     gate_slot = jnp.sum(jnp.where(is_slot, gate_local[:, :, None, :], 0.0), axis=-1)
 
     rows = jnp.einsum(
         "gst,gtd->gsd", pick, normed_all, preferred_element_type=jnp.float32
-    ).astype(jnp.bfloat16).reshape(groups, local_experts, CAP, width)
+    ).astype(jnp.bfloat16).reshape(groups, local_experts, slots, width)
     cots = jnp.einsum(
         "gst,gtd->gsd", pick, cot_all, preferred_element_type=jnp.float32
-    ).astype(jnp.bfloat16).reshape(groups, local_experts, CAP, width)
-    expert_pre = jnp.einsum(
-        "sxkd,xdcf->sxkcf", rows, expert_in, preferred_element_type=jnp.float32
-    )
-    gate_pre, up_pre = (expert_pre[..., 0, :], expert_pre[..., 1, :])
-    act = jax.nn.silu(gate_pre) * up_pre
-    hid_raw = jnp.einsum("sxkd,xfd->sxkf", cots, expert_out, preferred_element_type=jnp.float32)
-    gate_grad_slot = jnp.sum(act * hid_raw, axis=-1)
-    act_gated = (act * gate_slot[..., None]).astype(jnp.bfloat16)
-    gate_part, up_part = swiglu_grad(hid_raw * gate_slot[..., None], gate_pre, up_pre)
-    expert_pre_grad = jnp.stack([gate_part, up_part], axis=-2).astype(jnp.bfloat16)
-    back_slots = jnp.einsum(
-        "sxkcf,xdcf->sxkd", expert_pre_grad, expert_in, preferred_element_type=jnp.float32
-    ).astype(jnp.bfloat16).reshape(groups, local_experts * CAP, width)
-    out_slots = jnp.einsum(
-        "sxkf,xfd->sxkd", act_gated, expert_out, preferred_element_type=jnp.float32
-    ).astype(jnp.bfloat16).reshape(groups, local_experts * CAP, width)
-    expert_out_grad = jnp.einsum(
-        "sxkf,sxkd->xfd", act_gated, cots, preferred_element_type=jnp.float32
-    )
-    expert_in_grad = jnp.einsum(
-        "sxkd,sxkcf->xdcf", rows, expert_pre_grad, preferred_element_type=jnp.float32
-    )
+    ).astype(jnp.bfloat16).reshape(groups, local_experts, slots, width)
+    gate_column = jnp.swapaxes(gate_slot, 0, 1).reshape(local_experts, groups * slots, 1)
+    back_slots, act_gated, expert_pre_grad, gate_grad_column = expert_first(
+        rows, cots, gate_column, jnp.transpose(expert_in, (0, 2, 3, 1)), expert_out
+    )
+    out_slots, expert_in_grad, expert_out_grad = expert_second(
+        rows, cots, act_gated, expert_pre_grad, expert_out
+    )
+    back_slots = back_slots.reshape(groups, local_experts * slots, width)
+    out_slots = out_slots.reshape(groups, local_experts * slots, width)
+    expert_in_grad = jnp.transpose(expert_in_grad, (0, 3, 1, 2))
+    gate_grad_slot = jnp.swapaxes(gate_grad_column.reshape(local_experts, groups, slots), 0, 1)
     gate_grad_local = jnp.sum(jnp.where(is_slot, gate_grad_slot[..., None], 0.0), axis=2)
     gate_grad_all = lax.dynamic_update_slice_in_dim(
         jnp.zeros((groups * row_count, 2 * EXPERTS), jnp.bfloat16),
@@ -627,16 +757,13 @@
     shared_back = jnp.einsum(
         "gcf,dcf->gd", shared_pre_grad, shared_in_full, preferred_element_type=jnp.float32
     )
-    mine = (jnp.arange(groups, dtype=jnp.int32) == place_dp)[:, None, None]
-
-    def combine(slots, shared):
-        total = jnp.einsum("gst,gsd->gtd", pick, slots, preferred_element_type=jnp.float32)
-        total = total + jnp.where(mine, shared[None], 0.0)
+
+    def combine(slot_rows):
+        total = jnp.einsum("gst,gsd->gtd", pick, slot_rows, preferred_element_type=jnp.float32)
         return total.astype(jnp.bfloat16).reshape(groups * row_count, width)
 
-    back_sum = combine(back_slots, shared_back)
-    back_group = scatter_sum(back_sum, "dp")
-    out_sum = combine(out_slots, shared_part)
+    back_group = scatter_sum(combine(back_slots), "dp")
+    out_sum = combine(out_slots)
     (
         back_group,
         out_sum,
@@ -644,6 +771,8 @@
         expert_in_grad,
         shared_out_grad,
         shared_in_grad,
+        shared_back,
+        shared_part,
         gate_grad_all,
     ) = lax.optimization_barrier(
         (
@@ -653,13 +782,20 @@
             expert_in_grad,
             shared_out_grad,
             shared_in_grad,
+            shared_back,
+            shared_part,
             gate_grad_all,
         )
     )
-    back_own, gate_grad_own = reduce_blocks(
+    gate_grad_own, back_own = reduce_blocks(
         [
-            (back_group, ("tensor",), False, halves(own_rows)),
             (gate_grad_all, BOTH, False, 1),
+            (
+                (back_group.astype(jnp.float32) + shared_back).astype(jnp.bfloat16),
+                ("tensor",),
+                False,
+                halves(own_rows),
+            ),
         ],
         3,
     )
@@ -692,6 +828,7 @@
         [(hidden_grad.astype(jnp.bfloat16), ("tensor",), False, halves(own_rows))], 4
     )
 
+    hidden_units = shared_in.shape[2]
     output_grad = jnp.dot(mixed_flat.T, hidden_low, preferred_element_type=jnp.float32)
     mixed_grad = (
         jnp.dot(hidden_low, output_full.T, preferred_element_type=jnp.float32)
@@ -713,6 +850,7 @@
         .reshape(row_count, -1)
     )
     query_pre, out_group = lax.optimization_barrier((query_pre, out_group))
+    out_group = (out_group.astype(jnp.float32) + shared_part).astype(jnp.bfloat16)
     out_own = scatter_sum(out_group, "tensor").astype(jnp.float32)
     query_grad_weight = jnp.dot(normed.T, query_pre, preferred_element_type=jnp.float32)
     normed_grad = jnp.dot(query_pre, query_full.T, preferred_element_type=jnp.float32)
@@ -736,47 +874,48 @@
     )
     gain_one_grad = jnp.sum(normed_grad * wide * scale_one, axis=0)
 
-    lat_column = jnp.pad(
-        gain_lat_grad.reshape(-1, lat_rows), ((0, 0), (0, gain_rows - lat_rows))
-    ).reshape(-1)
-    columns = jnp.stack([gain_one_grad, gain_two_grad, lat_column], axis=1).astype(jnp.bfloat16)
-    latent_columns = latent_grad_weight.shape[1]
-    small = jnp.concatenate(
-        [latent_grad_weight.astype(jnp.bfloat16), router_grad.astype(jnp.bfloat16), columns], axis=1
-    )
-    small = jnp.pad(small, ((0, 0), (0, -small.shape[1] % 128)))
+    total = groups * lax.axis_size("tensor")
+    gains = jnp.stack(
+        [
+            jnp.pad(g.reshape(total, -1), ((0, 0), (0, -(g.shape[0] // total) % 128))).reshape(-1)
+            for g in (gain_one_grad, gain_two_grad, gain_lat_grad)
+        ]
+    )
+    gains = jnp.pad(gains, ((0, -gains.shape[0] % 8), (0, 0)))
     hidden_units = shared_in.shape[2]
-    normed_own, query_out, expand_out, output_out, shared_in_out, shared_out_out, small = (
-        reduce_blocks(
-            [
-                (normed_grad.astype(jnp.bfloat16), ("tensor",), False, halves(own_rows)),
-                (
-                    query_grad_weight.astype(jnp.bfloat16),
-                    ("dp",),
-                    False,
-                    halves(query_weight.shape[0]),
-                ),
-                (expand_grad.astype(jnp.bfloat16), ("dp",), False, halves(expand_weight.shape[0])),
-                (output_grad.astype(jnp.bfloat16), ("dp",), True, halves(output_weight.shape[0])),
-                (
-                    shared_in_grad.reshape(2 * hidden_units, width),
-                    ("dp",),
-                    True,
-                    halves(2 * hidden_units),
-                ),
-                (shared_out_grad, ("dp",), True, halves(hidden_units)),
-                (small, BOTH, False, 1),
-            ],
-            5,
-        )
+    (
+        latent_out,
+        router_out,
+        gains_out,
+        query_out,
+        output_out,
+        expand_out,
+        shared_in_out,
+        shared_out_out,
+        normed_own,
+    ) = reduce_blocks(
+        [
+            (latent_grad_weight.astype(jnp.bfloat16), BOTH, False, 1),
+            (router_grad.astype(jnp.bfloat16), BOTH, False, 1),
+            (gains, BOTH, True, 1),
+            (query_grad_weight.astype(jnp.bfloat16), ("dp",), False, halves(query_weight.shape[0])),
+            (output_grad.astype(jnp.bfloat16), ("dp",), True, halves(output_weight.shape[0])),
+            (expand_grad.astype(jnp.bfloat16), ("dp",), False, halves(expand_weight.shape[0])),
+            (
+                shared_in_grad.reshape(2 * hidden_units, width),
+                ("dp",),
+                True,
+                halves(2 * hidden_units),
+            ),
+            (shared_out_grad, ("dp",), True, halves(hidden_units)),
+            (normed_grad.astype(jnp.bfloat16), ("tensor",), False, halves(own_rows)),
+        ],
+        5,
     )
     shared_in_out = jnp.moveaxis(shared_in_out.reshape(2, hidden_units, -1), 2, 0)
-    latent_out = small[:, :latent_columns]
-    router_out = small[:, latent_columns : latent_columns + EXPERTS]
-    last = latent_columns + EXPERTS
-    gain_one_out = small[:, last]
-    gain_two_out = small[:, last + 1]
-    gain_lat_out = small[:lat_rows, last + 2]
+    gain_one_out = gains_out[0, :gain_rows]
+    gain_two_out = gains_out[1, :gain_rows]
+    gain_lat_out = gains_out[2, :lat_rows]
     scale_own = own_slice(scale_one, first_row, own_rows)
     weighted_one = normed_own * gain_one
     tokens_grad = (

time: 950 us -> 838 us (0.88)
  matrix products: 360 us -> 210 us
  Pallas kernels: 406 us -> 516 us
  local copies, waits for them, and re-layouts: 94.8 us -> 40.9 us
  other arithmetic: 58.8 us -> 48.1 us
    dot_general x8 -> x2, matrix products: 201 us -> 47.1 us  [combine(): jnp.einsum('gst,gsd->gtd', pick, slot_rows, preferred_element_type=jnp.fl...]
    pallas_call x0 -> x2, Pallas kernels: none -> 128 us  [the longest x1 64.3 us: expert_first(): pl.pallas_call(kernel, grid=grid, out_shape=[jax.ShapeDtypeStruct(rows.sh...]
    pallas_call x3, Pallas kernels: 194 us -> 176 us  [cube_reduce(): pl.pallas_call(kernel, out_shape=shapes, in_specs=[pl.BlockSpec(memory_sp...]
    convert_element_type x1 -> x0, local copies, waits for them, and re-layouts: 17.9 us -> none  [body(): out_slots = jnp.einsum('sxkf,xfd->sxkd', act_gated, expert_out, preferred...]
    dot_general x1 -> x0, local copies, waits for them, and re-layouts: 17 us -> none  [body(): jnp.einsum('sxkcf,xdcf->sxkd', expert_pre_grad, expert_in, preferred_elem...]
    another operation x6, other arithmetic: 15.9 us -> 2.49 us  [the longest x1 12.9 us: body(): jnp.stack([gate_part, up_part], axis=-2).astype(jnp.bfloat16)]
  transfers between devices with their start and end apart: 6 -> 6, of which waited for: 1 -> 0; matrix products, arithmetic and copies ran while one was open for 49% -> 33% of each run, Pallas kernels for 24% -> 51%
where the time goes in v3:
time: 838 us; the launch traced here: 831 us
  Pallas kernels  516 us (62%)
  matrix products  210 us (25%)
  other arithmetic  48.1 us (6%)
  local copies, waits for them, and re-layouts  40.9 us (5%)
  between operations  15.4 us (2%)
    pallas_call x3, Pallas kernels, cube_gather(): pl.pallas_call(kernel, out_shape=shapes, in_specs=[pl.BlockSpec(memory_sp...  213 us
    pallas_call x3, Pallas kernels, cube_reduce(): pl.pallas_call(kernel, out_shape=shapes, in_specs=[pl.BlockSpec(memory_sp...  176 us
    pallas_call x1, Pallas kernels, expert_first(): pl.pallas_call(kernel, grid=grid, out_shape=[jax.ShapeDtypeStruct(rows.sh...  64.3 us
    pallas_call x1, Pallas kernels, expert_second(): pl.pallas_call(kernel, grid=grid, out_shape=[jax.ShapeDtypeStruct(rows.sh...  63.3 us
    dot_general x2, matrix products, combine(): jnp.einsum('gst,gsd->gtd', pick, slot_rows, preferred_element_type=jnp.fl...  47.1 us
    dot_general x1, matrix products, body(): jnp.einsum('gst,gtd->gsd', pick, normed_all, preferred_element_type=jnp.f...  20.7 us
    dot_general x1, matrix products, body(): jnp.einsum('gst,gtd->gsd', pick, cot_all, preferred_element_type=jnp.floa...  20 us
  transfers between devices with their start and end apart: 6, of which 0 were waited for; matrix products, arithmetic and copies ran while one was open for 33% of the time, Pallas kernels for 51%

profile of v3, /device:TPU:0, one launch (start us, length us, event | category | flops | bytes accessed | tf_op | source)
XLA Modules:
  0.0 831.2 jit_solution(9615323182947543301)
XLA Ops:
  9.5 1.3 pad.29.refs_6_
  10.9 1.4 fusion.89.refs_5_
  12.3 94.4 %cube_gather.3 = (bf16[512,2048]{1,0:T(8,128)(2,1)}, bf16[512,2048]{1,0:T(8,128)(2,1)}, bf16[2048,576]{1,0:T(8,128)(2,1)}, bf16[2048,768]{1,0:T(8,128)(2,1)}, bf...) custom-call(bf16[128,2048]{1,0:T(8,128)(2,1)} %refs_0_.1, ...), custom_call_target="tpu_custom_call" | custom-call | bytes 108003328 | tf_op jit(solution)/shard_map/cube_gather/pallas_call | solution.py:311
  106.8 1.6 slice_reduce_fusion.1
  110.1 3.8 fusion.120
  115.3 1.8 convolution_convert_fusion.12
  117.1 1.9 copy.175
  119.2 4.9 fusion.118
  125.9 2.8 fusion.55
  129.0 5.8 convolution_convert_fusion.15
  134.9 4.4 convolution_convert_fusion.9.refs_0_
  139.3 38.5 %cube_reduce.3 = f32[128,2048]{1,0:T(8,128)} custom-call(bf16[512,2048]{1,0:T(8,128)(2,1)} %convolution_convert_fusion.9.refs_0_), custom_call_target="tpu_custom_call" | custom-call | bytes 16777216 | tf_op jit(solution)/shard_map/cube_reduce/pallas_call | solution.py:446
  177.8 1.4 multiply_reduce_fusion.5
  181.3 81.6 %cube_gather.4 = bf16[4096,2048]{1,0:T(8,128)(2,1)} custom-call(bf16[128,2048]{1,0:T(8,128)(2,1)} %multiply_convert_fusion.4.refs_0_), custom_call_target="tpu_custom_call" | custom-call | bytes 134217728 | tf_op jit(solution)/shard_map/cube_gather/pallas_call | solution.py:311
  265.0 2.9 bitcast_compare_fusion
  267.9 9.1 %fusion.124 = (f32[4096]{0:T(1024)S(1)}, f32[4096,64]{1,0:T(8,128)S(1)}) fusion(pred[4096,64]{1,0:T(32,128)(4,1)S(1)} %copy.150, bf16[4096,2048]{1,0:T(8,128)(2,1)} %cube_gather.4, bf16[2048,128]{1,0:T(8,128)(2,1)S(1)} %copy-done.4), kind=kOutput, calls=%fused_computation.201 | convolution fusion | flops 1075048448 | bytes 18628608 | tf_op jit(solution)/shard_map/dot_general | solution.py:695
  277.0 1.3 copy-done.18
  278.3 1.2 fusion.25
  280.1 1.2 select_reduce_fusion.1
  281.4 2.8 reshape.335.gate_ref
  284.2 20.7 %convolution_convert_fusion.3 = bf16[8,640,2048]{2,1,0:T(8,128)(2,1)} fusion(pred[8,640,512]{2,1,0:T(32,128)(4,1)S(1)} %copy-done.16, bf16[8,512,2048]{2,1,0:T(8,128)(2,1)} %bitcast.136), kind=kOutput, calls=%fused_computation.5 | convolution fusion | flops 10747904000 | bytes 40370176 | tf_op jit(solution)/shard_map/gst,gtd->gsd/dot_general | solution.py:714
  304.9 20.0 %convolution_convert_fusion.2 = bf16[8,640,2048]{2,1,0:T(8,128)(2,1)} fusion(pred[8,640,512]{2,1,0:T(32,128)(4,1)S(1)} %copy-done.16, bf16[8,512,2048]{2,1,0:T(8,128)(2,1)} %bitcast.170), kind=kOutput, calls=%fused_computation.4 | convolution fusion | flops 10747904000 | bytes 40370176 | tf_op jit(solution)/shard_map/gst,gtd->gsd/dot_general | solution.py:717
  325.0 64.3 %expert_first.1 = (bf16[8,8,80,2048]{3,2,1,0:T(8,128)(2,1)}, bf16[8,640,352]{2,1,0:T(8,128)(2,1)}, bf16[8,2,640,352]{3,2,1,0:T(8,128)(2,1)}, f32[8,640,1]{2,1,0:T(8,128)}) custom-call(bf16[8,8,80,2048]{3,2,1,0:T(8,128)(2,1)} %bitcast.174, bf16[8,8,80,2048]{3,2,1,0:T(8,128)(2,1)} %bitcast.176, f32[8,640,1]{2,1,0:T(8,128)} %reshape.335.gate_ref, ...), custom_call_target="tpu_custom_call" | custom-call | flops 36909875200 | bytes 97517568 | tf_op jit(solution)/shard_map/expert_first/pallas_call | solution.py:516
  389.3 23.3 %convolution_convert_fusion.1 = bf16[8,512,2048]{2,1,0:T(8,128)(2,1)} fusion(pred[8,640,512]{2,1,0:T(32,128)(4,1)S(1)} %copy-done.16, bf16[8,640,2048]{2,1,0:T(8,128)(2,1)} %bitcast.179), kind=kOutput, calls=%fused_computation.3 | convolution fusion | flops 10745806848 | bytes 40370176 | tf_op jit(solution)/shard_map/gst,gsd->gtd/dot_general | solution.py:762
  412.6 1.7 copy-done.17
  415.1 3.7 select_reduce_fusion
  419.4 3.9 dynamic_update_slice.3.refs_0_
  423.3 63.3 %expert_second.1 = (bf16[8,8,80,2048]{3,2,1,0:T(8,128)(2,1)}, f32[8,2,352,2048]{3,2,1,0:T(8,128)}, f32[8,352,2048]{2,1,0:T(8,128)}) custom-call(bf16[8,8,80,2048]{3,2,1,0:T(8,128)(2,1)} %bitcast.175, bf16[8,8,80,2048]{3,2,1,0:T(8,128)(2,1)} %bitcast.177, bf16[8,640,352]{2,1,0:T(8,128)(2,1)} %get-tuple-element.66.act_ref, ...), custom_call_target="tpu_custom_call" | custom-call | flops 29527900160 | bytes 143654912 | tf_op jit(solution)/shard_map/expert_second/pallas_call | solution.py:573
  486.7 23.8 %convolution_convert_fusion = bf16[8,512,2048]{2,1,0:T(8,128)(2,1)} fusion(pred[8,640,512]{2,1,0:T(32,128)(4,1)} %bitcast_compare_fusion, bf16[8,640,2048]{2,1,0:T(8,128)(2,1)} %bitcast.178), kind=kOutput, calls=%fused_computation.2 | convolution fusion | flops 10745806848 | bytes 40370176 | tf_op jit(solution)/shard_map/gst,gsd->gtd/dot_general | solution.py:762
  510.5 8.4 %fusion.27 = f32[512,2,704]{0,2,1:T(8,128)} fusion(bf16[2048,2,704]{0,2,1:T(8,128)(2,1)} %all-gather.6.cloned.1.call-done, bf16[8,512,2048]{2,1,0:T(8,128)(2,1)} %bitcast.137, s32[]{:T(128)S(6)} %select_n.44), kind=kOutput, calls=%fused_computation.50 | convolution fusion | flops 2952790016 | bytes 10747908 | tf_op jit(solution)/shard_map/gd,dcf->gcf/dot_general | solution.py:741
  519.0 5.0 fusion.54
  524.0 3.2 convolution_convert_fusion.6.refs_7_
  527.2 6.7 convolution_convert_fusion.4
  533.9 3.8 fusion.125
  537.8 5.2 convolution_bitcast_fusion
  543.9 7.8 fusion.12
  551.7 2.0 add_convert_fusion.1.refs_1_
  553.8 48.3 %cube_reduce.4 = (f32[128,128]{1,0:T(8,128)}, f32[128,2048]{1,0:T(8,128)}) custom-call(bf16[4096,128]{1,0:T(8,128)(2,1)} %copy-done.10, bf16[512,2048]{1,0:T(8,128)(2,1)} %add_convert_fusion.1.refs_1_), custom_call_target="tpu_custom_call" | custom-call | bytes 25165824 | tf_op jit(solution)/shard_map/cube_reduce/pallas_call | solution.py:446
  603.9 2.2 multiply_reduce_fusion.2
  606.2 1.5 fusion.122
  607.7 36.6 %cube_gather.5 = bf16[512,2048]{1,0:T(8,128)(2,1)} custom-call(bf16[128,2048]{1,0:T(8,128)(2,1)} %get-tuple-element.104.refs_0_), custom_call_target="tpu_custom_call" | custom-call | bytes 16777216 | tf_op jit(solution)/shard_map/cube_gather/pallas_call | solution.py:311
  644.3 3.9 convolution_convert_fusion.13
  649.0 2.8 fusion.56
  651.8 8.8 %fusion.36 = f32[512,4,192]{0,2,1:T(8,128)} fusion(f32[4,512,512]{1,2,0:T(8,128)} %fusion.12, f32[4,512,512]{1,2,0:T(8,128)} %fusion.56, bf16[512,4,64]{0,2,1:T(8,128)(2,1)S(1)} %copy-done.33, bf16[512,4,128]{0,2,1:T(8,128)(2,1)S(1)} %copy-done.30), kind=kOutput, calls=%fused_computation.62 | convolution fusion | flops 409471488 | bytes 10747904 | tf_op jit(solution)/shard_map/hqk,khd->qhd/dot_general | solution.py:110
  660.6 1.3 slice.207
  662.0 8.5 %fusion.39 = f32[512,4,192]{0,2,1:T(8,128)} fusion(f32[4,512,512]{1,2,0:T(8,128)} %fusion.12, f32[4,512,512]{1,2,0:T(8,128)} %fusion.56, bf16[512,4,32]{0,2,1:T(8,128)(2,1)S(1)} %copy-done.48, bf16[512,4,32]{0,2,1:T(8,128)(2,1)S(1)} %copy-done.46, bf16[512,4,128]{0,2,1:T(8,128)(2,1)S(1)} %copy-done.28), kind=kOutput, calls=%fused_computation.63 | convolution fusion | flops 410257920 | bytes 10747904 | tf_op jit(solution)/shard_map/hqk,qhd->khd/dot_general | solution.py:111
  670.4 1.3 slice.206
  672.8 6.9 fusion.43
  680.9 2.5 multiply_reduce_fusion.1
  684.8 3.0 convolution_convert_fusion.7
  687.8 4.5 copy.163.refs_0_
  694.4 5.0 add_convert_fusion
  699.4 1.3 convolution_convert_fusion.10
  701.9 3.1 convolution_convert_fusion.11.refs_5_
  705.1 3.8 convolution_convert_fusion.8.refs_4_
  708.8 1.8 fusion.126
  711.4 3.6 fusion.123
  715.1 4.9 convolution_convert_fusion.5.refs_3_
  720.6 89.2 %cube_reduce.5 = (f32[64,576]{1,0:T(8,128)}, f32[64,64]{1,0:T(8,128)}, f32[8,128]{1,0:T(8,128)}, f32[256,768]{1,0:T(8,128)}, f32[512,256]{1,0:T(8,128)}, /*index...) custom-call(bf16[2048,576]{1,0:T(8,128)(2,1)} %copy.163.refs_0_, ...), custom_call_target="tpu_custom_call" | custom-call | bytes 158334976 | tf_op jit(solution)/shard_map/cube_reduce/pallas_call | solution.py:446
  809.9 1.4 fusion.47
  811.3 1.2 slice_bitcast_fusion.3
  812.5 1.3 slice_bitcast_fusion.2
  813.8 2.6 fusion.46
  816.4 2.1 add_convert_fusion.2
  (246 shorter events, 31.2 us)
Async XLA Ops:
  7.2 255.8 %all-gather.4.cloned.1.call-start = ((), (), s32[]{:S(2)}) async-start(), calls=%async_computation.3 | async-start | bytes 18874368 | tf_op jit(solution)/shard_map/all_gather | solution.py:125
  106.7 403.8 %all-gather.6.cloned.1.call-start = ((), (), s32[]{:S(2)}) async-start(), calls=%async_computation.5 | async-start | bytes 6488064 | tf_op jit(solution)/shard_map/all_gather | solution.py:125
  108.5 6.2 copy-start.63
  109.2 9.9 %copy-start.57 = (f32[2048]{0:T(1024)}, f32[2048]{0:T(1024)S(1)}, u32[]{:S(2)}) copy-start(f32[2048]{0:T(1024)S(1)} %get-tuple-element.101) | copy-start | bytes 24580
  109.2 70.6 %copy-start.54 = (f32[2048]{0:T(1024)}, f32[2048]{0:T(1024)S(1)}, u32[]{:S(2)}) copy-start(f32[2048]{0:T(1024)S(1)} %get-tuple-element.100) | copy-start | bytes 24580
  109.8 9.4 %copy-start.73 = (f32[512]{0:T(512)}, f32[512]{0:T(512)S(1)}, u32[]{:S(2)}) copy-start(f32[512]{0:T(512)S(1)} %add_rsqrt_fusion.1) | copy-start | bytes 6148
  110.1 5.2 copy-start.78
  113.9 10.5 %copy-start.2 = (f32[512,576]{0,1:T(8,128)}, f32[512,576]{0,1:T(8,128)S(1)}, u32[]{:S(2)}) copy-start(f32[512,576]{0,1:T(8,128)S(1)} %fusion.120) | copy-start | bytes 3538948
  119.1 9.9 %copy-start.11 = (bf16[512,1024]{0,1:T(8,128)(2,1)}, bf16[512,1024]{0,1:T(8,128)(2,1)S(1)}, u32[]{:S(2)}) copy-start(bf16[512,1024]{0,1:T(8,128)(2,1)S(1)} %copy.175) | copy-start | bytes 3145732
  119.1 6.8 copy-start.29
  119.2 5.1 copy-start.61
  124.2 4.6 copy-start.27
  124.2 4.5 copy-start.69
  124.5 4.3 copy-start.59
  129.0 5.9 copy-start.50
  134.9 4.4 copy-start.79
  139.3 38.5 %copy-start.6 = (bf16[128,2048]{1,0:T(8,128)(2,1)S(1)}, bf16[128,2048]{1,0:T(8,128)(2,1)}, u32[]{:S(2)}) copy-start(bf16[128,2048]{1,0:T(8,128)(2,1)} %refs_0_.1) | copy-start | bytes 1572868
  181.3 81.8 %copy-start.56 = (s32[8,4096]{1,0:T(8,128)S(1)}, s32[8,4096]{1,0:T(8,128)}, u32[]{:S(2)}) copy-start(s32[8,4096]{1,0:T(8,128)} %get-tuple-element.61) | copy-start | bytes 393220
  263.0 256.0 %all-gather.8.cloned.1.call-start = ((), (), s32[]{:S(2)}) async-start(), calls=%async_computation.6 | async-start | bytes 3244032 | tf_op jit(solution)/shard_map/all_gather | solution.py:125
  280.1 4.0 copy-start.16
  324.9 218.0 %reduce-scatter.4.cloned.1.call-start = ((), (), s32[]{:S(2)}) async-start(), calls=%async_computation.4 | async-start | bytes 18874368 | tf_op jit(solution)/shard_map/reduce_scatter | solution.py:129
  412.6 281.8 %reduce-scatter.6.cloned.1.call-start = ((), (), s32[]{:S(2)}) async-start(), calls=%async_computation.7 | async-start | bytes 18874368 | tf_op jit(solution)/shard_map/reduce_scatter | solution.py:129
  423.3 63.3 %copy-start.10 = (bf16[4096,128]{1,0:T(8,128)(2,1)}, bf16[4096,128]{1,0:T(8,128)(2,1)S(1)}, u32[]{:S(2)}) copy-start(bf16[4096,128]{1,0:T(8,128)(2,1)S(1)} %dynamic_update_slice.3.refs_0_) | copy-start | bytes 3145732
  510.5 8.5 %copy-start.24 = (bf16[512,2048]{1,0:T(8,128)(2,1)S(1)}, bf16[512,2048]{1,0:T(8,128)(2,1)}, u32[]{:S(2)}) copy-start(bf16[512,2048]{1,0:T(8,128)(2,1)} %get-tuple-element.62) | copy-start | bytes 6291460
  524.0 13.8 %slice-start = ((s8[5767168]{0:T(1024)(128)(4,1)}), s8[4194304]{0:T(1024)(128)(4,1)S(1)}, s32[]{:S(2)}) async-start(s8[5767168]{0:T(1024)(128)(4,1)} %bitcast.171), calls=%async_computation.9 | async-start | bytes 8388608
  527.2 6.7 copy-start.15
  527.2 10.6 %slice-start.1 = ((s8[5767168]{0:T(1024)(128)(4,1)}), s8[1572864]{0:T(1024)(128)(4,1)S(1)}, s32[]{:S(2)}) async-start(s8[5767168]{0:T(1024)(128)(4,1)} %bitcast.171), calls=%async_computation.10 | async-start | bytes 3145728
  543.0 273.4 %reduce-scatter.8.cloned.1.call-start = ((), (), s32[]{:S(2)}) async-start(), calls=%async_computation.8 | async-start | bytes 2621440 | tf_op jit(solution)/shard_map/reduce_scatter | solution.py:129
  543.9 7.8 copy-start.13
  543.9 7.8 copy-start.26
  553.7 50.1 %copy-start.1 = (f32[128,2048]{1,0:T(8,128)S(1)}, f32[128,2048]{1,0:T(8,128)}, u32[]{:S(2)}) copy-start(f32[128,2048]{1,0:T(8,128)} %copy-done) | copy-start | bytes 3145732
  553.7 50.1 %copy-start.5 = (bf16[2048,128]{1,0:T(8,128)(2,1)S(1)}, bf16[2048,128]{1,0:T(8,128)(2,1)}, u32[]{:S(2)}) copy-start(bf16[2048,128]{1,0:T(8,128)(2,1)} %get-tuple-element.56) | copy-start | bytes 1572868
  553.7 50.1 %copy-start.55 = (f32[2048]{0:T(1024)S(1)}, f32[2048]{0:T(1024)}, u32[]{:S(2)}) copy-start(f32[2048]{0:T(1024)} %copy-done.54) | copy-start | bytes 24580
  553.7 50.1 %copy-start.72 = (f32[128]{0:T(128)S(1)}, f32[128]{0:T(128)}, u32[]{:S(2)}) copy-start(f32[128]{0:T(128)} %copy-done.71) | copy-start | bytes 1540
  553.7 52.4 %copy-start.25 = (bf16[128,2048]{1,0:T(8,128)(2,1)S(1)}, bf16[128,2048]{1,0:T(8,128)(2,1)}, u32[]{:S(2)}) copy-start(bf16[128,2048]{1,0:T(8,128)(2,1)} %refs_1_.1) | copy-start | bytes 1572868
  553.8 52.4 %copy-start.75 = (f32[128]{0:T(128)S(1)}, f32[128]{0:T(128)}, u32[]{:S(2)}) copy-start(f32[128]{0:T(128)} %get-tuple-element.131) | copy-start | bytes 1540
  644.3 4.7 copy-start.12
  648.2 3.6 copy-start.30
  648.2 3.6 copy-start.33
  651.8 10.1 %copy-start.28 = (bf16[512,4,128]{0,2,1:T(8,128)(2,1)S(1)}, bf16[512,4,128]{0,2,1:T(8,128)(2,1)}, u32[]{:S(2)}) copy-start(bf16[512,4,128]{0,2,1:T(8,128)(2,1)} %copy-done.27) | copy-start | bytes 1572868
  651.8 10.1 %copy-start.46 = (bf16[512,4,32]{0,2,1:T(8,128)(2,1)S(1)}, bf16[512,4,32]{0,2,1:T(8,128)(2,1)}, u32[]{:S(2)}) copy-start(bf16[512,4,32]{0,2,1:T(8,128)(2,1)} %copy-done.45) | copy-start | bytes 393220
  651.8 10.1 %copy-start.48 = (bf16[512,4,32]{0,2,1:T(8,128)(2,1)S(1)}, bf16[512,4,32]{0,2,1:T(8,128)(2,1)}, u32[]{:S(2)}) copy-start(bf16[512,4,32]{0,2,1:T(8,128)(2,1)} %copy-done.47) | copy-start | bytes 393220
  672.8 8.1 copy-start.3
  672.8 8.1 copy-start.64
  672.8 8.1 copy-start.66
  680.8 3.2 copy-start.14
  680.9 3.9 copy-start.22
  680.9 3.9 copy-start.58
  687.8 4.5 copy-start.39
  687.8 4.5 copy-start.41
  694.4 5.0 copy-start.8
  694.4 5.0 copy-start.37
  701.9 3.1 copy-start.19
  705.1 3.8 copy-start.34
  705.1 3.8 copy-start.76
  720.6 89.2 %copy-start.7 = (bf16[128,2048]{1,0:T(8,128)(2,1)S(1)}, bf16[128,2048]{1,0:T(8,128)(2,1)}, u32[]{:S(2)}) copy-start(bf16[128,2048]{1,0:T(8,128)(2,1)} %refs_0_.1) | copy-start | bytes 1572868
  720.6 93.1 %copy-start.9 = (f32[128,2048]{1,0:T(8,128)S(1)}, f32[128,2048]{1,0:T(8,128)}, u32[]{:S(2)}) copy-start(f32[128,2048]{1,0:T(8,128)} %get-tuple-element.105) | copy-start | bytes 3145732
  813.8 4.7 copy-start.35
  816.4 3.7 copy-start.52
  816.4 5.8 copy-start.31
  816.4 3.0 copy-start.53
  816.4 4.4 copy-start.49
  816.4 5.2 copy-start.62
  818.5 4.8 copy-start.36
  (24 other events, 41.2 us)
Sparse Core Ops, SparseCore 0:
  106.8 94.5 all-gather.3
  263.1 44.2 all-gather.5
  325.0 31.3 all-gather.7
  412.7 115.9 reduce-scatter.3
  543.1 121.6 reduce-scatter.5
  699.5 59.3 reduce-scatter.7
